TPU v7x, 128 devices: a whole 4x4x4 slice. The times are simulated.
128 devices in a mesh: hi: 64 (over y_lo, x, z, core), grp: 2 (over y_hi).
Axes of the slice: x: 4, y: 4 (y_hi: 2, y_lo: 2; y = y_hi * 2 + y_lo), z: 4, core: 2. Of those that a mesh axis runs over, the one named last changes fastest.
Arguments:
- rho: float32 [2, 8192, 8192], P(None, ('hi', 'grp')), may hold values from -6 to 9
- perm: int32 [2, 13], replicated, may hold values from 0 to 12, each once within a row
- superop: float32 [2, 2, 16, 16], replicated, may hold values from -0.3 to 1.1
Outputs:
- rho_out: float32 [2, 8192, 8192], P(None, ('hi', 'grp'))
- trace_mean: float32 [], replicated
All inputs are finite; a program needn't handle non-finite values.
Results may differ from a plain program's by a relative error of at most 0.0001.
Values sent between devices are 32-bit elements; how exact they have to be, the bound alone decides.
A program may use at most 256 MiB of HBM per device.

v0:
```python
import jax
import jax.numpy as jnp
from jax import lax
from jax.sharding import Mesh
from jax.sharding import PartitionSpec as P

ROWS = 8192
PAIRS = 2
HI_GRP = ("hi_0", "hi_1", "hi_2", "hi_3", "grp")


def in_blocks(array, dim, count):
    lengths = array.shape
    parts = array.reshape(*lengths[:dim], count, lengths[dim] // count, *lengths[dim + 1 :])
    return jnp.moveaxis(parts, dim, 0)


def piece_ends(length, count):
    unit = 8 if length >= 8 * count else 1
    return [length // unit * k // count * unit for k in range(1, count)]


def in_order(parts, dim):
    lengths = list(parts.shape[1:])
    lengths[dim] *= parts.shape[0]
    return jnp.moveaxis(parts, 0, dim).reshape(lengths)


def cut_exchange(array, axis, pieces, split_dim, concat_dim):
    parts = in_blocks(array, split_dim, lax.axis_size(axis))
    cut = max(range(1, max(2, parts.ndim - 1)), key=lambda d: parts.shape[d])
    done = []
    for share in jnp.split(parts, piece_ends(parts.shape[cut], pieces), axis=cut):
        if share.size:
            done.append(lax.all_to_all(share, axis, split_axis=0, concat_axis=0, tiled=True))
    return in_order(jnp.concatenate(done, axis=cut), concat_dim)


def by_axis(array, axes):
    for axis in axes:
        array = lax.psum(array, axis)
    return array


def relabel_table(order, count):
    positions = jnp.arange(count, dtype=jnp.int32)
    result = jnp.zeros((count,), jnp.int32)
    for qubit in range(order.shape[0]):
        bit_value = jnp.bitwise_and(jnp.right_shift(positions, qubit), 1)
        result = result + bit_value * jnp.left_shift(jnp.int32(1), order[qubit])
    return result


def apply_channel(matrix, layer_super, pairs):
    real_part = layer_super[0]
    imag_part = layer_super[1]
    kernel = jnp.stack(
        [jnp.stack([real_part, -imag_part], axis=1), jnp.stack([imag_part, real_part], axis=1)],
        axis=0,
    )
    kernel = kernel.reshape(32, 32)
    row_count = matrix.shape[1]
    col_count = matrix.shape[2]
    span = 4**pairs
    row_blocks = row_count // span
    col_blocks = col_count // span
    tile = matrix.reshape(2, row_blocks, span, col_blocks, span)
    tile = jnp.transpose(tile, (0, 2, 4, 1, 3)).reshape(2, span, span, row_blocks * col_blocks)
    rest = row_blocks * col_blocks
    for pair_idx in range(pairs):
        inner = 4**pair_idx
        outer = span // (4 * inner)
        shaped = tile.reshape(2, outer, 4, inner, outer, 4, inner, rest)
        moved = jnp.transpose(shaped, (0, 2, 5, 1, 3, 4, 6, 7)).reshape(32, -1)
        mixed = jnp.dot(
            kernel, moved, precision=lax.Precision.HIGHEST, preferred_element_type=jnp.float32
        )
        mixed = mixed.reshape(2, 4, 4, outer, inner, outer, inner, rest)
        tile = jnp.transpose(mixed, (0, 3, 1, 4, 5, 2, 6, 7)).reshape(2, span, span, rest)
    tile = tile.reshape(2, span, span, row_blocks, col_blocks)
    return jnp.transpose(tile, (0, 3, 1, 4, 2)).reshape(2, row_count, col_count)


def to_columns(matrix):
    return lax.all_to_all(matrix, HI_GRP, split_axis=2, concat_axis=1, tiled=True)


def to_rows(matrix):
    return cut_exchange(matrix, HI_GRP, 2, 1, 2)


def per_device(rho, perm, superop):
    matrix = rho
    full_order = rho.shape[2]
    layer_count = perm.shape[0]
    for layer_idx in range(layer_count):
        index_table = relabel_table(perm[layer_idx], full_order)
        matrix = jnp.take(matrix, index_table, axis=2)
        matrix = to_columns(matrix)
        matrix = jnp.take(matrix, index_table, axis=1)
        matrix = to_rows(matrix)
        matrix = apply_channel(matrix, superop[layer_idx], PAIRS)
    local_rows = matrix.shape[1]
    position = lax.axis_index(HI_GRP)
    diagonal_block = lax.dynamic_slice_in_dim(matrix[0], position * local_rows, local_rows, 1)
    local_trace = jnp.trace(diagonal_block)
    trace_total = by_axis(local_trace, HI_GRP)
    return (matrix, trace_total / ROWS)


def solution(mesh):
    torus = Mesh(
        mesh.devices.reshape(2, 4, 4, 2, mesh.shape["grp"]), ("hi_0", "hi_1", "hi_2", "hi_3", "grp")
    )
    in_specs = (P(None, HI_GRP, None), P(), P())
    out_specs = (P(None, HI_GRP, None), P())
    return jax.shard_map(
        per_device, mesh=torus, in_specs=in_specs, out_specs=out_specs, check_vma=False
    )
```

profile of v0, /device:TPU:0, one launch (start us, length us, event | category | flops | bytes accessed | tf_op | source)
XLA Modules:
  0.0 1230.2 jit_solution(5795579144434345701)
XLA Ops:
  23.3 59.5 %gather_fusion = f32[8192,2,64]{2,1,0:T(2,128)} fusion(f32[2,64,8192]{1,0,2:T(2,128)} %copy.41, s32[8192]{0:T(1024)S(1)} %broadcast_clamp_fusion.1), kind=kCustom, calls=%fused_computation.clone | custom fusion | bytes 8421376 | tf_op jit(solution)/shard_map/jit(_take)/gather | solution.py:98
  82.8 30.9 %fusion.30 = f32[8192,2,64]{2,1,0:T(2,128)} fusion(f32[8192,2,64]{2,1,0:T(2,128)} %gather_fusion, pred[8192]{0:T(1024)(128)(4,1)S(1)} %compare_and_fusion.1), kind=kLoop, calls=%fused_computation.67 | loop fusion | flops 1048576 | bytes 8396800
  124.8 65.3 %all_to_all.56 = f32[128,1,8192]{2,1,0:T(1,128)} all-to-all(f32[128,1,8192]{2,1,0:T(1,128)} %reshape.283), channel_id=1, replica_groups=mesh['hi_0'=2,'hi_1'=4,'hi_2'=4,'hi_3'=2,'grp'=2] {'hi_0','hi_1','hi_2',..., dimensions={0} | all-to-all | bytes 8388608 | tf_op jit(solution)/shard_map/all_to_all | solution.py:85
  190.6 13.8 %reduce = f32[128,8192]{1,0:T(8,128)} reduce(f32[128,1,8192]{2,1,0:T(1,128)} %all_to_all.56, f32[]{:T(128)} %broadcast.238), dimensions={1}, to_apply=%all_to_all.38.reduce_sub_computation | reduce | bytes 8388612 | tf_op jit(solution)/shard_map/all_to_all | solution.py:85
  238.5 59.5 %gather_fusion.1 = f32[8192,2,64]{2,1,0:T(2,128)} fusion(f32[2,8192,64]{2,0,1:T(2,128)} %bitcast.163, s32[8192]{0:T(1024)S(1)} %broadcast_clamp_fusion.1), kind=kCustom, calls=%fused_computation.1.clone | custom fusion | bytes 8421376 | tf_op jit(solution)/shard_map/jit(_take)/gather | solution.py:100
  298.0 29.5 %broadcast_select_fusion.1 = f32[8192,2,64]{2,1,0:T(2,128)S(1)} fusion(f32[8192,2,64]{2,1,0:T(2,128)} %gather_fusion.1, pred[8192]{0:T(1024)(128)(4,1)S(1)} %compare_and_fusion.1), kind=kLoop, calls=%fused_computation.13 | loop fusion | flops 1048576 | bytes 8396800 | tf_op jit(solution)/shard_map/jit(_take)/select_n | solution.py:100
  350.2 24.3 %all-to-all-done.1 = f32[128,1,4096]{2,1,0:T(1,128)S(1)} async-done(((f32[128,1,4096]{2,1,0:T(1,128)}), f32[128,1,4096]{2,1,0:T(1,128)S(1)}, u32[]{:S(2)}, u32[]{:S(2)}) %all-to-all-start.1) | async-done | bytes 2097184 | tf_op jit(solution)/shard_map/all_to_all | solution.py:35
  433.7 20.6 %reshape_reshape.24 = f32[2,4,16,512,16]{4,3,2,1,0:T(8,128)} reshape(f32[2,64,128,64]{3,2,1,0:T(8,128)} %copy.46) | data formatting | bytes 8388608 | tf_op jit(solution)/shard_map/reshape;reshape | solution.py:67
  454.4 20.5 %copy.47 = f32[2,16,16,4,512]{4,3,2,1,0:T(4,128)} copy(f32[2,16,16,4,512]{2,4,1,3,0:T(8,128)} %bitcast.159) | data formatting | bytes 8388608 | tf_op jit(solution)/shard_map/transpose | solution.py:68
  547.2 27.8 %copy.80 = f32[2,4,16,512,16]{2,1,0,4,3:T(4,128)} copy(f32[2,4,16,512,16]{3,1,4,2,0:T(4,128)} %bitcast.173) | data formatting | bytes 8388608 | tf_op jit(solution)/shard_map/reshape | solution.py:81
  575.0 29.5 %reshape.282 = f32[2,64,8192]{1,0,2:T(2,128)} reshape(f32[2,4,16,512,16]{2,1,0,4,3:T(4,128)} %copy.80) | data formatting | bytes 8388608 | tf_op jit(solution)/shard_map/reshape | solution.py:81
  604.5 59.4 %gather_fusion.2 = f32[8192,2,64]{2,1,0:T(2,128)} fusion(f32[2,64,8192]{1,0,2:T(2,128)} %reshape.282, s32[8192]{0:T(1024)S(1)} %broadcast_clamp_fusion), kind=kCustom, calls=%fused_computation.2.clone | custom fusion | bytes 8421376 | tf_op jit(solution)/shard_map/jit(_take)/gather | solution.py:98
  663.9 30.9 %fusion.31 = f32[8192,2,64]{2,1,0:T(2,128)} fusion(f32[8192,2,64]{2,1,0:T(2,128)} %gather_fusion.2, pred[8192]{0:T(1024)(128)(4,1)S(1)} %compare_and_fusion), kind=kLoop, calls=%fused_computation.68 | loop fusion | flops 1048576 | bytes 8396800
  705.9 60.0 %all_to_all.57 = f32[128,1,8192]{2,1,0:T(1,128)} all-to-all(f32[128,1,8192]{2,1,0:T(1,128)} %reshape.289), channel_id=1, replica_groups=mesh['hi_0'=2,'hi_1'=4,'hi_2'=4,'hi_3'=2,'grp'=2] {'hi_0','hi_1','hi_2',..., dimensions={0} | all-to-all | bytes 8388608 | tf_op jit(solution)/shard_map/all_to_all | solution.py:85
  765.9 13.8 %reduce.3 = f32[128,8192]{1,0:T(8,128)} reduce(f32[128,1,8192]{2,1,0:T(1,128)} %all_to_all.57, f32[]{:T(128)} %broadcast.238), dimensions={1}, to_apply=%all_to_all.44.reduce_sub_computation | reduce | bytes 8388612 | tf_op jit(solution)/shard_map/all_to_all | solution.py:85
  813.9 59.4 %gather_fusion.3 = f32[8192,2,64]{2,1,0:T(2,128)} fusion(f32[2,8192,64]{2,0,1:T(2,128)} %bitcast.165, s32[8192]{0:T(1024)S(1)} %broadcast_clamp_fusion), kind=kCustom, calls=%fused_computation.3.clone | custom fusion | bytes 8421376 | tf_op jit(solution)/shard_map/jit(_take)/gather | solution.py:100
  873.2 29.5 %broadcast_select_fusion = f32[8192,2,64]{2,1,0:T(2,128)S(1)} fusion(f32[8192,2,64]{2,1,0:T(2,128)} %gather_fusion.3, pred[8192]{0:T(1024)(128)(4,1)S(1)} %compare_and_fusion), kind=kLoop, calls=%fused_computation.12 | loop fusion | flops 1048576 | bytes 8396800 | tf_op jit(solution)/shard_map/jit(_take)/select_n | solution.py:100
  925.5 24.3 %all-to-all-done.4 = f32[128,1,4096]{2,1,0:T(1,128)S(1)} async-done(((f32[128,1,4096]{2,1,0:T(1,128)}), f32[128,1,4096]{2,1,0:T(1,128)S(1)}, u32[]{:S(2)}, u32[]{:S(2)}) %all-to-all-start.4) | async-done | bytes 2097184 | tf_op jit(solution)/shard_map/all_to_all | solution.py:35
  966.6 18.9 %all-to-all-done.5 = f32[128,1,4096]{2,1,0:T(1,128)} async-done(((f32[128,1,4096]{2,1,0:T(1,128)}), f32[128,1,4096]{2,1,0:T(1,128)}, u32[]{:S(2)}, u32[]{:S(2)}) %all-to-all-start.5) | async-done | bytes 2097184 | tf_op jit(solution)/shard_map/all_to_all | solution.py:35
  1008.8 20.6 %reshape_reshape.28 = f32[2,4,16,512,16]{4,3,2,1,0:T(8,128)} reshape(f32[2,64,128,64]{3,2,1,0:T(8,128)} %copy.58) | data formatting | bytes 8388608 | tf_op jit(solution)/shard_map/reshape;reshape | solution.py:67
  1029.4 20.5 %copy.59 = f32[2,16,16,4,512]{4,3,2,1,0:T(4,128)} copy(f32[2,16,16,4,512]{2,4,1,3,0:T(8,128)} %bitcast.160) | data formatting | bytes 8388608 | tf_op jit(solution)/shard_map/transpose | solution.py:68
  1132.8 14.2 %squeeze.8 = f32[64,8192]{1,0:T(8,128)S(1)} reshape(f32[1,4,16,512,16]{4,3,2,1,0:T(8,128)} %copy.66) | data formatting | bytes 4194304 | tf_op jit(solution)/shard_map/squeeze | solution.py:105
  1171.8 18.0 %copy.65 = f32[2,4,16,512,16]{4,3,2,1,0:T(8,128)} copy(f32[2,4,16,512,16]{3,1,4,2,0:T(4,128)} %bitcast.172) | data formatting | bytes 8388608 | tf_op jit(solution)/shard_map/transpose | solution.py:81
  1192.8 28.3 %reshape.231 = f32[2,64,8192]{2,1,0:T(8,128)} reshape(f32[2,4,16,512,16]{4,3,2,1,0:T(8,128)} %copy.65) | data formatting | bytes 8388608 | tf_op jit(solution)/shard_map/reshape | solution.py:81
  (88 shorter events, 432.2 us)
Async XLA Ops:
  338.5 36.0 %all-to-all-start.1 = ((f32[128,1,4096]{2,1,0:T(1,128)}), f32[128,1,4096]{2,1,0:T(1,128)S(1)}, u32[]{:S(2)}, u32[]{:S(2)}) async-start(f32[128,1,4096]{2,1,0:T(1,128)} %reshape.287), calls=%async_computation.1 | async-start | bytes 4194304 | tf_op jit(solution)/shard_map/all_to_all | solution.py:35
  344.7 36.5 %copy-start.2 = (f32[2,2,16,16]{3,2,1,0:T(8,128)S(1)}, f32[2,2,16,16]{3,2,1,0:T(8,128)}, u32[]{:S(2)}) copy-start(f32[2,2,16,16]{3,2,1,0:T(8,128)} %param.9) | copy-start | bytes 12292
  374.5 15.1 %copy-start = (f32[128,1,4096]{2,1,0:T(1,128)}, f32[128,1,4096]{2,1,0:T(1,128)S(1)}, u32[]{:S(2)}) copy-start(f32[128,1,4096]{2,1,0:T(1,128)S(1)} %all-to-all-done.1) | copy-start | bytes 6291460
  374.5 36.0 %all-to-all-start.2 = ((f32[128,1,4096]{2,1,0:T(1,128)}), f32[128,1,4096]{2,1,0:T(1,128)}, u32[]{:S(2)}, u32[]{:S(2)}) async-start(f32[128,1,4096]{2,1,0:T(1,128)} %reshape.285), calls=%async_computation.2 | async-start | bytes 4194304 | tf_op jit(solution)/shard_map/all_to_all | solution.py:35
  913.8 36.0 %all-to-all-start.4 = ((f32[128,1,4096]{2,1,0:T(1,128)}), f32[128,1,4096]{2,1,0:T(1,128)S(1)}, u32[]{:S(2)}, u32[]{:S(2)}) async-start(f32[128,1,4096]{2,1,0:T(1,128)} %reshape.293), calls=%async_computation.4 | async-start | bytes 4194304 | tf_op jit(solution)/shard_map/all_to_all | solution.py:35
  949.8 6.6 copy-start.1
  949.8 35.8 %all-to-all-start.5 = ((f32[128,1,4096]{2,1,0:T(1,128)}), f32[128,1,4096]{2,1,0:T(1,128)}, u32[]{:S(2)}, u32[]{:S(2)}) async-start(f32[128,1,4096]{2,1,0:T(1,128)} %reshape.291), calls=%async_computation.5 | async-start | bytes 4194304 | tf_op jit(solution)/shard_map/all_to_all | solution.py:35
where the time goes:
time: 1240 us; the launch traced here: 1230 us
  local copies, waits for them, and re-layouts  722 us (58%)
  other arithmetic  188 us (15%)
  blocking collectives  160 us (13%)
  waiting for transfers between devices  78.1 us (6%)
  matrix products  38.4 us (3%)
  starting transfers between devices  25.5 us (2%)
  between operations  19.1 us (2%)
    all_to_all x2, blocking collectives, to_columns(): lax.all_to_all(matrix, HI_GRP, split_axis=2, concat_axis=1, tiled=True)  125 us
    gather x2, local copies, waits for them, and re-layouts, per_device(): matrix = jnp.take(matrix, index_table, axis=1)  119 us
    gather x2, local copies, waits for them, and re-layouts, per_device(): matrix = jnp.take(matrix, index_table, axis=2)  119 us
    unnamed x19, local copies, waits for them, and re-layouts  86.7 us
    reshape x3, local copies, waits for them, and re-layouts, apply_channel(): return jnp.transpose(tile, (0, 3, 1, 4, 2)).reshape(2, row_count, col_count)  85.7 us
    all_to_all x4, waiting for transfers between devices, cut_exchange(): lax.all_to_all(share, axis, split_axis=0, concat_axis=0, tiled=True)  78.1 us
    unnamed x2, other arithmetic  61.7 us
    select_n x2, other arithmetic, per_device(): matrix = jnp.take(matrix, index_table, axis=1)  59.1 us
  transfers between devices with their start and end apart: 4, of which 4 were waited for; matrix products, arithmetic and copies ran while one was open for 3% of the time, Pallas kernels for 0%

commit v1 on v0

v1 whole, which is shorter than its diff:
```python
import functools

import jax
import jax.numpy as jnp
from jax import lax
from jax.experimental import pallas as pl
from jax.experimental.pallas import tpu as pltpu
from jax.sharding import Mesh
from jax.sharding import PartitionSpec as P

ROWS = 8192
QUBITS = 13
HI_GRP = ("hi", "grp")
F32 = jnp.float32
BF16 = jnp.bfloat16
SMEM = pltpu.SMEM
VMEM = pltpu.VMEM


def fill(table, weights):
    table[0] = jnp.int32(0)
    for k, weight in enumerate(weights):
        for j in range(1 << k):
            table[(1 << k) + j] = table[j] + weight


def one_shl(amount):
    return jnp.left_shift(jnp.int32(1), amount)


def column_order(perm, order):
    for j in range(4):
        order[j] = perm[0, j]
    count = jnp.int32(4)
    for q in range(QUBITS):
        order[count] = jnp.int32(q)
        mine = perm[0, 0] == q
        for j in range(1, 4):
            mine = mine | (perm[0, j] == q)
        count = count + jnp.where(mine, 0, 1)


def spread(perm, x, out, y, z0, z1, order, tc, te):
    column_order(perm, order)
    top = order[12]

    def weight(q):
        return one_shl(jnp.where(q < top, q, q - 1))

    fill(tc, [weight(order[i]) for i in range(6)])
    fill(te, [weight(order[6 + i]) for i in range(6)])
    step = one_shl(top - 7)

    @pl.loop(0, 32)
    def _(m):
        low = m & (step - 1)
        first = (m - low) * 2 + low
        for part in range(2):
            halves = [
                x[part, :, pl.ds(pl.multiple_of(t * 128, 128), 128)] for t in (first, first + step)
            ]
            start = pl.multiple_of(part * 4096 + m * 128, 128)
            y[pl.ds(start, 128), :] = jnp.concatenate(halves, axis=0).T

    @pl.loop(0, 32)
    def _(pair):
        for k, z in enumerate((z0, z1)):
            e = pair * 2 + k
            base = te[e]
            for c in range(64):
                row = base + tc[c]
                z[pl.ds(c, 1), :] = y[pl.ds(row, 1), :]
                z[pl.ds(64 + c, 1), :] = y[pl.ds(row + 4096, 1), :]
        for k, z in enumerate((z0, z1)):
            e = pair * 2 + k
            turned = z[...].T
            out[e] = turned[:64]
            out[64 + e] = turned[64:]


def split_bf16(value):
    high = value.astype(BF16)
    return high, (value - high.astype(F32)).astype(BF16)


def build_weights(sup, layer, pair, major_is_row, high_ref, low_ref):
    def uv(major, lane):
        minor = jnp.right_shift(lane, 2 * pair) & 3
        return 4 * major + minor if major_is_row else 4 * minor + major

    row = lax.broadcasted_iota(jnp.int32, (512, 16), 0)
    col16 = lax.broadcasted_iota(jnp.int32, (512, 16), 1)
    expand = jnp.where(uv(jnp.right_shift(row, 7), row & 127) == col16, 1.0, 0.0).astype(BF16)
    dims = (((1,), (1,)), ((), ()))
    lane_in = lax.broadcasted_iota(jnp.int32, (512, 128), 0) & 127
    lane_out = lax.broadcasted_iota(jnp.int32, (512, 128), 1)
    keep = 63 & ~(3 << (2 * pair))
    same_rest = (lane_in & keep) == (lane_out & keep)
    part_in = jnp.right_shift(lane_in, 6)
    part_out = jnp.right_shift(lane_out, 6)
    sign = jnp.where(part_out >= part_in, 1.0, -1.0).astype(F32)
    parts = [split_bf16(sup[layer, part]) for part in range(2)]
    for which, ref in enumerate((high_ref, low_ref)):
        half = [
            lax.dot_general(expand, parts[p][which], dims, preferred_element_type=F32).astype(BF16)
            for p in range(2)
        ]
        for block in range(4):
            target = expand[block * 128 : (block + 1) * 128]
            real, imag = (
                lax.dot_general(h, target, dims, preferred_element_type=F32) for h in half
            )
            value = jnp.where(part_in == part_out, real, sign * imag)
            ref[:, block * 128 : (block + 1) * 128] = jnp.where(same_rest, value, 0.0).astype(BF16)


def apply_pair(z, pair, high_ref, low_ref, rows=128):
    steps = 512 // rows

    @pl.loop(0, 4 * steps)
    def _(i):
        other = i // steps
        chunk = i % steps
        first = other * 4 if pair == 0 else other
        stride = 1 if pair == 0 else 4
        places = [
            pl.ds(pl.multiple_of((first + stride * k) * 512 + chunk * rows, rows), rows)
            for k in range(4)
        ]
        value = jnp.concatenate([z[place, :] for place in places], axis=1)
        high, low = split_bf16(value)
        mixed = jnp.dot(high, high_ref[...], preferred_element_type=F32)
        mixed += jnp.dot(low, high_ref[...], preferred_element_type=F32)
        mixed += jnp.dot(high, low_ref[...], preferred_element_type=F32)
        for k, place in enumerate(places):
            z[place, :] = mixed[:, k * 128 : (k + 1) * 128]


def channel(sup, layer, major_is_row, z, high_ref, low_ref):
    for pair in range(2):
        build_weights(sup, layer, pair, major_is_row, high_ref, low_ref)
        apply_pair(z, pair, high_ref, low_ref)


def middle(perm, sup, x, out, z, high, low, inv, rest, ta, tl, th, da, dl, dh):
    count = jnp.int32(0)
    for q in range(QUBITS):
        source = perm[1, q]
        inv[source] = jnp.int32(q)
        rest[count] = jnp.int32(q)
        count = count + jnp.where(source >= 4, 1, 0)
    first_row = [one_shl(perm[0, perm[1, rest[j]]]) for j in range(9)]
    fill(ta, [one_shl(perm[0, j]) for j in range(4)])
    fill(tl, first_row[:5])
    fill(th, first_row[5:])
    fill(da, [one_shl(inv[j]) for j in range(4)])
    fill(dl, [one_shl(rest[j]) for j in range(5)])
    fill(dh, [one_shl(rest[5 + j]) for j in range(4)])

    @pl.loop(0, 256)
    def _(i):
        base = ta[i // 16] + th[i % 16]
        place = pl.multiple_of(i * 32, 32)
        for k in range(32):
            z[pl.ds(place + k, 1), :] = x[pl.ds(base + tl[k], 1), :]

    channel(sup, 0, True, z, high, low)

    @pl.loop(0, 256)
    def _(i):
        base = da[i // 16] + dh[i % 16]
        place = pl.multiple_of(i * 32, 32)
        for k in range(32):
            out[pl.ds(base + dl[k], 1), :] = z[pl.ds(place + k, 1), :]


def gather_back(perm, sup, where, x, out, trace, y, z, b0, b1, high, low, order, inv, ta, tl, th):
    column_order(perm, order)
    for i in range(QUBITS):
        inv[order[i]] = jnp.int32(i)
    weights = [one_shl(inv[perm[0, perm[1, q]]]) for q in range(QUBITS)]
    fill(ta, weights[:4])
    fill(tl, weights[4:9])
    fill(th, weights[9:])

    @pl.loop(0, 64)
    def _(p):
        turned = jnp.concatenate([x[p], x[p + 64]], axis=0).T
        real, imag = turned[:64], turned[64:]
        start = pl.multiple_of(p * 64, 64)
        y[pl.ds(start, 64), :] = jnp.concatenate([real[:, :64], imag[:, :64]], axis=1)
        y[pl.ds(start + 4096, 64), :] = jnp.concatenate([real[:, 64:], imag[:, 64:]], axis=1)

    @pl.loop(0, 256)
    def _(i):
        base = ta[i // 16] + th[i % 16]
        place = pl.multiple_of(i * 32, 32)
        for k in range(32):
            z[pl.ds(place + k, 1), :] = y[pl.ds(base + tl[k], 1), :]

    channel(sup, 1, False, z, high, low)

    @pl.loop(0, 32)
    def _(pair):
        for k, b in enumerate((b0, b1)):
            t = pair * 2 + k
            for low_bits in range(16):
                b[pl.ds(low_bits, 8, stride=16), :] = z[
                    pl.ds(pl.multiple_of(low_bits * 512 + t * 8, 8), 8), :
                ]
        for k, b in enumerate((b0, b1)):
            lanes = pl.ds(pl.multiple_of((pair * 2 + k) * 128, 128), 128)
            turned = b[...].T
            out[0, :, lanes] = turned[:64]
            out[1, :, lanes] = turned[64:]

    me = where[0]
    block = out[0, :, pl.ds(pl.multiple_of((me // 2) * 128, 128), 128)]
    lane = lax.broadcasted_iota(jnp.int32, (64, 128), 1)
    row = lax.broadcasted_iota(jnp.int32, (64, 128), 0)
    kept = jnp.where(lane == row + (me % 2) * 64, block, 0.0)
    trace[...] = jnp.sum(kept, axis=0, keepdims=True)


def call(body, outs, n_smem, n_vmem, scratch, args):
    smem = pl.BlockSpec(memory_space=SMEM)
    vmem = pl.BlockSpec(memory_space=VMEM)
    kinds = [smem if i in n_smem else vmem for i in range(n_vmem)]
    return pl.pallas_call(
        body,
        out_shape=outs,
        in_specs=kinds,
        out_specs=jax.tree.map(lambda _: vmem, outs),
        scratch_shapes=scratch,
        compiler_params=pltpu.CompilerParams(vmem_limit_bytes=60 * 2**20),
    )(*args)


def table(*sizes):
    return [SMEM((n,), jnp.int32) for n in sizes]


def spread_call(perm, x):
    return call(
        spread, jax.ShapeDtypeStruct((128, 64, 128), F32), (0,), 2,
        [VMEM((8192, 128), F32), VMEM((128, 128), F32), VMEM((128, 128), F32)] + table(14, 64, 64),
        (perm, x),
    )


def middle_call(perm, sup, x):
    return call(
        middle, jax.ShapeDtypeStruct((8192, 128), F32), (0,), 3,
        [VMEM((8192, 128), F32), VMEM((512, 512), BF16), VMEM((512, 512), BF16)]
        + table(13, 14, 16, 32, 16, 16, 32, 16),
        (perm, sup, x),
    )


def back_call(perm, sup, where, x):
    return call(
        gather_back,
        (jax.ShapeDtypeStruct((2, 64, 8192), F32), jax.ShapeDtypeStruct((1, 128), F32)),
        (0, 2), 4,
        [VMEM((8192, 128), F32), VMEM((8192, 128), F32), VMEM((128, 128), F32), VMEM((128, 128), F32),
         VMEM((512, 512), BF16), VMEM((512, 512), BF16)]
        + table(14, 13, 16, 32, 16),
        (perm, sup, where, x),
    )


def exchange(value):
    return lax.all_to_all(value, HI_GRP, split_axis=0, concat_axis=0, tiled=True)


def per_device(rho, perm, superop):
    sent = spread_call(perm, rho)
    mid = middle_call(perm, superop, exchange(sent).reshape(8192, 128))
    where = lax.axis_index(HI_GRP).astype(jnp.int32).reshape(1)
    matrix, trace = back_call(perm, superop, where, exchange(mid.reshape(128, 64, 128)))
    return matrix, lax.psum(jnp.sum(trace), HI_GRP) / ROWS


def solution(mesh):
    in_specs = (P(None, HI_GRP, None), P(), P())
    out_specs = (P(None, HI_GRP, None), P())
    return jax.shard_map(
        per_device, mesh=mesh, in_specs=in_specs, out_specs=out_specs, check_vma=False
    )
```

time: 1240 us -> 289 us (0.23)
  local copies, waits for them, and re-layouts: 722 us -> 0 us
  other arithmetic: 188 us -> 1.21 us
  Pallas kernels: 0 us -> 95.8 us
  matrix products: 38.4 us -> 0 us
  blocking collectives: 160 us -> 128 us
  waiting for transfers between devices: 78.1 us -> 53.3 us
  starting transfers between devices: 25.5 us -> 6.58 us
  between operations: 19.1 us -> 2.42 us
    gather x4 -> x0, local copies, waits for them, and re-layouts: 238 us -> none  [the longest x2 119 us: per_device(): matrix = jnp.take(matrix, index_table, axis=1)]
    reshape x9 -> x0, local copies, waits for them, and re-layouts: 113 us -> none  [the longest x3 85.7 us: apply_channel(): return jnp.transpose(tile, (0, 3, 1, 4, 2)).reshape(2, row_count, col_count)]
    transpose x11 -> x0, local copies, waits for them, and re-layouts: 105 us -> none  [the longest x2 41.1 us: apply_channel(): jnp.transpose(tile, (0, 2, 4, 1, 3))]
    pallas_call x0 -> x3, Pallas kernels: none -> 95.8 us  [call(): pl.pallas_call(body, out_shape=outs, in_specs=kinds, out_specs=jax.tree.m...]
    another operation x18 -> x0, local copies, waits for them, and re-layouts: 92.7 us -> none  [the longest x2 41.3 us: apply_channel(): tile = matrix.reshape(2, row_blocks, span, col_blocks, span)]
    unnamed x19 -> x0, local copies, waits for them, and re-layouts: 86.7 us -> none
    unnamed x2 -> x0, other arithmetic: 61.7 us -> none
    all_to_all x2 -> x1, blocking collectives: 125 us -> 65 us  [exchange(): lax.all_to_all(value, HI_GRP, split_axis=0, concat_axis=0, tiled=True)]
  transfers between devices with their start and end apart: 4 -> 1, of which waited for: 4 -> 1; matrix products, arithmetic and copies ran while one was open for 3% -> 0% of each run, Pallas kernels for 0% -> 0%
where the time goes in v1:
time: 289 us; the launch traced here: 288 us
  blocking collectives  128 us (44%)
  Pallas kernels  95.8 us (33%)
  waiting for transfers between devices  53.3 us (18%)
  starting transfers between devices  6.58 us (2%)
    pallas_call x3, Pallas kernels, call(): pl.pallas_call(body, out_shape=outs, in_specs=kinds, out_specs=jax.tree.m...  95.8 us
    all_to_all x1, blocking collectives, exchange(): lax.all_to_all(value, HI_GRP, split_axis=0, concat_axis=0, tiled=True)  65 us
    psum x1, blocking collectives, per_device(): return (matrix, lax.psum(jnp.sum(trace), HI_GRP) / ROWS)  63.3 us
    all_to_all x1, waiting for transfers between devices, exchange(): lax.all_to_all(value, HI_GRP, split_axis=0, concat_axis=0, tiled=True)  53.3 us
    all_to_all x1, starting transfers between devices, exchange(): lax.all_to_all(value, HI_GRP, split_axis=0, concat_axis=0, tiled=True)  6.58 us
  transfers between devices with their start and end apart: 1, of which 1 were waited for; matrix products, arithmetic and copies ran while one was open for 0% of the time, Pallas kernels for 0%

profile of v1, /device:TPU:0, one launch (start us, length us, event | category | flops | bytes accessed | tf_op | source)
XLA Modules:
  0.0 287.6 jit_solution(17319650456126008114)
XLA Ops:
  0.6 15.6 %shard_map.50 = f32[128,64,128]{2,1,0:T(8,128)} custom-call(s32[2,13]{1,0:T(2,128)} %perm.5, f32[2,64,8192]{2,1,0:T(8,128)} %x.1), custom_call_target="tpu_custom_call" | custom-call | tf_op jit(solution)/shard_map/pallas_call | solution.py:229
  16.3 65.0 %all_to_all.10 = f32[128,64,128]{2,1,0:T(8,128)} all-to-all(f32[128,64,128]{2,1,0:T(8,128)} %shard_map.50), channel_id=1, replica_groups=mesh['hi'=64,'grp'=2] {'hi','grp'}, dimensions={0} | all-to-all | bytes 8388608 | tf_op jit(solution)/shard_map/all_to_all | solution.py:273
  81.3 37.0 %shard_map.51 = f32[8192,128]{1,0:T(8,128)} custom-call(s32[2,13]{1,0:T(2,128)} %perm.5, f32[2,2,16,16]{3,2,1,0:T(8,128)} %sup.3, f32[8192,128]{1,0:T(8,128)} %bitcast.4), custom_call_target="tpu_custom_call" | custom-call | tf_op jit(solution)/shard_map/pallas_call | solution.py:229
  118.3 6.6 %all-to-all-start.1 = ((f32[128,64,128]{2,1,0:T(8,128)}), f32[128,64,128]{2,1,0:T(8,128)}, u32[]{:S(2)}, u32[]{:S(2)}) async-start(f32[128,64,128]{2,1,0:T(8,128)} %bitcast.3), calls=%async_computation.1 | async-start | bytes 8388608 | tf_op jit(solution)/shard_map/all_to_all | solution.py:273
  124.9 53.3 %all-to-all-done.1.x = f32[128,64,128]{2,1,0:T(8,128)} async-done(((f32[128,64,128]{2,1,0:T(8,128)}), f32[128,64,128]{2,1,0:T(8,128)}, u32[]{:S(2)}, u32[]{:S(2)}) %all-to-all-start.1) | async-done | bytes 4194336 | tf_op jit(solution)/shard_map/all_to_all | solution.py:273
  178.2 43.2 %shard_map.52 = (f32[2,64,8192]{2,1,0:T(8,128)}, f32[1,128]{1,0:T(1,128)}) custom-call(s32[2,13]{1,0:T(2,128)} %perm.5, f32[2,2,16,16]{3,2,1,0:T(8,128)} %sup.3, s32[1]{0:T(128)} %bitcast.where, f32[128,64,128]{2,1,0:T(8,128)} %all-to-all-done.1.x), custom_call_target="tpu_custom_call" | custom-call | tf_op jit(solution)/shard_map/pallas_call | solution.py:229
  221.3 1.2 reduce_sum.9
  222.5 63.3 %psum.7 = f32[]{:T(128)} all-reduce(f32[]{:T(128)} %reduce_sum.9), channel_id=1, replica_groups=mesh['hi'=64,'grp'=2] {'hi','grp'}, use_global_device_ids=true, to_apply=%region_1.0 | all-reduce | flops 1 | bytes 8 | tf_op jit(solution)/shard_map/psum | solution.py:281
Async XLA Ops:
  118.3 59.9 %all-to-all-start.1 = ((f32[128,64,128]{2,1,0:T(8,128)}), f32[128,64,128]{2,1,0:T(8,128)}, u32[]{:S(2)}, u32[]{:S(2)}) async-start(f32[128,64,128]{2,1,0:T(8,128)} %bitcast.3), calls=%async_computation.1 | async-start | bytes 8388608 | tf_op jit(solution)/shard_map/all_to_all | solution.py:273

commit v2 on v1

v2 whole, which is shorter than its diff:
```python
import functools

import jax
import jax.numpy as jnp
from jax import lax
from jax.experimental import pallas as pl
from jax.experimental.pallas import tpu as pltpu
from jax.sharding import Mesh
from jax.sharding import PartitionSpec as P

ROWS = 8192
QUBITS = 13
HI_GRP = ("hi", "grp")
F32 = jnp.float32
BF16 = jnp.bfloat16
SMEM = pltpu.SMEM
VMEM = pltpu.VMEM


def fill(table, weights):
    table[0] = jnp.int32(0)
    for k, weight in enumerate(weights):
        for j in range(1 << k):
            table[(1 << k) + j] = table[j] + weight


def one_shl(amount):
    return jnp.left_shift(jnp.int32(1), amount)


def column_order(perm, order):
    for j in range(4):
        order[j] = perm[0, j]
    count = jnp.int32(4)
    for q in range(QUBITS):
        order[count] = jnp.int32(q)
        mine = perm[0, 0] == q
        for j in range(1, 4):
            mine = mine | (perm[0, j] == q)
        count = count + jnp.where(mine, 0, 1)


def tile_at(vreg):
    return pl.ds(pl.multiple_of(vreg * 8, 8), 8)


def insert_zero(index, bit):
    low = index & (one_shl(bit) - 1)
    return (index - low) * 2 + low


def swap_stage(buf, sub, bit, unroll=8):
    step = 1 << sub
    keep = (lax.broadcasted_iota(jnp.int32, (8, 128), 0) & step) == 0

    @pl.loop(0, 512 // unroll)
    def _(i):
        pairs = []
        for k in range(unroll):
            v = insert_zero(i * unroll + k, bit)
            w = v + one_shl(bit)
            pairs.append((v, w, buf[tile_at(v), :], buf[tile_at(w), :]))
        for v, w, a, b in pairs:
            buf[tile_at(v), :] = jnp.where(keep, a, pltpu.roll(b, step, 0))
            buf[tile_at(w), :] = jnp.where(keep, pltpu.roll(a, 8 - step, 0), b)


def exchange_bits(buf, loc, occ, sub, place):
    swap_stage(buf, sub, place - 3)
    here, there = occ[sub], occ[place]
    occ[sub] = there
    occ[place] = here
    loc[there] = jnp.int32(sub)
    loc[here] = place


def settle_sublanes(buf, loc, occ, wanted, bits):
    for sub in range(3):
        best = jnp.int32(-1)
        for bit in bits:
            best = jnp.where(wanted(bit) & (loc[bit] >= 3), loc[bit], best)

        @pl.when(jnp.logical_not(wanted(occ[sub])) & (best >= 3))
        def _():
            exchange_bits(buf, loc, occ, sub, best)


def spread(perm, x, out, lanes, y, order, loc, occ, tc, te):
    column_order(perm, order)
    top = order[12]
    for q in range(QUBITS):
        place = jnp.where(jnp.int32(q) < top, q, q - 1)
        loc[q] = jnp.where(jnp.int32(q) == top, jnp.int32(13), place)
        occ[place] = jnp.int32(q)
    for q in range(QUBITS):

        @pl.when(jnp.int32(q) != top)
        def _():
            occ[loc[q]] = jnp.int32(q)

    step = one_shl(top - 7)

    @pl.loop(0, 16)
    def _(pair):
        for k in range(2):
            m = pair * 2 + k
            first = insert_zero(m, top - 7)
            for part in range(2):
                halves = [
                    x[part, :, pl.ds(pl.multiple_of(t * 128, 128), 128)]
                    for t in (first, first + step)
                ]
                start = pl.multiple_of(part * 4096 + m * 128, 128)
                y[pl.ds(start, 128), :] = jnp.concatenate(halves, axis=0).T

    def local(bit):
        found = bit == order[0]
        for i in range(1, 6):
            found = found | (bit == order[i])
        return found

    settle_sublanes(y, loc, occ, local, [order[i] for i in range(6)])
    for s in range(3):
        found = jnp.int32(0)
        for i in range(6):
            found = jnp.where(order[i] == occ[s], i, found)
        lanes[s] = found
    count = jnp.int32(3)
    for i in range(6):
        lanes[count] = jnp.int32(i)
        count = count + jnp.where(loc[order[i]] >= 3, 1, 0)
    fill(tc, [one_shl(loc[order[lanes[3 + i]]] - 3) for i in range(3)])
    fill(te, [one_shl(loc[order[6 + i]] - 3) for i in range(6)])

    @pl.loop(0, 16)
    def _(group):
        for k in range(4):
            e = group * 4 + k
            base = te[e]
            tiles = [y[tile_at(base + tc[j] + part * 512), :] for part in range(2) for j in range(8)]
            turned = jnp.concatenate(tiles, axis=0).T
            out[e] = turned[:64]
            out[64 + e] = turned[64:]


def split_bf16(value):
    high = value.astype(BF16)
    return high, (value - high.astype(F32)).astype(BF16)


def build_weights(sup, layer, pair, major_is_row, lanes, high_ref, low_ref):
    def canonical(lane):
        if lanes is None:
            return lane & 63
        total = jnp.zeros_like(lane)
        for k in range(6):
            total = total + jnp.left_shift(jnp.right_shift(lane, k) & 1, lanes[k])
        return total

    def uv(major, lane):
        minor = jnp.right_shift(lane, 2 * pair) & 3
        return 4 * major + minor if major_is_row else 4 * minor + major

    row = lax.broadcasted_iota(jnp.int32, (512, 16), 0)
    col16 = lax.broadcasted_iota(jnp.int32, (512, 16), 1)

    def one_hot(lane):
        hit = uv(jnp.right_shift(row, 7), lane) == col16
        return jnp.where(hit, 1.0, 0.0).astype(BF16)

    expand_out = one_hot(row & 63)
    expand_in = expand_out if lanes is None else one_hot(canonical(row))
    dims = (((1,), (1,)), ((), ()))
    raw_in = lax.broadcasted_iota(jnp.int32, (512, 128), 0) & 127
    lane_in = canonical(raw_in)
    raw_out = lax.broadcasted_iota(jnp.int32, (512, 128), 1)
    keep = 63 & ~(3 << (2 * pair))
    same_rest = (lane_in & keep) == (raw_out & keep)
    part_in = jnp.right_shift(raw_in, 6)
    part_out = jnp.right_shift(raw_out, 6)
    sign = jnp.where(part_out >= part_in, 1.0, -1.0).astype(F32)
    parts = [split_bf16(sup[layer, part]) for part in range(2)]
    for which, ref in enumerate((high_ref, low_ref)):
        half = [
            lax.dot_general(expand_in, parts[p][which], dims, preferred_element_type=F32).astype(BF16)
            for p in range(2)
        ]
        for block in range(4):
            target = expand_out[block * 128 : (block + 1) * 128]
            real, imag = (
                lax.dot_general(h, target, dims, preferred_element_type=F32) for h in half
            )
            value = jnp.where(part_in == part_out, real, sign * imag)
            ref[:, block * 128 : (block + 1) * 128] = jnp.where(same_rest, value, 0.0).astype(BF16)


def apply_pair(z, pair, ta, rv, xh, xl, mixed, high_ref, low_ref):
    @pl.loop(0, 4)
    def _(other):
        first = other * 4 if pair == 0 else other
        stride = 1 if pair == 0 else 4
        bases = [ta[first + stride * k] for k in range(4)]

        @pl.loop(0, 16)
        def _(r):
            for half in range(2):
                v0 = rv[r * 4 + half * 2]
                v1 = rv[r * 4 + half * 2 + 1]
                rows = pl.ds(pl.multiple_of(r * 32 + half * 16, 16), 16)
                for k in range(4):
                    both = [z[tile_at(bases[k] + v), :] for v in (v0, v1)]
                    high, low = split_bf16(jnp.concatenate(both, axis=0))
                    xh[rows, k * 128 : (k + 1) * 128] = high
                    xl[rows, k * 128 : (k + 1) * 128] = low

        total = jnp.dot(xh[...], high_ref[...], preferred_element_type=F32)
        total += jnp.dot(xl[...], high_ref[...], preferred_element_type=F32)
        total += jnp.dot(xh[...], low_ref[...], preferred_element_type=F32)
        mixed[...] = total

        @pl.loop(0, 16)
        def _(r):
            for j in range(4):
                v = rv[r * 4 + j]
                rows = pl.ds(pl.multiple_of(r * 32 + j * 8, 8), 8)
                for k in range(4):
                    z[tile_at(bases[k] + v), :] = mixed[rows, k * 128 : (k + 1) * 128]


def channel(sup, layer, major_is_row, lanes, z, ta, rv, xh, xl, mixed, high_ref, low_ref):
    for pair in range(2):
        build_weights(sup, layer, pair, major_is_row, lanes if pair == 0 else None, high_ref, low_ref)
        apply_pair(z, pair, ta, rv, xh, xl, mixed, high_ref, low_ref)


def middle(perm, lanes, sup, x, out, rows_out, z, xh, xl, mixed, high, low,
           final, outpos, loc, occ, rest, ta, rv, ti, td):
    for q in range(QUBITS):
        bit = perm[0, perm[1, q]]
        final[q] = bit
        outpos[bit] = jnp.int32(q)
        loc[q] = jnp.int32(q)
        occ[q] = jnp.int32(q)
    z[...] = x[...]
    mixes = [perm[0, j] for j in range(4)]

    def mixed_bit(bit):
        found = bit == mixes[0]
        for m in mixes[1:]:
            found = found | (bit == m)
        return found

    everything = [jnp.int32(q) for q in range(QUBITS)]
    stays = lambda bit: outpos[bit] < 6
    settle_sublanes(z, loc, occ, lambda bit: jnp.logical_not(mixed_bit(bit)) & stays(bit), everything)
    settle_sublanes(z, loc, occ, lambda bit: jnp.logical_not(mixed_bit(bit)), everything)
    count = jnp.int32(0)
    for place in range(3, QUBITS):
        rest[count] = jnp.int32(place)
        count = count + jnp.where(mixed_bit(occ[place]), 0, 1)
    fill(ta, [one_shl(loc[m] - 3) for m in mixes])
    fill(rv, [one_shl(rest[j] - 3) for j in range(6)])
    channel(sup, 0, True, lanes, z, ta, rv, xh, xl, mixed, high, low)
    settle_sublanes(z, loc, occ, stays, everything)
    for s in range(3):
        rows_out[s] = outpos[occ[s]]
    count = jnp.int32(3)
    for q in range(6):
        rows_out[count] = jnp.int32(q)
        count = count + jnp.where(loc[final[q]] >= 3, 1, 0)
    fill(ti, [one_shl(loc[final[rows_out[3 + i]]] - 3) for i in range(3)])
    fill(td, [one_shl(loc[final[6 + i]] - 3) for i in range(7)])

    @pl.loop(0, 64)
    def _(i):
        for k in range(2):
            d = i * 2 + k
            base = td[d]
            for j in range(8):
                out[tile_at(d * 8 + j), :] = z[tile_at(base + ti[j]), :]


def gather_back(perm, lanes, where, sup, x, out, trace, y, b0, b1, xh, xl, mixed, high, low,
                order, inv, loc, occ, ta, rv):
    column_order(perm, order)
    for i in range(QUBITS):
        inv[order[i]] = jnp.int32(i)
    for q in range(QUBITS):
        place = inv[perm[0, perm[1, q]]]
        loc[q] = place
        occ[place] = jnp.int32(q)

    @pl.loop(0, 32)
    def _(pair):
        for k in range(2):
            p = pair * 2 + k
            turned = jnp.concatenate([x[p], x[p + 64]], axis=0).T
            real, imag = turned[:64], turned[64:]
            start = pl.multiple_of(p * 64, 64)
            y[pl.ds(start, 64), :] = jnp.concatenate([real[:, :64], imag[:, :64]], axis=1)
            y[pl.ds(start + 4096, 64), :] = jnp.concatenate([real[:, 64:], imag[:, 64:]], axis=1)

    for sub in range(3):
        for other in range(sub + 1, 3):

            @pl.when(loc[4 + sub] == other)
            def _():
                exchange_bits(y, loc, occ, other, jnp.int32(12))

        @pl.when(loc[4 + sub] >= 3)
        def _():
            exchange_bits(y, loc, occ, sub, loc[4 + sub])

    fill(ta, [one_shl(loc[q] - 3) for q in range(4)])
    fill(rv, [one_shl(loc[q] - 3) for q in range(7, QUBITS)])
    channel(sup, 1, False, lanes, y, ta, rv, xh, xl, mixed, high, low)

    @pl.loop(0, 32)
    def _(pair):
        for k, b in enumerate((b0, b1)):
            base = rv[pair * 2 + k]
            for low_bits in range(16):
                b[pl.ds(low_bits, 8, stride=16), :] = y[tile_at(base + ta[low_bits]), :]
        for k, b in enumerate((b0, b1)):
            columns = pl.ds(pl.multiple_of((pair * 2 + k) * 128, 128), 128)
            turned = b[...].T
            out[0, :, columns] = turned[:64]
            out[1, :, columns] = turned[64:]

    me = where[0]
    block = out[0, :, pl.ds(pl.multiple_of((me // 2) * 128, 128), 128)]
    lane = lax.broadcasted_iota(jnp.int32, (64, 128), 1)
    row = lax.broadcasted_iota(jnp.int32, (64, 128), 0)
    kept = jnp.where(lane == row + (me % 2) * 64, block, 0.0)
    folded = kept[0:8]
    for j in range(1, 8):
        folded = folded + kept[8 * j : 8 * j + 8]
    trace[...] = folded


def add_all(x, total, parts, send, recv):
    me = lax.axis_index(HI_GRP)
    devices = parts.shape[0]

    def place(k):
        d = lax.rem(me + k, devices)
        return {"hi": d // 2, "grp": lax.rem(d, 2)}

    barrier = pltpu.get_barrier_semaphore()

    @pl.loop(1, devices)
    def _(k):
        pl.semaphore_signal(
            barrier, inc=1, device_id=place(k), device_id_type=pl.DeviceIdType.MESH
        )

    pl.semaphore_wait(barrier, devices - 1)

    def copy(k):
        return pltpu.make_async_remote_copy(
            src_ref=x,
            dst_ref=parts.at[k],
            send_sem=send.at[k],
            recv_sem=recv.at[k],
            device_id=place(k),
            device_id_type=pl.DeviceIdType.MESH,
        )

    @pl.loop(1, devices)
    def _(k):
        copy(k).start()

    parts[0] = x[...]

    @pl.loop(1, devices)
    def _(k):
        copy(k).wait()

    grand = jnp.sum(parts[...], axis=0)
    total[...] = jnp.sum(jnp.sum(grand, axis=1, keepdims=True), axis=0, keepdims=True) / ROWS


def call(body, outs, out_smem, n_smem, n_args, scratch, args):
    smem = pl.BlockSpec(memory_space=SMEM)
    vmem = pl.BlockSpec(memory_space=VMEM)
    return pl.pallas_call(
        body,
        out_shape=outs,
        in_specs=[smem if i < n_smem else vmem for i in range(n_args)],
        out_specs=tuple(smem if i in out_smem else vmem for i in range(len(outs))),
        scratch_shapes=scratch,
        compiler_params=pltpu.CompilerParams(vmem_limit_bytes=60 * 2**20),
    )(*args)


def table(*sizes):
    return [SMEM((n,), jnp.int32) for n in sizes]


def square(dtype):
    return VMEM((512, 512), dtype)


FULL = VMEM((8192, 128), F32)
BLOCK = VMEM((128, 128), F32)
MAP = jax.ShapeDtypeStruct((8,), jnp.int32)
WORK = [square(BF16), square(BF16), square(F32), square(BF16), square(BF16)]


def spread_call(perm, x):
    return call(
        spread, (jax.ShapeDtypeStruct((128, 64, 128), F32), MAP), (1,), 1, 2,
        [FULL] + table(14, 14, 14, 8, 64), (perm, x),
    )


def middle_call(perm, lanes, sup, x):
    return call(
        middle, (jax.ShapeDtypeStruct((8192, 128), F32), MAP), (1,), 2, 4,
        [FULL] + WORK + table(13, 13, 13, 13, 13, 16, 64, 8, 128), (perm, lanes, sup, x),
    )


def back_call(perm, lanes, where, sup, x):
    return call(
        gather_back,
        (jax.ShapeDtypeStruct((2, 64, 8192), F32), jax.ShapeDtypeStruct((8, 128), F32)),
        (), 3, 5,
        [FULL, BLOCK, BLOCK] + WORK + table(14, 13, 13, 13, 16, 64), (perm, lanes, where, sup, x),
    )


def add_all_call(block, devices):
    vmem = pl.BlockSpec(memory_space=VMEM)
    return pl.pallas_call(
        add_all,
        out_shape=jax.ShapeDtypeStruct((1, 1), F32),
        in_specs=[vmem],
        out_specs=vmem,
        scratch_shapes=[
            VMEM((devices, 8, 128), F32),
            pltpu.SemaphoreType.DMA((devices,)),
            pltpu.SemaphoreType.DMA((devices,)),
        ],
        compiler_params=pltpu.CompilerParams(collective_id=1, has_side_effects=True),
    )(block)


def exchange(value):
    return lax.all_to_all(value, HI_GRP, split_axis=0, concat_axis=0, tiled=True)


def per_device(rho, perm, superop):
    sent, lanes = spread_call(perm, rho)
    mid, rows = middle_call(perm, lanes, superop, exchange(sent).reshape(8192, 128))
    where = lax.axis_index(HI_GRP).astype(jnp.int32).reshape(1)
    matrix, trace = back_call(perm, rows, where, superop, exchange(mid.reshape(128, 64, 128)))
    return matrix, add_all_call(trace, lax.axis_size(HI_GRP)).reshape(())


def solution(mesh):
    in_specs = (P(None, HI_GRP, None), P(), P())
    out_specs = (P(None, HI_GRP, None), P())
    return jax.shard_map(
        per_device, mesh=mesh, in_specs=in_specs, out_specs=out_specs, check_vma=False
    )
```

time: 289 us -> 223 us (0.77)
  blocking collectives: 128 us -> 65 us
    psum x1 -> x0, blocking collectives: 63.3 us -> none  [per_device(): return (matrix, lax.psum(jnp.sum(trace), HI_GRP) / ROWS)]
    pallas_call x3 -> x4, Pallas kernels: 95.8 us -> 94.3 us  [the longest x3 73.6 us: call(): pl.pallas_call(body, out_shape=outs, in_specs=[smem if i < n_smem else vm...]
where the time goes in v2:
time: 223 us; the launch traced here: 222 us
  Pallas kernels  94.3 us (42%)
  blocking collectives  65 us (29%)
  waiting for transfers between devices  53.3 us (24%)
  starting transfers between devices  6.59 us (3%)
  between operations  2.41 us (1%)
    pallas_call x3, Pallas kernels, call(): pl.pallas_call(body, out_shape=outs, in_specs=[smem if i < n_smem else vm...  73.6 us
    all_to_all x1, blocking collectives, exchange(): lax.all_to_all(value, HI_GRP, split_axis=0, concat_axis=0, tiled=True)  65 us
    all_to_all x1, waiting for transfers between devices, exchange(): lax.all_to_all(value, HI_GRP, split_axis=0, concat_axis=0, tiled=True)  53.3 us
    pallas_call x1, Pallas kernels, add_all_call(): pl.pallas_call(add_all, out_shape=jax.ShapeDtypeStruct((1, 1), F32), in_s...  20.7 us
    all_to_all x1, starting transfers between devices, exchange(): lax.all_to_all(value, HI_GRP, split_axis=0, concat_axis=0, tiled=True)  6.59 us
  transfers between devices with their start and end apart: 1, of which 1 were waited for; matrix products, arithmetic and copies ran while one was open for 0% of the time, Pallas kernels for 0%

profile of v2, /device:TPU:0, one launch (start us, length us, event | category | flops | bytes accessed | tf_op | source)
XLA Modules:
  0.0 221.6 jit_solution(6847169359757503259)
XLA Ops:
  0.6 8.8 %shard_map.50 = (f32[128,64,128]{2,1,0:T(8,128)}, s32[8]{0:T(128)}) custom-call(s32[2,13]{1,0:T(2,128)} %perm.5, f32[2,64,8192]{2,1,0:T(8,128)} %x.1), custom_call_target="tpu_custom_call" | custom-call | tf_op jit(solution)/shard_map/pallas_call | solution.py:386
  9.4 65.0 %all_to_all.10 = f32[128,64,128]{2,1,0:T(8,128)} all-to-all(f32[128,64,128]{2,1,0:T(8,128)} %get-tuple-element.9), channel_id=1, replica_groups=mesh['hi'=64,'grp'=2] {'hi','grp'}, dimensions={0} | all-to-all | bytes 8388608 | tf_op jit(solution)/shard_map/all_to_all | solution.py:450
  74.4 29.2 %shard_map.51 = (f32[8192,128]{1,0:T(8,128)}, s32[8]{0:T(128)}) custom-call(s32[2,13]{1,0:T(2,128)} %perm.5, s32[8]{0:T(128)} %get-tuple-element.8.lanes, f32[2,2,16,16]{3,2,1,0:T(8,128)} %sup.3, f32[8192,128]{1,0:T(8,128)} %bitcast.4), custom_call_target="tpu_custom_call" | custom-call | tf_op jit(solution)/shard_map/pallas_call | solution.py:386
  103.7 6.6 %all-to-all-start.1 = ((f32[128,64,128]{2,1,0:T(8,128)}), f32[128,64,128]{2,1,0:T(8,128)}, u32[]{:S(2)}, u32[]{:S(2)}) async-start(f32[128,64,128]{2,1,0:T(8,128)} %bitcast.5), calls=%async_computation.1 | async-start | bytes 8388608 | tf_op jit(solution)/shard_map/all_to_all | solution.py:450
  110.3 53.3 %all-to-all-done.1.x = f32[128,64,128]{2,1,0:T(8,128)} async-done(((f32[128,64,128]{2,1,0:T(8,128)}), f32[128,64,128]{2,1,0:T(8,128)}, u32[]{:S(2)}, u32[]{:S(2)}) %all-to-all-start.1) | async-done | bytes 4194336 | tf_op jit(solution)/shard_map/all_to_all | solution.py:450
  163.5 35.6 %shard_map.52 = (f32[2,64,8192]{2,1,0:T(8,128)}, f32[8,128]{1,0:T(8,128)}) custom-call(s32[2,13]{1,0:T(2,128)} %perm.5, s32[8]{0:T(128)} %get-tuple-element.10.lanes, s32[1]{0:T(128)} %bitcast.1.where, f32[2,2,16,16]{3,2,1,0:T(8,128)} %sup.3, f32[128,64,128]{2,1,0:T(8,128)} %all-to-all-done.1.x), custom_call_target="tpu_custom_call" | custom-call | tf_op jit(solution)/shard_map/pallas_call | solution.py:386
  199.1 20.7 %shard_map.53 = f32[1,1]{1,0:T(1,128)} custom-call(f32[8,128]{1,0:T(8,128)} %get-tuple-element.13.x), custom_call_target="tpu_custom_call" | custom-call | tf_op jit(solution)/shard_map/pallas_call | solution.py:435
Async XLA Ops:
  103.7 59.9 %all-to-all-start.1 = ((f32[128,64,128]{2,1,0:T(8,128)}), f32[128,64,128]{2,1,0:T(8,128)}, u32[]{:S(2)}, u32[]{:S(2)}) async-start(f32[128,64,128]{2,1,0:T(8,128)} %bitcast.5), calls=%async_computation.1 | async-start | bytes 8388608 | tf_op jit(solution)/shard_map/all_to_all | solution.py:450

commit v3 on v2

--- a/solution.py
+++ b/solution.py
@@ -2,6 +2,7 @@
 
 import jax
 import jax.numpy as jnp
+import numpy as np
 from jax import lax
 from jax.experimental import pallas as pl
 from jax.experimental.pallas import tpu as pltpu
@@ -85,7 +86,11 @@
             exchange_bits(buf, loc, occ, sub, best)
 
 
-def spread(perm, x, out, lanes, y, order, loc, occ, tc, te):
+def own_slots(slots, where):
+    return [slots[part, where[0]] ^ (64 * part) for part in range(PARTS)]
+
+
+def spread(perm, slots, where, x, out, lanes, y, order, loc, occ, tc, te):
     column_order(perm, order)
     top = order[12]
     for q in range(QUBITS):
@@ -131,6 +136,7 @@
         count = count + jnp.where(loc[order[i]] >= 3, 1, 0)
     fill(tc, [one_shl(loc[order[lanes[3 + i]]] - 3) for i in range(3)])
     fill(te, [one_shl(loc[order[6 + i]] - 3) for i in range(6)])
+    mine = own_slots(slots, where)
 
     @pl.loop(0, 16)
     def _(group):
@@ -139,8 +145,10 @@
             base = te[e]
             tiles = [y[tile_at(base + tc[j] + part * 512), :] for part in range(2) for j in range(8)]
             turned = jnp.concatenate(tiles, axis=0).T
-            out[e] = turned[:64]
-            out[64 + e] = turned[64:]
+            for j in range(16):
+                part = j % 8
+                v = slots[part, e + 64 * (j // 8)] ^ mine[part]
+                out[tile_at(v), :] = turned[8 * j : 8 * j + 8]
 
 
 def split_bf16(value):
@@ -233,15 +241,84 @@
         apply_pair(z, pair, ta, rv, xh, xl, mixed, high_ref, low_ref)
 
 
-def middle(perm, lanes, sup, x, out, rows_out, z, xh, xl, mixed, high, low,
-           final, outpos, loc, occ, rest, ta, rv, ti, td):
+def trace_share(perm, where, sup, z, loc, outpos, final, order, tu, tc):
+    column_order(perm, order)
+    me = where[0]
+
+    def place_of(bit):
+        found = jnp.int32(0)
+        for i in range(QUBITS):
+            found = jnp.where(order[i] == bit, i, found)
+        return found
+
+    lane = lax.broadcasted_iota(jnp.int32, (16, 128), 1)
+    group = jnp.zeros((16, 128), jnp.int32)
+    for j in range(4):
+        place = place_of(final[j])
+        local = jnp.right_shift(lane, jnp.minimum(place, 5)) & 1
+        remote_bit = jnp.right_shift(me, jnp.maximum(place - 6, 0)) & 1
+        group = group + jnp.left_shift(jnp.where(place < 6, local, remote_bit), j)
+    row16 = lax.broadcasted_iota(jnp.int32, (16, 16), 0)
+    col16 = lax.broadcasted_iota(jnp.int32, (16, 16), 1)
+    hot = jnp.where(lax.broadcasted_iota(jnp.int32, (16, 128), 0) == group, 1.0, 0.0).astype(F32)
+    single = []
+    for part in range(2):
+        s = sup[1, part]
+        tau = s[0:1] + s[5:6] + s[10:11] + s[15:16]
+        both = []
+        for pair in range(2):
+            pick = 4 * (jnp.right_shift(row16, 2 * pair) & 3) + (jnp.right_shift(col16, 2 * pair) & 3)
+            value = jnp.zeros((16, 16), F32)
+            for uv in range(16):
+                value = jnp.where(pick == uv, tau[:, uv : uv + 1], value)
+            both.append(value)
+        single.append(both)
+    real = single[0][0] * single[0][1] - single[1][0] * single[1][1]
+    imag = single[0][0] * single[1][1] + single[1][0] * single[0][1]
+    exact = functools.partial(jnp.dot, precision=lax.Precision.HIGHEST, preferred_element_type=F32)
+    weight = jnp.where(lane < 64, exact(real, hot), -exact(imag, hot))
+
+    fill(tu, [one_shl(loc[final[j]]) for j in range(4)])
+
+    def weight_of(bit):
+        return jnp.where(outpos[bit] >= 4, one_shl(loc[bit]), 0)
+
+    fill(tc, [weight_of(order[i]) for i in range(6)])
+    base = jnp.int32(0)
+    for i in range(6, QUBITS):
+        base = base + weight_of(order[i]) * (jnp.right_shift(me, i - 6) & 1)
+    lane1 = lax.broadcasted_iota(jnp.int32, (1, 128), 1) & 63
+    sums = jnp.zeros((1, 128), F32)
+
+    def column(c, rows):
+        start = base + tc[c]
+        return tuple(
+            jnp.where(lane1 == c, z[pl.ds(start + tu[u], 1), :], rows[u]) for u in range(16)
+        )
+
+    rows = lax.fori_loop(0, 64, column, tuple(sums for _ in range(16)))
+    for u in range(16):
+        sums = sums + weight[u : u + 1] * rows[u]
+    return sums
+
+
+def middle(perm, lanes, slots, where, sup, x, out, rows_out, share, z, xh, xl, mixed, high, low,
+           final, outpos, loc, occ, rest, ta, rv, ti, td, order, tu, tc):
     for q in range(QUBITS):
         bit = perm[0, perm[1, q]]
         final[q] = bit
         outpos[bit] = jnp.int32(q)
         loc[q] = jnp.int32(q)
         occ[q] = jnp.int32(q)
-    z[...] = x[...]
+    mine = own_slots(slots, where)
+
+    @pl.loop(0, 64)
+    def _(i):
+        for k in range(2):
+            d = i * 2 + k
+            for part in range(PARTS):
+                z[tile_at(d * 8 + part), :] = x[tile_at(slots[part, d] ^ mine[part]), :]
+
     mixes = [perm[0, j] for j in range(4)]
 
     def mixed_bit(bit):
@@ -261,6 +338,7 @@
     fill(ta, [one_shl(loc[m] - 3) for m in mixes])
     fill(rv, [one_shl(rest[j] - 3) for j in range(6)])
     channel(sup, 0, True, lanes, z, ta, rv, xh, xl, mixed, high, low)
+    share[...] = trace_share(perm, where, sup, z, loc, outpos, final, order, tu, tc)
     settle_sublanes(z, loc, occ, stays, everything)
     for s in range(3):
         rows_out[s] = outpos[occ[s]]
@@ -277,10 +355,10 @@
             d = i * 2 + k
             base = td[d]
             for j in range(8):
-                out[tile_at(d * 8 + j), :] = z[tile_at(base + ti[j]), :]
-
-
-def gather_back(perm, lanes, where, sup, x, out, trace, y, b0, b1, xh, xl, mixed, high, low,
+                out[tile_at(slots[j, d] ^ mine[j]), :] = z[tile_at(base + ti[j]), :]
+
+
+def gather_back(perm, lanes, slots, where, sup, x, out, y, b0, b1, xh, xl, mixed, high, low,
                 order, inv, loc, occ, ta, rv):
     column_order(perm, order)
     for i in range(QUBITS):
@@ -289,12 +367,16 @@
         place = inv[perm[0, perm[1, q]]]
         loc[q] = place
         occ[place] = jnp.int32(q)
+    mine = own_slots(slots, where)
 
     @pl.loop(0, 32)
     def _(pair):
         for k in range(2):
             p = pair * 2 + k
-            turned = jnp.concatenate([x[p], x[p + 64]], axis=0).T
+            tiles = [
+                x[tile_at(slots[j, p + 64 * k] ^ mine[j]), :] for k in range(2) for j in range(PARTS)
+            ]
+            turned = jnp.concatenate(tiles, axis=0).T
             real, imag = turned[:64], turned[64:]
             start = pl.multiple_of(p * 64, 64)
             y[pl.ds(start, 64), :] = jnp.concatenate([real[:, :64], imag[:, :64]], axis=1)
@@ -327,57 +409,183 @@
             out[0, :, columns] = turned[:64]
             out[1, :, columns] = turned[64:]
 
-    me = where[0]
-    block = out[0, :, pl.ds(pl.multiple_of((me // 2) * 128, 128), 128)]
-    lane = lax.broadcasted_iota(jnp.int32, (64, 128), 1)
-    row = lax.broadcasted_iota(jnp.int32, (64, 128), 0)
-    kept = jnp.where(lane == row + (me % 2) * 64, block, 0.0)
-    folded = kept[0:8]
-    for j in range(1, 8):
-        folded = folded + kept[8 * j : 8 * j + 8]
-    trace[...] = folded
-
-
-def add_all(x, total, parts, send, recv):
-    me = lax.axis_index(HI_GRP)
-    devices = parts.shape[0]
-
-    def place(k):
-        d = lax.rem(me + k, devices)
-        return {"hi": d // 2, "grp": lax.rem(d, 2)}
-
+
+LINKS = 6
+PARTS = 8
+
+
+def part_links(part):
+    return [(t, (part + t) % 8) for t in range(8) if (part + t) % 8 < LINKS]
+
+
+def slot_table():
+    low_high = ((4, 5), (6, 0), (2, 3))
+    table = np.zeros((PARTS, 128), np.int32)
+    for part in range(PARTS):
+        place = {link: 1 << (5 - s) for s, (_, link) in enumerate(part_links(part))}
+        weight = [0] * 7
+        weight[1] = 512
+        for axis, (low, high) in enumerate(low_high):
+            weight[low] = place[2 * axis]
+            weight[high] = place[2 * axis] | place[2 * axis + 1]
+        for device in range(128):
+            for bit in range(7):
+                if device >> bit & 1:
+                    table[part, device] ^= weight[bit]
+        table[part] += 64 * part
+    return table
+
+
+def swap_all(with_sum, *refs):
+    if with_sum:
+        x, mine, out, total, shares, share_send, share_recv, *refs = refs
+    else:
+        x, out, *refs = refs
+    held, (send, recv, first_send, first_recv, out_sem) = refs[:7], refs[7:]
+    hi = lax.axis_index("hi")
+    grp = lax.axis_index("grp")
+    bits = [lax.rem(hi // (1 << k), 2) for k in range(6)]
+
+    def flip(k):
+        return (1 - 2 * bits[k]) * (1 << k)
+
+    core = {"hi": hi + flip(0), "grp": grp}
+    link_device = [
+        {"hi": hi + flip(3), "grp": grp},
+        {"hi": hi + flip(3) + flip(4), "grp": grp},
+        {"hi": hi + flip(5), "grp": grp},
+        {"hi": hi + flip(5), "grp": 1 - grp},
+        {"hi": hi + flip(1), "grp": grp},
+        {"hi": hi + flip(1) + flip(2), "grp": grp},
+    ]
+    mesh_ids = pl.DeviceIdType.MESH
     barrier = pltpu.get_barrier_semaphore()
-
-    @pl.loop(1, devices)
-    def _(k):
-        pl.semaphore_signal(
-            barrier, inc=1, device_id=place(k), device_id_type=pl.DeviceIdType.MESH
+    for device in [core] + link_device:
+        pl.semaphore_signal(barrier, inc=1, device_id=device, device_id_type=mesh_ids)
+    pl.semaphore_wait(barrier, 7)
+
+    def remote(src, dst, send_sem, recv_sem, device):
+        return pltpu.make_async_remote_copy(
+            src_ref=src, dst_ref=dst, send_sem=send_sem, recv_sem=recv_sem,
+            device_id=device, device_id_type=mesh_ids,
         )
 
-    pl.semaphore_wait(barrier, devices - 1)
-
-    def copy(k):
-        return pltpu.make_async_remote_copy(
-            src_ref=x,
-            dst_ref=parts.at[k],
-            send_sem=send.at[k],
-            recv_sem=recv.at[k],
-            device_id=place(k),
-            device_id_type=pl.DeviceIdType.MESH,
-        )
-
-    @pl.loop(1, devices)
-    def _(k):
-        copy(k).start()
-
-    parts[0] = x[...]
-
-    @pl.loop(1, devices)
-    def _(k):
-        copy(k).wait()
-
-    grand = jnp.sum(parts[...], axis=0)
-    total[...] = jnp.sum(jnp.sum(grand, axis=1, keepdims=True), axis=0, keepdims=True) / ROWS
+    for p in range(PARTS):
+        pltpu.make_async_copy(x.at[0, p], held[0].at[0, p], first_recv.at[0, p]).start()
+        remote(x.at[1, p], held[0].at[1, p], first_send.at[p], first_recv.at[1, p], core).start()
+
+    def arrived(h, p, s):
+        ref = held[s].at[h, p]
+        sem = first_recv.at[h, p] if s == 0 else recv.at[h, p, s - 1]
+        pltpu.make_async_copy(ref, ref, sem).wait()
+
+    def pick(s, chosen):
+        return tuple(chosen[b] for b in range(1, 7) if b != s)
+
+    def cross(h, p, s, link):
+        for j in range(s):
+            source = {b: slice(None) for b in range(1, 7)}
+            for b in range(j + 1, s):
+                source[b] = 0
+            source[s] = 1
+            target = dict(source)
+            if j:
+                target[j] = 1
+            remote(
+                held[j].at[(h, p) + pick(j, source)], held[s].at[(h, p) + pick(s, target)],
+                send.at[h, p, s - 1], recv.at[h, p, s - 1], link_device[link],
+            ).start()
+
+    def deliver(h, p):
+        for j in range(7):
+            source = {b: slice(None) if b < j else 0 for b in range(1, 7)}
+            target = dict(source)
+            if j:
+                target[j] = 1
+            pltpu.make_async_copy(
+                held[j].at[(h, p) + pick(j, source)],
+                out.at[(h, p) + tuple(target[b] for b in range(1, 7))],
+                out_sem.at[h, p],
+            ).start()
+
+    done = {p: 0 for p in range(PARTS)}
+    if with_sum:
+        own = pltpu.make_async_copy(mine, shares.at[0], share_recv.at[7])
+        own.start()
+        own.wait()
+
+        def double(k):
+            return remote(
+                shares.at[0 : 1 << k], shares.at[1 << k : 2 << k], share_send.at[k],
+                share_recv.at[k], ([core] + link_device)[k],
+            )
+
+    for t in range(8):
+
+        @pl.loop(0, 2)
+        def _(h):
+            for p in range(PARTS):
+                link = (p + t) % 8
+                if link < LINKS:
+                    arrived(h, p, done[p])
+                    cross(h, p, done[p] + 1, link)
+
+        if with_sum and t < 7:
+            if t:
+                double(t - 1).wait()
+            double(t).start()
+        for p in range(PARTS):
+            if (p + t) % 8 < LINKS:
+                done[p] += 1
+
+    @pl.loop(0, 2)
+    def _(h):
+        for p in (0, 7, 1, 2, 3, 4, 5, 6):
+            arrived(h, p, 6)
+            deliver(h, p)
+
+    if with_sum:
+        double(6).wait()
+        grand = jnp.sum(shares[...], axis=0)
+        total[...] = jnp.sum(grand, axis=1, keepdims=True) / ROWS
+
+    for p in range(PARTS):
+        pltpu.make_async_copy(x.at[1, p], x.at[1, p], first_send.at[p]).wait()
+
+    @pl.loop(0, 2)
+    def _(h):
+        for p in range(PARTS):
+            for s in range(1, 7):
+                ref = held[s].at[h, p]
+                pltpu.make_async_copy(ref, ref, send.at[h, p, s - 1]).wait()
+            pltpu.make_async_copy(out.at[h, p], out.at[h, p], out_sem.at[h, p]).wait()
+
+
+def exchange(value, collective_id, share=None):
+    two = (2,) * 6
+    whole = jax.ShapeDtypeStruct((2, PARTS) + two + (8, 128), F32)
+    dma = pltpu.SemaphoreType.DMA
+    anywhere = pl.BlockSpec(memory_space=pltpu.HBM)
+    vmem = pl.BlockSpec(memory_space=VMEM)
+    extra = share is not None
+    scratch = [VMEM((2, PARTS) + two + (8, 128), F32)]
+    scratch += [VMEM((2, PARTS) + two[:5] + (8, 128), F32) for _ in range(6)]
+    scratch += [dma((2, PARTS, 6)), dma((2, PARTS, 6)), dma((PARTS,)), dma((2, PARTS)), dma((2, PARTS))]
+    if extra:
+        scratch = [VMEM((128, 1, 128), F32), dma((7,)), dma((8,))] + scratch
+    result = pl.pallas_call(
+        functools.partial(swap_all, extra),
+        out_shape=(whole, jax.ShapeDtypeStruct((1, 1), F32)) if extra else whole,
+        in_specs=[anywhere] * (1 + extra),
+        out_specs=(anywhere, vmem) if extra else anywhere,
+        scratch_shapes=scratch,
+        compiler_params=pltpu.CompilerParams(
+            collective_id=collective_id, has_side_effects=True, vmem_limit_bytes=40 * 2**20
+        ),
+    )(*((value.reshape(whole.shape), share) if extra else (value.reshape(whole.shape),)))
+    if extra:
+        return result[0].reshape(8192, 128), result[1]
+    return result.reshape(8192, 128)
 
 
 def call(body, outs, out_smem, n_smem, n_args, scratch, args):
@@ -407,55 +615,38 @@
 WORK = [square(BF16), square(BF16), square(F32), square(BF16), square(BF16)]
 
 
-def spread_call(perm, x):
+def spread_call(perm, slots, where, x):
     return call(
-        spread, (jax.ShapeDtypeStruct((128, 64, 128), F32), MAP), (1,), 1, 2,
-        [FULL] + table(14, 14, 14, 8, 64), (perm, x),
+        spread, (jax.ShapeDtypeStruct((8192, 128), F32), MAP), (1,), 3, 4,
+        [FULL] + table(14, 14, 14, 8, 64), (perm, slots, where, x),
     )
 
 
-def middle_call(perm, lanes, sup, x):
+def middle_call(perm, lanes, slots, where, sup, x):
     return call(
-        middle, (jax.ShapeDtypeStruct((8192, 128), F32), MAP), (1,), 2, 4,
-        [FULL] + WORK + table(13, 13, 13, 13, 13, 16, 64, 8, 128), (perm, lanes, sup, x),
+        middle,
+        (jax.ShapeDtypeStruct((8192, 128), F32), MAP, jax.ShapeDtypeStruct((1, 128), F32)),
+        (1,), 4, 6,
+        [FULL] + WORK + table(13, 13, 13, 13, 13, 16, 64, 8, 128, 14, 16, 64),
+        (perm, lanes, slots, where, sup, x),
     )
 
 
-def back_call(perm, lanes, where, sup, x):
+def back_call(perm, lanes, slots, where, sup, x):
     return call(
-        gather_back,
-        (jax.ShapeDtypeStruct((2, 64, 8192), F32), jax.ShapeDtypeStruct((8, 128), F32)),
-        (), 3, 5,
-        [FULL, BLOCK, BLOCK] + WORK + table(14, 13, 13, 13, 16, 64), (perm, lanes, where, sup, x),
-    )
-
-
-def add_all_call(block, devices):
-    vmem = pl.BlockSpec(memory_space=VMEM)
-    return pl.pallas_call(
-        add_all,
-        out_shape=jax.ShapeDtypeStruct((1, 1), F32),
-        in_specs=[vmem],
-        out_specs=vmem,
-        scratch_shapes=[
-            VMEM((devices, 8, 128), F32),
-            pltpu.SemaphoreType.DMA((devices,)),
-            pltpu.SemaphoreType.DMA((devices,)),
-        ],
-        compiler_params=pltpu.CompilerParams(collective_id=1, has_side_effects=True),
-    )(block)
-
-
-def exchange(value):
-    return lax.all_to_all(value, HI_GRP, split_axis=0, concat_axis=0, tiled=True)
+        gather_back, (jax.ShapeDtypeStruct((2, 64, 8192), F32),), (), 4, 6,
+        [FULL, BLOCK, BLOCK] + WORK + table(14, 13, 13, 13, 16, 64),
+        (perm, lanes, slots, where, sup, x),
+    )[0]
 
 
 def per_device(rho, perm, superop):
-    sent, lanes = spread_call(perm, rho)
-    mid, rows = middle_call(perm, lanes, superop, exchange(sent).reshape(8192, 128))
+    slots = jnp.asarray(slot_table())
     where = lax.axis_index(HI_GRP).astype(jnp.int32).reshape(1)
-    matrix, trace = back_call(perm, rows, where, superop, exchange(mid.reshape(128, 64, 128)))
-    return matrix, add_all_call(trace, lax.axis_size(HI_GRP)).reshape(())
+    sent, lanes = spread_call(perm, slots, where, rho)
+    mid, rows, share = middle_call(perm, lanes, slots, where, superop, exchange(sent, 0))
+    last, total = exchange(mid, 1, share)
+    return back_call(perm, rows, slots, where, superop, last), total.reshape(())
 
 
 def solution(mesh):

time: 223 us -> 202 us (0.906)
  Pallas kernels: 94.3 us -> 190 us
  blocking collectives: 65 us -> 0 us
  waiting for transfers between devices: 53.3 us -> 0 us
  local copies, waits for them, and re-layouts: 0 us -> 8.9 us
  starting transfers between devices: 6.59 us -> 0 us
    pallas_call x1 -> x2, Pallas kernels: 20.7 us -> 109 us  [exchange(): pl.pallas_call(functools.partial(swap_all, extra), out_shape=(whole, jax....]
    all_to_all x1 -> x0, blocking collectives: 65 us -> none  [exchange(): lax.all_to_all(value, HI_GRP, split_axis=0, concat_axis=0, tiled=True)]
    all_to_all x1 -> x0, waiting for transfers between devices: 53.3 us -> none  [exchange(): lax.all_to_all(value, HI_GRP, split_axis=0, concat_axis=0, tiled=True)]
    unnamed x0 -> x10, local copies, waits for them, and re-layouts: none -> 8.9 us
    pallas_call x3, Pallas kernels: 73.6 us -> 80.6 us  [call(): pl.pallas_call(body, out_shape=outs, in_specs=[smem if i < n_smem else vm...]
    all_to_all x1 -> x0, starting transfers between devices: 6.59 us -> none  [exchange(): lax.all_to_all(value, HI_GRP, split_axis=0, concat_axis=0, tiled=True)]
  transfers between devices with their start and end apart: 1 -> 0, of which waited for: 1 -> 0; matrix products, arithmetic and copies ran while one was open for 0% -> 0% of each run, Pallas kernels for 0% -> 0%
where the time goes in v3:
time: 202 us; the launch traced here: 201 us
  Pallas kernels  190 us (94%)
  local copies, waits for them, and re-layouts  8.9 us (4%)
  between operations  2.45 us (1%)
    pallas_call x2, Pallas kernels, exchange(): pl.pallas_call(functools.partial(swap_all, extra), out_shape=(whole, jax....  109 us
    pallas_call x3, Pallas kernels, call(): pl.pallas_call(body, out_shape=outs, in_specs=[smem if i < n_smem else vm...  80.6 us
    unnamed x10, local copies, waits for them, and re-layouts  8.9 us

profile of v3, /device:TPU:0, one launch (start us, length us, event | category | flops | bytes accessed | tf_op | source)
XLA Modules:
  0.0 201.3 jit_solution(15399851478500252826)
XLA Ops:
  0.6 11.6 %shard_map.59 = (f32[8192,128]{1,0:T(8,128)}, s32[8]{0:T(128)}) custom-call(s32[2,13]{1,0:T(2,128)} %perm.5, s32[8,128]{1,0:T(8,128)} %constant.12.clone.slots, s32[1]{0:T(128)} %bitcast.where, f32[2,64,8192]{2,1,0:T(8,128)} %x.1), custom_call_target="tpu_custom_call" | custom-call | tf_op jit(solution)/shard_map/pallas_call | solution.py:594
  12.2 0.0 copy-start.3
  12.2 2.2 %copy-done.3 = f32[8192,128]{1,0:T(8,128)S(1)} copy-done((f32[8192,128]{1,0:T(8,128)S(1)}, f32[8192,128]{1,0:T(8,128)}, u32[]{:S(2)}) %copy-start.3) | copy-done | bytes 4194328
  14.4 56.5 %shard_map.60 = f32[2,8,2,2,2,2,2,2,8,128]{9,8,7,6,5,4,3,2,1,0:T(8,128)S(1)} custom-call(f32[2,8,2,2,2,2,2,2,8,128]{9,8,7,6,5,4,3,2,1,0:T(8,128)S(1)} %bitcast.9), custom_call_target="tpu_custom_call" | custom-call | tf_op jit(solution)/shard_map/pallas_call | solution.py:576
  70.9 0.0 copy-start
  70.9 2.0 copy-done
  72.9 30.7 %shard_map.61 = (f32[8192,128]{1,0:T(8,128)}, s32[8]{0:T(128)}, f32[1,128]{1,0:T(1,128)}) custom-call(s32[2,13]{1,0:T(2,128)} %perm.5, s32[8]{0:T(128)} %get-tuple-element.9.lanes, s32[8,128]{1,0:T(8,128)} %constant.12.clone.slots, s32[1]{0:T(128)} %bitcast.where, f32[2,2,16,16]{3,2,1,0:T(8,128)} %sup.3, f32[8192,128]{1,0:T(8,128)} %bitcast.6), custom_call_target="tpu_custom_call" | custom-call | tf_op jit(solution)/shard_map/pallas_call | solution.py:594
  103.6 0.0 copy-start.1
  103.6 2.2 %copy-done.1 = f32[8192,128]{1,0:T(8,128)S(1)} copy-done((f32[8192,128]{1,0:T(8,128)S(1)}, f32[8192,128]{1,0:T(8,128)}, u32[]{:S(2)}) %copy-start.1) | copy-done | bytes 4194328
  105.8 0.0 copy-start.4
  105.8 0.6 copy-done.4
  106.4 52.9 %shard_map.62 = (f32[2,8,2,2,2,2,2,2,8,128]{9,8,7,6,5,4,3,2,1,0:T(8,128)S(1)}, f32[1,1]{1,0:T(1,128)}) custom-call(f32[2,8,2,2,2,2,2,2,8,128]{9,8,7,6,5,4,3,2,1,0:T(8,128)S(1)} %bitcast.7, f32[1,128]{1,0:T(1,128)S(1)} %copy-done.4), custom_call_target="tpu_custom_call" | custom-call | tf_op jit(solution)/shard_map/pallas_call | solution.py:576
  159.3 0.0 copy-start.2
  159.3 1.9 copy-done.2
  161.2 38.4 %shard_map.63 = f32[2,64,8192]{2,1,0:T(8,128)} custom-call(s32[2,13]{1,0:T(2,128)} %perm.5, s32[8]{0:T(128)} %get-tuple-element.11.lanes, s32[8,128]{1,0:T(8,128)} %constant.12.clone.slots, s32[1]{0:T(128)} %bitcast.where, f32[2,2,16,16]{3,2,1,0:T(8,128)} %sup.3, f32[8192,128]{1,0:T(8,128)} %bitcast.8), custom_call_target="tpu_custom_call" | custom-call | tf_op jit(solution)/shard_map/pallas_call | solution.py:594
Async XLA Ops:
  12.2 2.2 %copy-start.3 = (f32[8192,128]{1,0:T(8,128)S(1)}, f32[8192,128]{1,0:T(8,128)}, u32[]{:S(2)}) copy-start(f32[8192,128]{1,0:T(8,128)} %get-tuple-element.10) | copy-start | bytes 12582916
  70.9 2.0 %copy-start = (f32[2,8,2,2,2,2,2,2,8,128]{9,8,7,6,5,4,3,2,1,0:T(8,128)}, f32[2,8,2,2,2,2,2,2,8,128]{9,8,7,6,5,4,3,2,1,0:T(8,128)S(1)}, u32[]{:S(2)}) copy-start(f32[2,8,2,2,2,2,2,2,8,128]{9,8,7,6,5,4,3,2,1,0:T(8,128)S(1)} %shard_map.60) | copy-start | bytes 12582916
  103.6 2.2 %copy-start.1 = (f32[8192,128]{1,0:T(8,128)S(1)}, f32[8192,128]{1,0:T(8,128)}, u32[]{:S(2)}) copy-start(f32[8192,128]{1,0:T(8,128)} %get-tuple-element.12) | copy-start | bytes 12582916
  105.8 0.6 copy-start.4
  159.3 1.9 copy-start.2

commit v4 on v3

--- a/solution.py
+++ b/solution.py
@@ -41,8 +41,8 @@
         count = count + jnp.where(mine, 0, 1)
 
 
-def tile_at(vreg):
-    return pl.ds(pl.multiple_of(vreg * 8, 8), 8)
+def tile_at(row):
+    return pl.ds(pl.multiple_of(row, 8), 8)
 
 
 def insert_zero(index, bit):
@@ -50,24 +50,28 @@
     return (index - low) * 2 + low
 
 
-def swap_stage(buf, sub, bit, unroll=8):
+def swap_stage(buf, sub, bit, pairs_low, pairs_high):
     step = 1 << sub
     keep = (lax.broadcasted_iota(jnp.int32, (8, 128), 0) & step) == 0
-
-    @pl.loop(0, 512 // unroll)
+    weights = [8 * one_shl(jnp.int32(k) + jnp.where(k >= bit, 1, 0)) for k in range(9)]
+    fill(pairs_low, weights[:3])
+    fill(pairs_high, weights[3:])
+    far = 8 * one_shl(bit)
+
+    @pl.loop(0, 64)
     def _(i):
+        base = pairs_high[i]
         pairs = []
-        for k in range(unroll):
-            v = insert_zero(i * unroll + k, bit)
-            w = v + one_shl(bit)
-            pairs.append((v, w, buf[tile_at(v), :], buf[tile_at(w), :]))
+        for k in range(8):
+            v = base + pairs_low[k]
+            pairs.append((v, v + far, buf[tile_at(v), :], buf[tile_at(v + far), :]))
         for v, w, a, b in pairs:
             buf[tile_at(v), :] = jnp.where(keep, a, pltpu.roll(b, step, 0))
             buf[tile_at(w), :] = jnp.where(keep, pltpu.roll(a, 8 - step, 0), b)
 
 
-def exchange_bits(buf, loc, occ, sub, place):
-    swap_stage(buf, sub, place - 3)
+def exchange_bits(buf, loc, occ, sub, place, pairs):
+    swap_stage(buf, sub, place - 3, *pairs)
     here, there = occ[sub], occ[place]
     occ[sub] = there
     occ[place] = here
@@ -75,7 +79,7 @@
     loc[here] = place
 
 
-def settle_sublanes(buf, loc, occ, wanted, bits):
+def settle_sublanes(buf, loc, occ, wanted, bits, pairs):
     for sub in range(3):
         best = jnp.int32(-1)
         for bit in bits:
@@ -83,14 +87,14 @@
 
         @pl.when(jnp.logical_not(wanted(occ[sub])) & (best >= 3))
         def _():
-            exchange_bits(buf, loc, occ, sub, best)
+            exchange_bits(buf, loc, occ, sub, best, pairs)
 
 
 def own_slots(slots, where):
-    return [slots[part, where[0]] ^ (64 * part) for part in range(PARTS)]
-
-
-def spread(perm, slots, where, x, out, lanes, y, order, loc, occ, tc, te):
+    return [slots[where[0] * 8 + part] ^ (512 * part) for part in range(PARTS)]
+
+
+def spread(perm, slots, where, x, out, lanes, y, order, loc, occ, tc, te, *pairs):
     column_order(perm, order)
     top = order[12]
     for q in range(QUBITS):
@@ -105,10 +109,10 @@
 
     step = one_shl(top - 7)
 
-    @pl.loop(0, 16)
-    def _(pair):
-        for k in range(2):
-            m = pair * 2 + k
+    @pl.loop(0, 8)
+    def _(group):
+        for k in range(4):
+            m = group * 4 + k
             first = insert_zero(m, top - 7)
             for part in range(2):
                 halves = [
@@ -124,7 +128,7 @@
             found = found | (bit == order[i])
         return found
 
-    settle_sublanes(y, loc, occ, local, [order[i] for i in range(6)])
+    settle_sublanes(y, loc, occ, local, [order[i] for i in range(6)], pairs)
     for s in range(3):
         found = jnp.int32(0)
         for i in range(6):
@@ -134,8 +138,8 @@
     for i in range(6):
         lanes[count] = jnp.int32(i)
         count = count + jnp.where(loc[order[i]] >= 3, 1, 0)
-    fill(tc, [one_shl(loc[order[lanes[3 + i]]] - 3) for i in range(3)])
-    fill(te, [one_shl(loc[order[6 + i]] - 3) for i in range(6)])
+    fill(tc, [one_shl(loc[order[lanes[3 + i]]]) for i in range(3)])
+    fill(te, [one_shl(loc[order[6 + i]]) for i in range(6)])
     mine = own_slots(slots, where)
 
     @pl.loop(0, 16)
@@ -143,11 +147,11 @@
         for k in range(4):
             e = group * 4 + k
             base = te[e]
-            tiles = [y[tile_at(base + tc[j] + part * 512), :] for part in range(2) for j in range(8)]
+            tiles = [y[tile_at(base + tc[j] + part * 4096), :] for part in range(2) for j in range(8)]
             turned = jnp.concatenate(tiles, axis=0).T
             for j in range(16):
                 part = j % 8
-                v = slots[part, e + 64 * (j // 8)] ^ mine[part]
+                v = slots[e * 8 + 512 * (j // 8) + part] ^ mine[part]
                 out[tile_at(v), :] = turned[8 * j : 8 * j + 8]
 
 
@@ -156,7 +160,7 @@
     return high, (value - high.astype(F32)).astype(BF16)
 
 
-def build_weights(sup, layer, pair, major_is_row, lanes, high_ref, low_ref):
+def build_weights(sup, layer, pair, major_is_row, lanes, weights):
     def canonical(lane):
         if lanes is None:
             return lane & 63
@@ -188,7 +192,7 @@
     part_out = jnp.right_shift(raw_out, 6)
     sign = jnp.where(part_out >= part_in, 1.0, -1.0).astype(F32)
     parts = [split_bf16(sup[layer, part]) for part in range(2)]
-    for which, ref in enumerate((high_ref, low_ref)):
+    for which, starts in enumerate(((0, 512), (1024,))):
         half = [
             lax.dot_general(expand_in, parts[p][which], dims, preferred_element_type=F32).astype(BF16)
             for p in range(2)
@@ -199,46 +203,57 @@
                 lax.dot_general(h, target, dims, preferred_element_type=F32) for h in half
             )
             value = jnp.where(part_in == part_out, real, sign * imag)
-            ref[:, block * 128 : (block + 1) * 128] = jnp.where(same_rest, value, 0.0).astype(BF16)
-
-
-def apply_pair(z, pair, ta, rv, xh, xl, mixed, high_ref, low_ref):
-    @pl.loop(0, 4)
-    def _(other):
+            value = jnp.where(same_rest, value, 0.0).astype(BF16)
+            for begin in starts:
+                weights[begin : begin + 512, block * 128 : (block + 1) * 128] = value
+
+
+def apply_pair(z, result, pair, ta, rv, xa, xb, weights):
+    def bases_of(other):
         first = other * 4 if pair == 0 else other
-        stride = 1 if pair == 0 else 4
-        bases = [ta[first + stride * k] for k in range(4)]
-
-        @pl.loop(0, 16)
-        def _(r):
+        return [ta[first + (1 if pair == 0 else 4) * k] for k in range(4)]
+
+    def split_rows(bases, xs, r, start):
+        vregs = [rv[r], rv[r + 1]]
+        for k in range(4):
+            both = [z[tile_at(bases[k] + v), :] for v in vregs]
+            high, low = split_bf16(jnp.concatenate(both, axis=0))
+            rows = pl.ds(start, 16)
+            xs[rows, k * 128 : (k + 1) * 128] = high
+            xs[rows, 512 + k * 128 : 512 + (k + 1) * 128] = low
+            xs[rows, 1024 + k * 128 : 1024 + (k + 1) * 128] = high
+
+    first = bases_of(0)
+
+    @pl.loop(0, 8)
+    def _(i):
+        for k in range(4):
+            split_rows(first, xa, i * 8 + k * 2, pl.multiple_of(i * 64 + k * 16, 16))
+
+    @pl.loop(0, 2)
+    def _(i):
+        for k, (xs, spare) in enumerate(((xa, xb), (xb, xa))):
+            other = 2 * i + k
+            following = bases_of(lax.rem(other + 1, 4))
+            bases = bases_of(other)
+            for r in range(0, 64, 2):
+                split_rows(following, spare, r, 8 * r)
             for half in range(2):
-                v0 = rv[r * 4 + half * 2]
-                v1 = rv[r * 4 + half * 2 + 1]
-                rows = pl.ds(pl.multiple_of(r * 32 + half * 16, 16), 16)
-                for k in range(4):
-                    both = [z[tile_at(bases[k] + v), :] for v in (v0, v1)]
-                    high, low = split_bf16(jnp.concatenate(both, axis=0))
-                    xh[rows, k * 128 : (k + 1) * 128] = high
-                    xl[rows, k * 128 : (k + 1) * 128] = low
-
-        total = jnp.dot(xh[...], high_ref[...], preferred_element_type=F32)
-        total += jnp.dot(xl[...], high_ref[...], preferred_element_type=F32)
-        total += jnp.dot(xh[...], low_ref[...], preferred_element_type=F32)
-        mixed[...] = total
-
-        @pl.loop(0, 16)
-        def _(r):
-            for j in range(4):
-                v = rv[r * 4 + j]
-                rows = pl.ds(pl.multiple_of(r * 32 + j * 8, 8), 8)
-                for k in range(4):
-                    z[tile_at(bases[k] + v), :] = mixed[rows, k * 128 : (k + 1) * 128]
-
-
-def channel(sup, layer, major_is_row, lanes, z, ta, rv, xh, xl, mixed, high_ref, low_ref):
-    for pair in range(2):
-        build_weights(sup, layer, pair, major_is_row, lanes if pair == 0 else None, high_ref, low_ref)
-        apply_pair(z, pair, ta, rv, xh, xl, mixed, high_ref, low_ref)
+                mixed = jnp.dot(
+                    xs[...], weights[:, half * 256 : (half + 1) * 256], preferred_element_type=F32
+                )
+                for r in range(64):
+                    v = rv[r]
+                    for q in range(2):
+                        result[tile_at(bases[2 * half + q] + v), :] = mixed[
+                            8 * r : 8 * r + 8, q * 128 : (q + 1) * 128
+                        ]
+
+
+def channel(sup, layer, major_is_row, lanes, z, spare, ta, rv, xa, xb, weights):
+    for pair, (source, result) in enumerate(((z, spare), (spare, z))):
+        build_weights(sup, layer, pair, major_is_row, lanes if pair == 0 else None, weights)
+        apply_pair(source, result, pair, ta, rv, xa, xb, weights)
 
 
 def trace_share(perm, where, sup, z, loc, outpos, final, order, tu, tc):
@@ -302,8 +317,8 @@
     return sums
 
 
-def middle(perm, lanes, slots, where, sup, x, out, rows_out, share, z, xh, xl, mixed, high, low,
-           final, outpos, loc, occ, rest, ta, rv, ti, td, order, tu, tc):
+def middle(perm, lanes, slots, where, sup, x, out, rows_out, share, z, spare, xa, xb, weights,
+           final, outpos, loc, occ, rest, ta, rv, ti, td, order, tu, tc, *pairs):
     for q in range(QUBITS):
         bit = perm[0, perm[1, q]]
         final[q] = bit
@@ -317,7 +332,7 @@
         for k in range(2):
             d = i * 2 + k
             for part in range(PARTS):
-                z[tile_at(d * 8 + part), :] = x[tile_at(slots[part, d] ^ mine[part]), :]
+                z[tile_at(d * 64 + part * 8), :] = x[tile_at(slots[d * 8 + part] ^ mine[part]), :]
 
     mixes = [perm[0, j] for j in range(4)]
 
@@ -329,25 +344,25 @@
 
     everything = [jnp.int32(q) for q in range(QUBITS)]
     stays = lambda bit: outpos[bit] < 6
-    settle_sublanes(z, loc, occ, lambda bit: jnp.logical_not(mixed_bit(bit)) & stays(bit), everything)
-    settle_sublanes(z, loc, occ, lambda bit: jnp.logical_not(mixed_bit(bit)), everything)
+    settle_sublanes(z, loc, occ, lambda bit: jnp.logical_not(mixed_bit(bit)) & stays(bit), everything, pairs)
+    settle_sublanes(z, loc, occ, lambda bit: jnp.logical_not(mixed_bit(bit)), everything, pairs)
     count = jnp.int32(0)
     for place in range(3, QUBITS):
         rest[count] = jnp.int32(place)
         count = count + jnp.where(mixed_bit(occ[place]), 0, 1)
-    fill(ta, [one_shl(loc[m] - 3) for m in mixes])
-    fill(rv, [one_shl(rest[j] - 3) for j in range(6)])
-    channel(sup, 0, True, lanes, z, ta, rv, xh, xl, mixed, high, low)
+    fill(ta, [one_shl(loc[m]) for m in mixes])
+    fill(rv, [one_shl(rest[j]) for j in range(6)])
+    channel(sup, 0, True, lanes, z, spare, ta, rv, xa, xb, weights)
     share[...] = trace_share(perm, where, sup, z, loc, outpos, final, order, tu, tc)
-    settle_sublanes(z, loc, occ, stays, everything)
+    settle_sublanes(z, loc, occ, stays, everything, pairs)
     for s in range(3):
         rows_out[s] = outpos[occ[s]]
     count = jnp.int32(3)
     for q in range(6):
         rows_out[count] = jnp.int32(q)
         count = count + jnp.where(loc[final[q]] >= 3, 1, 0)
-    fill(ti, [one_shl(loc[final[rows_out[3 + i]]] - 3) for i in range(3)])
-    fill(td, [one_shl(loc[final[6 + i]] - 3) for i in range(7)])
+    fill(ti, [one_shl(loc[final[rows_out[3 + i]]]) for i in range(3)])
+    fill(td, [one_shl(loc[final[6 + i]]) for i in range(7)])
 
     @pl.loop(0, 64)
     def _(i):
@@ -355,11 +370,11 @@
             d = i * 2 + k
             base = td[d]
             for j in range(8):
-                out[tile_at(slots[j, d] ^ mine[j]), :] = z[tile_at(base + ti[j]), :]
-
-
-def gather_back(perm, lanes, slots, where, sup, x, out, y, b0, b1, xh, xl, mixed, high, low,
-                order, inv, loc, occ, ta, rv):
+                out[tile_at(slots[d * 8 + j] ^ mine[j]), :] = z[tile_at(base + ti[j]), :]
+
+
+def gather_back(perm, lanes, slots, where, sup, x, out, y, spare, xa, xb, weights,
+                order, inv, loc, occ, ta, rv, *pairs):
     column_order(perm, order)
     for i in range(QUBITS):
         inv[order[i]] = jnp.int32(i)
@@ -369,12 +384,12 @@
         occ[place] = jnp.int32(q)
     mine = own_slots(slots, where)
 
-    @pl.loop(0, 32)
-    def _(pair):
-        for k in range(2):
-            p = pair * 2 + k
+    @pl.loop(0, 16)
+    def _(group):
+        for q in range(4):
+            p = group * 4 + q
             tiles = [
-                x[tile_at(slots[j, p + 64 * k] ^ mine[j]), :] for k in range(2) for j in range(PARTS)
+                x[tile_at(slots[p * 8 + 512 * k + j] ^ mine[j]), :] for k in range(2) for j in range(PARTS)
             ]
             turned = jnp.concatenate(tiles, axis=0).T
             real, imag = turned[:64], turned[64:]
@@ -387,25 +402,35 @@
 
             @pl.when(loc[4 + sub] == other)
             def _():
-                exchange_bits(y, loc, occ, other, jnp.int32(12))
+                exchange_bits(y, loc, occ, other, jnp.int32(12), pairs)
 
         @pl.when(loc[4 + sub] >= 3)
         def _():
-            exchange_bits(y, loc, occ, sub, loc[4 + sub])
-
-    fill(ta, [one_shl(loc[q] - 3) for q in range(4)])
-    fill(rv, [one_shl(loc[q] - 3) for q in range(7, QUBITS)])
-    channel(sup, 1, False, lanes, y, ta, rv, xh, xl, mixed, high, low)
-
-    @pl.loop(0, 32)
-    def _(pair):
-        for k, b in enumerate((b0, b1)):
-            base = rv[pair * 2 + k]
-            for low_bits in range(16):
-                b[pl.ds(low_bits, 8, stride=16), :] = y[tile_at(base + ta[low_bits]), :]
-        for k, b in enumerate((b0, b1)):
-            columns = pl.ds(pl.multiple_of((pair * 2 + k) * 128, 128), 128)
-            turned = b[...].T
+            exchange_bits(y, loc, occ, sub, loc[4 + sub], pairs)
+
+    fill(ta, [one_shl(loc[q]) for q in range(4)])
+    fill(rv, [one_shl(loc[q]) for q in range(7, QUBITS)])
+    channel(sup, 1, False, lanes, y, spare, ta, rv, xa, xb, weights)
+
+    sublane = lax.broadcasted_iota(jnp.int32, (8, 128), 0)
+
+    @pl.loop(0, 16)
+    def _(group):
+        for q in range(4):
+            t = group * 4 + q
+            base = rv[t]
+            tiles = [y[tile_at(base + ta[b]), :] for b in range(16)]
+            for k in range(3):
+                step = 1 << k
+                keep = (sublane & step) == 0
+                for b in range(16):
+                    if not b & step:
+                        lower, upper = tiles[b], tiles[b + step]
+                        tiles[b] = jnp.where(keep, lower, pltpu.roll(upper, step, 0))
+                        tiles[b + step] = jnp.where(keep, pltpu.roll(lower, 8 - step, 0), upper)
+            ordered = [tiles[8 * (v % 2) + v // 2] for v in range(16)]
+            columns = pl.ds(pl.multiple_of(t * 128, 128), 128)
+            turned = jnp.concatenate(ordered, axis=0).T
             out[0, :, columns] = turned[:64]
             out[1, :, columns] = turned[64:]
 
@@ -433,7 +458,7 @@
                 if device >> bit & 1:
                     table[part, device] ^= weight[bit]
         table[part] += 64 * part
-    return table
+    return 8 * table.T.reshape(-1)
 
 
 def swap_all(with_sum, *refs):
@@ -580,7 +605,7 @@
         out_specs=(anywhere, vmem) if extra else anywhere,
         scratch_shapes=scratch,
         compiler_params=pltpu.CompilerParams(
-            collective_id=collective_id, has_side_effects=True, vmem_limit_bytes=40 * 2**20
+            collective_id=collective_id, has_side_effects=True, vmem_limit_bytes=60 * 2**20
         ),
     )(*((value.reshape(whole.shape), share) if extra else (value.reshape(whole.shape),)))
     if extra:
@@ -605,20 +630,15 @@
     return [SMEM((n,), jnp.int32) for n in sizes]
 
 
-def square(dtype):
-    return VMEM((512, 512), dtype)
-
-
 FULL = VMEM((8192, 128), F32)
-BLOCK = VMEM((128, 128), F32)
 MAP = jax.ShapeDtypeStruct((8,), jnp.int32)
-WORK = [square(BF16), square(BF16), square(F32), square(BF16), square(BF16)]
+WORK = [FULL, VMEM((512, 1536), BF16), VMEM((512, 1536), BF16), VMEM((1536, 512), BF16)]
 
 
 def spread_call(perm, slots, where, x):
     return call(
         spread, (jax.ShapeDtypeStruct((8192, 128), F32), MAP), (1,), 3, 4,
-        [FULL] + table(14, 14, 14, 8, 64), (perm, slots, where, x),
+        [FULL] + table(14, 14, 14, 8, 64, 8, 64), (perm, slots, where, x),
     )
 
 
@@ -627,7 +647,7 @@
         middle,
         (jax.ShapeDtypeStruct((8192, 128), F32), MAP, jax.ShapeDtypeStruct((1, 128), F32)),
         (1,), 4, 6,
-        [FULL] + WORK + table(13, 13, 13, 13, 13, 16, 64, 8, 128, 14, 16, 64),
+        [FULL] + WORK + table(13, 13, 13, 13, 13, 16, 64, 8, 128, 14, 16, 64, 8, 64),
         (perm, lanes, slots, where, sup, x),
     )
 
@@ -635,7 +655,7 @@
 def back_call(perm, lanes, slots, where, sup, x):
     return call(
         gather_back, (jax.ShapeDtypeStruct((2, 64, 8192), F32),), (), 4, 6,
-        [FULL, BLOCK, BLOCK] + WORK + table(14, 13, 13, 13, 16, 64),
+        [FULL] + WORK + table(14, 13, 13, 13, 16, 64, 8, 64),
         (perm, lanes, slots, where, sup, x),
     )[0]
 

time: 202 us -> 181 us (0.90)
  Pallas kernels: 190 us -> 179 us
  local copies, waits for them, and re-layouts: 8.9 us -> 0 us
    pallas_call x3, Pallas kernels: 80.6 us -> 65.5 us  [call(): pl.pallas_call(body, out_shape=outs, in_specs=[smem if i < n_smem else vm...]
    unnamed x10 -> x0, local copies, waits for them, and re-layouts: 8.9 us -> none
    pallas_call x2, Pallas kernels: 109 us -> 113 us  [exchange(): pl.pallas_call(functools.partial(swap_all, extra), out_shape=(whole, jax....]
where the time goes in v4:
time: 181 us
  Pallas kernels  179 us (99%)
  between operations  2.48 us (1%)
    pallas_call x2, Pallas kernels, exchange(): pl.pallas_call(functools.partial(swap_all, extra), out_shape=(whole, jax....  113 us
    pallas_call x3, Pallas kernels, call(): pl.pallas_call(body, out_shape=outs, in_specs=[smem if i < n_smem else vm...  65.5 us

profile of v4, /device:TPU:0, one launch (start us, length us, event | category | flops | bytes accessed | tf_op | source)
XLA Modules:
  0.0 181.0 jit_solution(13301362331937691924)
XLA Ops:
  0.6 10.1 %shard_map.59 = (f32[8192,128]{1,0:T(8,128)}, s32[8]{0:T(128)}) custom-call(s32[2,13]{1,0:T(2,128)} %perm.5, s32[1024]{0:T(1024)} %constant.12.clone.slots, s32[1]{0:T(128)} %bitcast.where, f32[2,64,8192]{2,1,0:T(8,128)} %x.1), custom_call_target="tpu_custom_call" | custom-call | tf_op jit(solution)/shard_map/pallas_call | solution.py:619
  10.7 58.4 %shard_map.60 = f32[2,8,2,2,2,2,2,2,8,128]{9,8,7,6,5,4,3,2,1,0:T(8,128)} custom-call(f32[2,8,2,2,2,2,2,2,8,128]{9,8,7,6,5,4,3,2,1,0:T(8,128)} %bitcast.9), custom_call_target="tpu_custom_call" | custom-call | tf_op jit(solution)/shard_map/pallas_call | solution.py:601
  69.1 28.0 %shard_map.61 = (f32[8192,128]{1,0:T(8,128)}, s32[8]{0:T(128)}, f32[1,128]{1,0:T(1,128)}) custom-call(s32[2,13]{1,0:T(2,128)} %perm.5, s32[8]{0:T(128)} %get-tuple-element.9.lanes, s32[1024]{0:T(1024)} %constant.12.clone.slots, s32[1]{0:T(128)} %bitcast.where, f32[2,2,16,16]{3,2,1,0:T(8,128)} %sup.3, f32[8192,128]{1,0:T(8,128)} %bitcast.6), custom_call_target="tpu_custom_call" | custom-call | tf_op jit(solution)/shard_map/pallas_call | solution.py:619
  97.1 54.6 %shard_map.62 = (f32[2,8,2,2,2,2,2,2,8,128]{9,8,7,6,5,4,3,2,1,0:T(8,128)}, f32[1,1]{1,0:T(1,128)}) custom-call(f32[2,8,2,2,2,2,2,2,8,128]{9,8,7,6,5,4,3,2,1,0:T(8,128)} %bitcast.7, f32[1,128]{1,0:T(1,128)} %get-tuple-element.13.refs_1_), custom_call_target="tpu_custom_call" | custom-call | tf_op jit(solution)/shard_map/pallas_call | solution.py:601
  151.7 27.5 %shard_map.63 = f32[2,64,8192]{2,1,0:T(8,128)} custom-call(s32[2,13]{1,0:T(2,128)} %perm.5, s32[8]{0:T(128)} %get-tuple-element.11.lanes, s32[1024]{0:T(1024)} %constant.12.clone.slots, s32[1]{0:T(128)} %bitcast.where, f32[2,2,16,16]{3,2,1,0:T(8,128)} %sup.3, f32[8192,128]{1,0:T(8,128)} %bitcast.8), custom_call_target="tpu_custom_call" | custom-call | tf_op jit(solution)/shard_map/pallas_call | solution.py:619

commit v5 on v4

--- a/solution.py
+++ b/solution.py
@@ -50,51 +50,102 @@
     return (index - low) * 2 + low
 
 
-def swap_stage(buf, sub, bit, pairs_low, pairs_high):
+def swap_rows(lower, upper, sub, keep_lower, keep_upper):
     step = 1 << sub
-    keep = (lax.broadcasted_iota(jnp.int32, (8, 128), 0) & step) == 0
-    weights = [8 * one_shl(jnp.int32(k) + jnp.where(k >= bit, 1, 0)) for k in range(9)]
-    fill(pairs_low, weights[:3])
-    fill(pairs_high, weights[3:])
-    far = 8 * one_shl(bit)
-
-    @pl.loop(0, 64)
-    def _(i):
-        base = pairs_high[i]
-        pairs = []
-        for k in range(8):
-            v = base + pairs_low[k]
-            pairs.append((v, v + far, buf[tile_at(v), :], buf[tile_at(v + far), :]))
-        for v, w, a, b in pairs:
-            buf[tile_at(v), :] = jnp.where(keep, a, pltpu.roll(b, step, 0))
-            buf[tile_at(w), :] = jnp.where(keep, pltpu.roll(a, 8 - step, 0), b)
-
-
-def exchange_bits(buf, loc, occ, sub, place, pairs):
-    swap_stage(buf, sub, place - 3, *pairs)
-    here, there = occ[sub], occ[place]
-    occ[sub] = there
-    occ[place] = here
-    loc[there] = jnp.int32(sub)
-    loc[here] = place
-
-
-def settle_sublanes(buf, loc, occ, wanted, bits, pairs):
+    return (
+        jnp.where(keep_lower, lower, pltpu.roll(upper, step, 0)),
+        jnp.where(keep_upper, upper, pltpu.roll(lower, 8 - step, 0)),
+    )
+
+
+def swap_lanes(lower, upper, bit):
+    lane = lax.broadcasted_iota(jnp.int32, (8, 128), 1)
+    keep = (jnp.right_shift(lane, bit) & 1) == 0
+    shift = one_shl(bit) if not isinstance(bit, int) else 1 << bit
+    return (
+        jnp.where(keep, lower, pltpu.roll(upper, shift, 1)),
+        jnp.where(keep, pltpu.roll(lower, 128 - shift, 1), upper),
+    )
+
+
+def swap_lane_pairs(tiles, bits):
+    t = list(tiles)
+    for k, bit in enumerate(bits):
+        step = 1 << k
+        for i in range(4):
+            if not i & step:
+                t[i], t[i + step] = swap_lanes(t[i], t[i + step], bit)
+    return t
+
+
+def plan_sublanes(loc, occ, wanted, bits, places, enabled):
     for sub in range(3):
         best = jnp.int32(-1)
         for bit in bits:
             best = jnp.where(wanted(bit) & (loc[bit] >= 3), loc[bit], best)
-
-        @pl.when(jnp.logical_not(wanted(occ[sub])) & (best >= 3))
+        needed = jnp.logical_not(wanted(occ[sub])) & (best >= 3)
+        enabled[sub] = jnp.where(needed, 1, 0)
+        places[sub] = best
+
+        @pl.when(needed)
         def _():
-            exchange_bits(buf, loc, occ, sub, best, pairs)
-
-
-def own_slots(slots, where):
-    return [slots[where[0] * 8 + part] ^ (512 * part) for part in range(PARTS)]
-
-
-def spread(perm, slots, where, x, out, lanes, y, order, loc, occ, tc, te, *pairs):
+            here, there = occ[sub], occ[best]
+            occ[sub] = there
+            occ[best] = here
+            loc[there] = jnp.int32(sub)
+            loc[here] = best
+
+
+def regroup(load, dst, places, enabled, others, group_low, group_high, origin=None):
+    for sub in range(3):
+        free = jnp.int32(3)
+        for _ in range(5):
+            taken = jnp.bool_(False)
+            for k in range(3):
+                if k != sub:
+                    taken = taken | ((places[k] == free) & ((enabled[k] == 1) | (k < sub)))
+            free = free + jnp.where(taken, 1, 0)
+        places[sub] = jnp.where(enabled[sub] == 1, places[sub], free)
+    count = jnp.int32(0)
+    for place in range(3, QUBITS):
+        others[count] = jnp.int32(place)
+        mine = (places[0] == place) | (places[1] == place) | (places[2] == place)
+        count = count + jnp.where(mine, 0, 1)
+    fill(group_low, [one_shl(others[k]) for k in range(3)])
+    fill(group_high, [one_shl(others[3 + k]) for k in range(4)])
+    steps = [one_shl(places[k]) for k in range(3)]
+    sublane = lax.broadcasted_iota(jnp.int32, (8, 128), 0)
+    masks = []
+    for k in range(3):
+        bit = jnp.right_shift(sublane, k) & 1
+        off = enabled[k] == 0
+        masks.append(((bit == 0) | off, (bit == 1) | off))
+    if origin is not None:
+        index = jnp.zeros((8, 128), jnp.int32)
+        for k in range(3):
+            index = index + jnp.left_shift(jnp.right_shift(sublane, k) & 1, origin[k])
+
+    @pl.loop(0, 16)
+    def _(i):
+        high = group_high[i]
+        for j in range(8):
+            base = high + group_low[j]
+            rows = [base]
+            for k in range(3):
+                rows = rows + [r + steps[k] for r in rows]
+            tiles = [load(r) for r in rows]
+            if origin is not None:
+                tiles = [jnp.take_along_axis(t, index, axis=0) for t in tiles]
+            for k in range(3):
+                for v in range(8):
+                    if not v >> k & 1:
+                        w = v + (1 << k)
+                        tiles[v], tiles[w] = swap_rows(tiles[v], tiles[w], k, *masks[k])
+            for r, t in zip(rows, tiles):
+                dst[tile_at(r), :] = t
+
+
+def spread(perm, slots, where, x, out, lanes, y, order, loc, occ, tc, te, places, enabled, *spare):
     column_order(perm, order)
     top = order[12]
     for q in range(QUBITS):
@@ -128,7 +179,12 @@
             found = found | (bit == order[i])
         return found
 
-    settle_sublanes(y, loc, occ, local, [order[i] for i in range(6)], pairs)
+    plan_sublanes(loc, occ, local, [order[i] for i in range(6)], places, enabled)
+
+    @pl.when(enabled[0] + enabled[1] + enabled[2] > 0)
+    def _():
+        regroup(lambda row: y[tile_at(row), :], y, places, enabled, *spare)
+
     for s in range(3):
         found = jnp.int32(0)
         for i in range(6):
@@ -140,7 +196,7 @@
         count = count + jnp.where(loc[order[i]] >= 3, 1, 0)
     fill(tc, [one_shl(loc[order[lanes[3 + i]]]) for i in range(3)])
     fill(te, [one_shl(loc[order[6 + i]]) for i in range(6)])
-    mine = own_slots(slots, where)
+    me = where[0]
 
     @pl.loop(0, 16)
     def _(group):
@@ -149,10 +205,10 @@
             base = te[e]
             tiles = [y[tile_at(base + tc[j] + part * 4096), :] for part in range(2) for j in range(8)]
             turned = jnp.concatenate(tiles, axis=0).T
+            apart = (e ^ me) * 8
+            starts = (apart, apart ^ 512)
             for j in range(16):
-                part = j % 8
-                v = slots[e * 8 + 512 * (j // 8) + part] ^ mine[part]
-                out[tile_at(v), :] = turned[8 * j : 8 * j + 8]
+                out[tile_at(slots[starts[j // 8] + j % 8]), :] = turned[8 * j : 8 * j + 8]
 
 
 def split_bf16(value):
@@ -160,103 +216,111 @@
     return high, (value - high.astype(F32)).astype(BF16)
 
 
-def build_weights(sup, layer, pair, major_is_row, lanes, weights):
+def build_weights(sup, layer, major_is_row, lanes, weights):
     def canonical(lane):
-        if lanes is None:
-            return lane & 63
         total = jnp.zeros_like(lane)
         for k in range(6):
             total = total + jnp.left_shift(jnp.right_shift(lane, k) & 1, lanes[k])
         return total
 
-    def uv(major, lane):
-        minor = jnp.right_shift(lane, 2 * pair) & 3
-        return 4 * major + minor if major_is_row else 4 * minor + major
-
     row = lax.broadcasted_iota(jnp.int32, (512, 16), 0)
     col16 = lax.broadcasted_iota(jnp.int32, (512, 16), 1)
 
-    def one_hot(lane):
-        hit = uv(jnp.right_shift(row, 7), lane) == col16
-        return jnp.where(hit, 1.0, 0.0).astype(BF16)
-
-    expand_out = one_hot(row & 63)
-    expand_in = expand_out if lanes is None else one_hot(canonical(row))
+    def one_hot(pair, lane):
+        inner = jnp.right_shift(lane, 2 * pair) & 3
+        other = jnp.right_shift(row, 7) if pair else jnp.right_shift(lane, 4) & 3
+        uv = 4 * other + inner if major_is_row else 4 * inner + other
+        return jnp.where(uv == col16, 1.0, 0.0).astype(BF16)
+
     dims = (((1,), (1,)), ((), ()))
-    raw_in = lax.broadcasted_iota(jnp.int32, (512, 128), 0) & 127
-    lane_in = canonical(raw_in)
-    raw_out = lax.broadcasted_iota(jnp.int32, (512, 128), 1)
-    keep = 63 & ~(3 << (2 * pair))
-    same_rest = (lane_in & keep) == (raw_out & keep)
-    part_in = jnp.right_shift(raw_in, 6)
-    part_out = jnp.right_shift(raw_out, 6)
-    sign = jnp.where(part_out >= part_in, 1.0, -1.0).astype(F32)
     parts = [split_bf16(sup[layer, part]) for part in range(2)]
-    for which, starts in enumerate(((0, 512), (1024,))):
-        half = [
-            lax.dot_general(expand_in, parts[p][which], dims, preferred_element_type=F32).astype(BF16)
-            for p in range(2)
-        ]
-        for block in range(4):
-            target = expand_out[block * 128 : (block + 1) * 128]
-            real, imag = (
-                lax.dot_general(h, target, dims, preferred_element_type=F32) for h in half
-            )
-            value = jnp.where(part_in == part_out, real, sign * imag)
-            value = jnp.where(same_rest, value, 0.0).astype(BF16)
-            for begin in starts:
-                weights[begin : begin + 512, block * 128 : (block + 1) * 128] = value
-
-
-def apply_pair(z, result, pair, ta, rv, xa, xb, weights):
-    def bases_of(other):
-        first = other * 4 if pair == 0 else other
-        return [ta[first + (1 if pair == 0 else 4) * k] for k in range(4)]
-
-    def split_rows(bases, xs, r, start):
-        vregs = [rv[r], rv[r + 1]]
+    lane_in = canonical(row)
+    source = []
+    target = []
+    for pair in range(2):
+        expand = one_hot(pair, lane_in)
+        source.append(
+            [
+                jnp.concatenate(
+                    [
+                        lax.dot_general(expand, p, dims, preferred_element_type=F32).astype(BF16)
+                        for p in parts[part]
+                    ],
+                    axis=1,
+                )
+                for part in range(2)
+            ]
+        )
+        expand = one_hot(pair, row & 63)
+        target.append(jnp.concatenate([expand, expand], axis=1))
+    part_in = jnp.right_shift(lax.broadcasted_iota(jnp.int32, (512, 128), 0) & 127, 6)
+    part_out = jnp.right_shift(lax.broadcasted_iota(jnp.int32, (512, 128), 1), 6)
+    for block in range(4):
+        columns = slice(block * 128, (block + 1) * 128)
+        (r0, i0), (r1, i1) = (
+            [
+                lax.dot_general(source[pair][part], target[pair][columns], dims, preferred_element_type=F32)
+                for part in range(2)
+            ]
+            for pair in range(2)
+        )
+        imag = r0 * i1 + i0 * r1
+        value = jnp.where(
+            part_in == part_out, r0 * r1 - i0 * i1, jnp.where(part_out > part_in, imag, -imag)
+        )
+        high, low = split_bf16(value)
+        weights[0:512, columns] = high
+        weights[512:1024, columns] = high
+        weights[1024:1536, columns] = low
+
+
+def channel(z, result, major, rest, lane_bits, xa, xb, weights):
+    bases = [major[k] for k in range(4)]
+
+    def split_rows(xs, r, start):
+        vregs = [rest[r + q] for q in range(4)]
         for k in range(4):
-            both = [z[tile_at(bases[k] + v), :] for v in vregs]
-            high, low = split_bf16(jnp.concatenate(both, axis=0))
-            rows = pl.ds(start, 16)
-            xs[rows, k * 128 : (k + 1) * 128] = high
-            xs[rows, 512 + k * 128 : 512 + (k + 1) * 128] = low
-            xs[rows, 1024 + k * 128 : 1024 + (k + 1) * 128] = high
-
-    first = bases_of(0)
+            tiles = swap_lane_pairs([z[tile_at(bases[k] + v), :] for v in vregs], lane_bits)
+            for half in range(2):
+                both = jnp.concatenate(tiles[2 * half : 2 * half + 2], axis=0)
+                high, low = split_bf16(both)
+                rows = pl.ds(start + 16 * half, 16)
+                xs[rows, k * 128 : (k + 1) * 128] = high
+                xs[rows, 512 + k * 128 : 512 + (k + 1) * 128] = low
+                xs[rows, 1024 + k * 128 : 1024 + (k + 1) * 128] = high
 
     @pl.loop(0, 8)
     def _(i):
-        for k in range(4):
-            split_rows(first, xa, i * 8 + k * 2, pl.multiple_of(i * 64 + k * 16, 16))
+        for k in range(2):
+            split_rows(xa, i * 8 + k * 4, pl.multiple_of(i * 64 + k * 32, 16))
 
     @pl.loop(0, 2)
     def _(i):
         for k, (xs, spare) in enumerate(((xa, xb), (xb, xa))):
-            other = 2 * i + k
-            following = bases_of(lax.rem(other + 1, 4))
-            bases = bases_of(other)
-            for r in range(0, 64, 2):
-                split_rows(following, spare, r, 8 * r)
+            block = 2 * i + k
+            following = lax.rem(block + 1, 4)
+            for r in range(0, 64, 4):
+                split_rows(spare, following * 64 + r, 8 * r)
             for half in range(2):
                 mixed = jnp.dot(
                     xs[...], weights[:, half * 256 : (half + 1) * 256], preferred_element_type=F32
                 )
                 for r in range(64):
-                    v = rv[r]
+                    v = rest[block * 64 + r]
                     for q in range(2):
                         result[tile_at(bases[2 * half + q] + v), :] = mixed[
                             8 * r : 8 * r + 8, q * 128 : (q + 1) * 128
                         ]
 
 
-def channel(sup, layer, major_is_row, lanes, z, spare, ta, rv, xa, xb, weights):
-    for pair, (source, result) in enumerate(((z, spare), (spare, z))):
-        build_weights(sup, layer, pair, major_is_row, lanes if pair == 0 else None, weights)
-        apply_pair(source, result, pair, ta, rv, xa, xb, weights)
-
-
-def trace_share(perm, where, sup, z, loc, outpos, final, order, tu, tc):
+def find_lane(lanes, which):
+    found = jnp.int32(0)
+    for k in range(6):
+        found = jnp.where(lanes[k] == which, k, found)
+    return found
+
+
+def trace_share(perm, slots, where, sup, out, row_weight, outpos, final, order, tu, tc):
     column_order(perm, order)
     me = where[0]
 
@@ -293,10 +357,10 @@
     exact = functools.partial(jnp.dot, precision=lax.Precision.HIGHEST, preferred_element_type=F32)
     weight = jnp.where(lane < 64, exact(real, hot), -exact(imag, hot))
 
-    fill(tu, [one_shl(loc[final[j]]) for j in range(4)])
+    fill(tu, [row_weight(final[j]) for j in range(4)])
 
     def weight_of(bit):
-        return jnp.where(outpos[bit] >= 4, one_shl(loc[bit]), 0)
+        return jnp.where(outpos[bit] >= 4, row_weight(bit), 0)
 
     fill(tc, [weight_of(order[i]) for i in range(6)])
     base = jnp.int32(0)
@@ -307,9 +371,12 @@
 
     def column(c, rows):
         start = base + tc[c]
-        return tuple(
-            jnp.where(lane1 == c, z[pl.ds(start + tu[u], 1), :], rows[u]) for u in range(16)
-        )
+        found = []
+        for u in range(16):
+            index = start + tu[u]
+            row = slots[jnp.right_shift(index, 3) ^ (me * 8)] + (index & 7)
+            found.append(jnp.where(lane1 == c, out[pl.ds(row, 1), :], rows[u]))
+        return tuple(found)
 
     rows = lax.fori_loop(0, 64, column, tuple(sums for _ in range(16)))
     for u in range(16):
@@ -318,22 +385,15 @@
 
 
 def middle(perm, lanes, slots, where, sup, x, out, rows_out, share, z, spare, xa, xb, weights,
-           final, outpos, loc, occ, rest, ta, rv, ti, td, order, tu, tc, *pairs):
+           final, outpos, loc, occ, rest, major, rv, order, tu, tc, out_of, low_from, low_to,
+           high_from, high_to, places, enabled, *groups):
+    me = where[0]
     for q in range(QUBITS):
         bit = perm[0, perm[1, q]]
         final[q] = bit
         outpos[bit] = jnp.int32(q)
         loc[q] = jnp.int32(q)
         occ[q] = jnp.int32(q)
-    mine = own_slots(slots, where)
-
-    @pl.loop(0, 64)
-    def _(i):
-        for k in range(2):
-            d = i * 2 + k
-            for part in range(PARTS):
-                z[tile_at(d * 64 + part * 8), :] = x[tile_at(slots[d * 8 + part] ^ mine[part]), :]
-
     mixes = [perm[0, j] for j in range(4)]
 
     def mixed_bit(bit):
@@ -344,37 +404,74 @@
 
     everything = [jnp.int32(q) for q in range(QUBITS)]
     stays = lambda bit: outpos[bit] < 6
-    settle_sublanes(z, loc, occ, lambda bit: jnp.logical_not(mixed_bit(bit)) & stays(bit), everything, pairs)
-    settle_sublanes(z, loc, occ, lambda bit: jnp.logical_not(mixed_bit(bit)), everything, pairs)
+    best = lambda bit: jnp.logical_not(mixed_bit(bit)) & stays(bit)
+    calm = lambda bit: jnp.logical_not(mixed_bit(bit))
+    plenty = jnp.int32(0)
+    for bit in everything:
+        plenty = plenty + jnp.where(best(bit), 1, 0)
+    good = lambda bit: jnp.where(plenty >= 3, best(bit), calm(bit))
+    plan_sublanes(loc, occ, good, everything, places, enabled)
+    mine = me * 8
+    regroup(
+        lambda row: x[tile_at(slots[jnp.right_shift(row, 3) ^ mine]), :], z, places, enabled, *groups
+    )
     count = jnp.int32(0)
     for place in range(3, QUBITS):
         rest[count] = jnp.int32(place)
         count = count + jnp.where(mixed_bit(occ[place]), 0, 1)
-    fill(ta, [one_shl(loc[m]) for m in mixes])
-    fill(rv, [one_shl(rest[j]) for j in range(6)])
-    channel(sup, 0, True, lanes, z, spare, ta, rv, xa, xb, weights)
-    share[...] = trace_share(perm, where, sup, z, loc, outpos, final, order, tu, tc)
-    settle_sublanes(z, loc, occ, stays, everything, pairs)
+    fill(major, [one_shl(loc[m]) for m in mixes[2:]])
+    fill(rv, [one_shl(loc[m]) for m in mixes[:2]] + [one_shl(rest[j]) for j in range(6)])
+    build_weights(sup, 0, True, lanes, weights)
+    channel(z, spare, major, rv, [find_lane(lanes, 4), find_lane(lanes, 5)], xa, xb, weights)
+    fixed = lambda bit: stays(bit) & (bit != mixes[0]) & (bit != mixes[1])
+    plan_sublanes(loc, occ, fixed, everything, places, enabled)
+
+    @pl.when(enabled[0] + enabled[1] + enabled[2] > 0)
+    def _():
+        regroup(lambda row: spare[tile_at(row), :], spare, places, enabled, *groups)
+
     for s in range(3):
         rows_out[s] = outpos[occ[s]]
     count = jnp.int32(3)
     for q in range(6):
         rows_out[count] = jnp.int32(q)
         count = count + jnp.where(loc[final[q]] >= 3, 1, 0)
-    fill(ti, [one_shl(loc[final[rows_out[3 + i]]]) for i in range(3)])
-    fill(td, [one_shl(loc[final[6 + i]]) for i in range(7)])
-
-    @pl.loop(0, 64)
+    for q in range(6, QUBITS):
+        out_of[final[q]] = jnp.int32(8 << (q - 6))
+    for s in range(3):
+        out_of[occ[s]] = jnp.int32(0)
+        out_of[final[rows_out[3 + s]]] = jnp.int32(1 << s)
+    count = jnp.int32(0)
+    for place in range(3, QUBITS):
+        rest[count] = jnp.int32(place)
+        skip = (loc[mixes[0]] == place) | (loc[mixes[1]] == place)
+        count = count + jnp.where(skip, 0, 1)
+    fill(low_from, [one_shl(rest[j]) for j in range(3)])
+    fill(high_from, [one_shl(rest[3 + j]) for j in range(5)])
+    fill(low_to, [out_of[occ[rest[j]]] for j in range(3)])
+    fill(high_to, [out_of[occ[rest[3 + j]]] for j in range(5)])
+    from_steps = [one_shl(loc[m]) for m in mixes[:2]]
+    to_steps = [out_of[m] for m in mixes[:2]]
+    from_quad = [0, from_steps[0], from_steps[1], from_steps[0] + from_steps[1]]
+    to_quad = [0, to_steps[0], to_steps[1], to_steps[0] + to_steps[1]]
+
+    @pl.loop(0, 32)
     def _(i):
-        for k in range(2):
-            d = i * 2 + k
-            base = td[d]
-            for j in range(8):
-                out[tile_at(slots[d * 8 + j] ^ mine[j]), :] = z[tile_at(base + ti[j]), :]
+        origin, target = high_from[i], high_to[i]
+        for j in range(8):
+            start, end = origin + low_from[j], target + low_to[j]
+            tiles = swap_lane_pairs([spare[tile_at(start + f), :] for f in from_quad], (4, 5))
+            for t, tile in zip(to_quad, tiles):
+                out[tile_at(slots[(end + t) ^ mine]), :] = tile
+
+    def row_weight(bit):
+        return jnp.where(loc[bit] < 3, one_shl(jnp.minimum(loc[bit], 3)), 8 * out_of[bit])
+
+    share[...] = trace_share(perm, slots, where, sup, out, row_weight, outpos, final, order, tu, tc)
 
 
 def gather_back(perm, lanes, slots, where, sup, x, out, y, spare, xa, xb, weights,
-                order, inv, loc, occ, ta, rv, *pairs):
+                order, inv, loc, occ, ta, rv, major, rest, origin, places, enabled, *groups):
     column_order(perm, order)
     for i in range(QUBITS):
         inv[order[i]] = jnp.int32(i)
@@ -382,14 +479,15 @@
         place = inv[perm[0, perm[1, q]]]
         loc[q] = place
         occ[place] = jnp.int32(q)
-    mine = own_slots(slots, where)
+    me = where[0]
 
     @pl.loop(0, 16)
     def _(group):
         for q in range(4):
             p = group * 4 + q
+            apart = (p ^ me) * 8
             tiles = [
-                x[tile_at(slots[p * 8 + 512 * k + j] ^ mine[j]), :] for k in range(2) for j in range(PARTS)
+                x[tile_at(slots[start + j]), :] for start in (apart, apart ^ 512) for j in range(PARTS)
             ]
             turned = jnp.concatenate(tiles, axis=0).T
             real, imag = turned[:64], turned[64:]
@@ -398,19 +496,34 @@
             y[pl.ds(start + 4096, 64), :] = jnp.concatenate([real[:, 64:], imag[:, 64:]], axis=1)
 
     for sub in range(3):
-        for other in range(sub + 1, 3):
-
-            @pl.when(loc[4 + sub] == other)
-            def _():
-                exchange_bits(y, loc, occ, other, jnp.int32(12), pairs)
-
-        @pl.when(loc[4 + sub] >= 3)
+        inside = loc[4 + sub] < 3
+        enabled[sub] = jnp.where(inside, 0, 1)
+        places[sub] = loc[4 + sub]
+    for sub in range(3):
+        free = jnp.int32(0)
+        for _ in range(3):
+            taken = jnp.bool_(False)
+            for k in range(3):
+                taken = taken | ((enabled[k] == 0) & (places[k] == free))
+                if k < sub:
+                    taken = taken | ((enabled[k] == 1) & (origin[k] == free))
+            free = free + jnp.where(taken, 1, 0)
+        origin[sub] = jnp.where(enabled[sub] == 1, free, places[sub])
+    leaving = [occ[origin[sub]] for sub in range(3)]
+    for sub in range(3):
+
+        @pl.when(enabled[sub] == 1)
         def _():
-            exchange_bits(y, loc, occ, sub, loc[4 + sub], pairs)
-
+            loc[leaving[sub]] = places[sub]
+
+        loc[4 + sub] = jnp.int32(sub)
+    regroup(lambda row: y[tile_at(row), :], y, places, enabled, *groups, origin=origin)
     fill(ta, [one_shl(loc[q]) for q in range(4)])
     fill(rv, [one_shl(loc[q]) for q in range(7, QUBITS)])
-    channel(sup, 1, False, lanes, y, spare, ta, rv, xa, xb, weights)
+    fill(major, [one_shl(loc[q]) for q in range(2, 4)])
+    fill(rest, [one_shl(loc[q]) for q in (0, 1, 7, 8, 9, 10, 11, 12)])
+    build_weights(sup, 1, False, lanes, weights)
+    channel(y, spare, major, rest, [find_lane(lanes, 4), find_lane(lanes, 5)], xa, xb, weights)
 
     sublane = lax.broadcasted_iota(jnp.int32, (8, 128), 0)
 
@@ -419,15 +532,17 @@
         for q in range(4):
             t = group * 4 + q
             base = rv[t]
-            tiles = [y[tile_at(base + ta[b]), :] for b in range(16)]
+            tiles = [spare[tile_at(base + ta[b]), :] for b in range(16)]
+            for b in range(0, 16, 4):
+                tiles[b : b + 4] = swap_lane_pairs(tiles[b : b + 4], (4, 5))
             for k in range(3):
                 step = 1 << k
                 keep = (sublane & step) == 0
                 for b in range(16):
                     if not b & step:
-                        lower, upper = tiles[b], tiles[b + step]
-                        tiles[b] = jnp.where(keep, lower, pltpu.roll(upper, step, 0))
-                        tiles[b + step] = jnp.where(keep, pltpu.roll(lower, 8 - step, 0), upper)
+                        tiles[b], tiles[b + step] = swap_rows(
+                            tiles[b], tiles[b + step], k, keep, jnp.logical_not(keep)
+                        )
             ordered = [tiles[8 * (v % 2) + v // 2] for v in range(16)]
             columns = pl.ds(pl.multiple_of(t * 128, 128), 128)
             turned = jnp.concatenate(ordered, axis=0).T
@@ -605,7 +720,7 @@
         out_specs=(anywhere, vmem) if extra else anywhere,
         scratch_shapes=scratch,
         compiler_params=pltpu.CompilerParams(
-            collective_id=collective_id, has_side_effects=True, vmem_limit_bytes=60 * 2**20
+            collective_id=collective_id, has_side_effects=True, vmem_limit_bytes=24 * 2**20
         ),
     )(*((value.reshape(whole.shape), share) if extra else (value.reshape(whole.shape),)))
     if extra:
@@ -622,7 +737,7 @@
         in_specs=[smem if i < n_smem else vmem for i in range(n_args)],
         out_specs=tuple(smem if i in out_smem else vmem for i in range(len(outs))),
         scratch_shapes=scratch,
-        compiler_params=pltpu.CompilerParams(vmem_limit_bytes=60 * 2**20),
+        compiler_params=pltpu.CompilerParams(vmem_limit_bytes=26 * 2**20),
     )(*args)
 
 
@@ -631,6 +746,7 @@
 
 
 FULL = VMEM((8192, 128), F32)
+GROUPS = (3, 3, 14, 8, 16)
 MAP = jax.ShapeDtypeStruct((8,), jnp.int32)
 WORK = [FULL, VMEM((512, 1536), BF16), VMEM((512, 1536), BF16), VMEM((1536, 512), BF16)]
 
@@ -638,7 +754,7 @@
 def spread_call(perm, slots, where, x):
     return call(
         spread, (jax.ShapeDtypeStruct((8192, 128), F32), MAP), (1,), 3, 4,
-        [FULL] + table(14, 14, 14, 8, 64, 8, 64), (perm, slots, where, x),
+        [FULL] + table(14, 14, 14, 8, 64, *GROUPS), (perm, slots, where, x),
     )
 
 
@@ -647,7 +763,7 @@
         middle,
         (jax.ShapeDtypeStruct((8192, 128), F32), MAP, jax.ShapeDtypeStruct((1, 128), F32)),
         (1,), 4, 6,
-        [FULL] + WORK + table(13, 13, 13, 13, 13, 16, 64, 8, 128, 14, 16, 64, 8, 64),
+        [FULL] + WORK + table(13, 13, 13, 13, 14, 4, 256, 14, 16, 64, 13, 8, 8, 32, 32, *GROUPS),
         (perm, lanes, slots, where, sup, x),
     )
 
@@ -655,7 +771,7 @@
 def back_call(perm, lanes, slots, where, sup, x):
     return call(
         gather_back, (jax.ShapeDtypeStruct((2, 64, 8192), F32),), (), 4, 6,
-        [FULL] + WORK + table(14, 13, 13, 13, 16, 64, 8, 64),
+        [FULL] + WORK + table(14, 13, 13, 13, 16, 64, 4, 256, 3, *GROUPS),
         (perm, lanes, slots, where, sup, x),
     )[0]
 

time: 181 us -> 179 us (0.989)
  Pallas kernels: 179 us -> 172 us
  local copies, waits for them, and re-layouts: 0 us -> 3.55 us
    unnamed x0 -> x8, local copies, waits for them, and re-layouts: none -> 3.55 us
    pallas_call x3, Pallas kernels: 65.5 us -> 62.1 us  [call(): pl.pallas_call(body, out_shape=outs, in_specs=[smem if i < n_smem else vm...]
    pallas_call x2, Pallas kernels: 113 us -> 110 us  [exchange(): pl.pallas_call(functools.partial(swap_all, extra), out_shape=(whole, jax....]
where the time goes in v5:
time: 179 us; the launch traced here: 178 us
  Pallas kernels  172 us (96%)
  local copies, waits for them, and re-layouts  3.55 us (2%)
  between operations  2.51 us (1%)
    pallas_call x2, Pallas kernels, exchange(): pl.pallas_call(functools.partial(swap_all, extra), out_shape=(whole, jax....  110 us
    pallas_call x3, Pallas kernels, call(): pl.pallas_call(body, out_shape=outs, in_specs=[smem if i < n_smem else vm...  62.1 us

profile of v5, /device:TPU:0, one launch (start us, length us, event | category | flops | bytes accessed | tf_op | source)
XLA Modules:
  0.0 177.9 jit_solution(6935378889112738240)
XLA Ops:
  0.6 0.0 copy-start
  0.6 2.2 %copy-done = f32[2,64,8192]{2,1,0:T(8,128)S(1)} copy-done((f32[2,64,8192]{2,1,0:T(8,128)S(1)}, f32[2,64,8192]{2,1,0:T(8,128)}, u32[]{:S(2)}) %copy-start) | copy-done | bytes 4194328
  2.8 0.0 copy-start.2
  2.8 0.7 copy-done.2
  3.5 0.0 copy-start.3
  3.5 0.7 copy-done.3
  4.2 5.3 %shard_map.59 = (f32[8192,128]{1,0:T(8,128)S(1)}, s32[8]{0:T(128)S(1)}) custom-call(s32[2,13]{1,0:T(2,128)S(1)} %copy-done.3, s32[1024]{0:T(1024)S(1)} %copy-done.2, s32[1]{0:T(128)} %bitcast.where, f32[2,64,8192]{2,1,0:T(8,128)S(1)} %copy-done), custom_call_target="tpu_custom_call" | custom-call | tf_op jit(solution)/shard_map/pallas_call | solution.py:734
  9.5 0.0 copy-start.1
  9.5 56.6 %shard_map.60 = f32[2,8,2,2,2,2,2,2,8,128]{9,8,7,6,5,4,3,2,1,0:T(8,128)S(1)} custom-call(f32[2,8,2,2,2,2,2,2,8,128]{9,8,7,6,5,4,3,2,1,0:T(8,128)S(1)} %bitcast.9), custom_call_target="tpu_custom_call" | custom-call | tf_op jit(solution)/shard_map/pallas_call | solution.py:716
  66.2 0.0 copy-done.1
  66.2 27.0 %shard_map.61 = (f32[8192,128]{1,0:T(8,128)S(1)}, s32[8]{0:T(128)S(1)}, f32[1,128]{1,0:T(1,128)S(1)}) custom-call(s32[2,13]{1,0:T(2,128)S(1)} %copy-done.3, s32[8]{0:T(128)S(1)} %get-tuple-element.9.lanes, s32[1024]{0:T(1024)S(1)} %copy-done.2, s32[1]{0:T(128)} %bitcast.where, f32[2,2,16,16]{3,2,1,0:T(8,128)S(1)} %copy-done.1, f32[8192,128]{1,0:T(8,128)S(1)} %bitcast.6), custom_call_target="tpu_custom_call" | custom-call | tf_op jit(solution)/shard_map/pallas_call | solution.py:734
  93.2 53.1 %shard_map.62 = (f32[2,8,2,2,2,2,2,2,8,128]{9,8,7,6,5,4,3,2,1,0:T(8,128)S(1)}, f32[1,1]{1,0:T(1,128)}) custom-call(f32[2,8,2,2,2,2,2,2,8,128]{9,8,7,6,5,4,3,2,1,0:T(8,128)S(1)} %bitcast.7, f32[1,128]{1,0:T(1,128)S(1)} %get-tuple-element.13.refs_1_), custom_call_target="tpu_custom_call" | custom-call | tf_op jit(solution)/shard_map/pallas_call | solution.py:716
  146.3 29.8 %shard_map.63 = f32[2,64,8192]{2,1,0:T(8,128)} custom-call(s32[2,13]{1,0:T(2,128)S(1)} %copy-done.3, s32[8]{0:T(128)S(1)} %get-tuple-element.11.lanes, s32[1024]{0:T(1024)S(1)} %copy-done.2, s32[1]{0:T(128)} %bitcast.where, f32[2,2,16,16]{3,2,1,0:T(8,128)S(1)} %copy-done.1, f32[8192,128]{1,0:T(8,128)S(1)} %bitcast.8), custom_call_target="tpu_custom_call" | custom-call | tf_op jit(solution)/shard_map/pallas_call | solution.py:734
Async XLA Ops:
  0.6 2.2 %copy-start = (f32[2,64,8192]{2,1,0:T(8,128)S(1)}, f32[2,64,8192]{2,1,0:T(8,128)}, u32[]{:S(2)}) copy-start(f32[2,64,8192]{2,1,0:T(8,128)} %x.1) | copy-start | bytes 12582916
  2.8 0.7 copy-start.2
  3.5 0.7 copy-start.3
  9.5 56.7 %copy-start.1 = (f32[2,2,16,16]{3,2,1,0:T(8,128)S(1)}, f32[2,2,16,16]{3,2,1,0:T(8,128)}, u32[]{:S(2)}) copy-start(f32[2,2,16,16]{3,2,1,0:T(8,128)} %sup.3) | copy-start | bytes 12292

commit v6 on v5

--- a/solution.py
+++ b/solution.py
@@ -56,26 +56,6 @@
         jnp.where(keep_lower, lower, pltpu.roll(upper, step, 0)),
         jnp.where(keep_upper, upper, pltpu.roll(lower, 8 - step, 0)),
     )
-
-
-def swap_lanes(lower, upper, bit):
-    lane = lax.broadcasted_iota(jnp.int32, (8, 128), 1)
-    keep = (jnp.right_shift(lane, bit) & 1) == 0
-    shift = one_shl(bit) if not isinstance(bit, int) else 1 << bit
-    return (
-        jnp.where(keep, lower, pltpu.roll(upper, shift, 1)),
-        jnp.where(keep, pltpu.roll(lower, 128 - shift, 1), upper),
-    )
-
-
-def swap_lane_pairs(tiles, bits):
-    t = list(tiles)
-    for k, bit in enumerate(bits):
-        step = 1 << k
-        for i in range(4):
-            if not i & step:
-                t[i], t[i + step] = swap_lanes(t[i], t[i + step], bit)
-    return t
 
 
 def plan_sublanes(loc, occ, wanted, bits, places, enabled):
@@ -145,7 +125,7 @@
                 dst[tile_at(r), :] = t
 
 
-def spread(perm, slots, where, x, out, lanes, y, order, loc, occ, tc, te, places, enabled, *spare):
+def spread(perm, slots, where, x, out, lanes, y, z, order, loc, occ, tc, te, places, enabled, *groups):
     column_order(perm, order)
     top = order[12]
     for q in range(QUBITS):
@@ -181,9 +161,7 @@
 
     plan_sublanes(loc, occ, local, [order[i] for i in range(6)], places, enabled)
 
-    @pl.when(enabled[0] + enabled[1] + enabled[2] > 0)
-    def _():
-        regroup(lambda row: y[tile_at(row), :], y, places, enabled, *spare)
+    regroup(lambda row: y[tile_at(row), :], z, places, enabled, *groups)
 
     for s in range(3):
         found = jnp.int32(0)
@@ -203,7 +181,7 @@
         for k in range(4):
             e = group * 4 + k
             base = te[e]
-            tiles = [y[tile_at(base + tc[j] + part * 4096), :] for part in range(2) for j in range(8)]
+            tiles = [z[tile_at(base + tc[j] + part * 4096), :] for part in range(2) for j in range(8)]
             turned = jnp.concatenate(tiles, axis=0).T
             apart = (e ^ me) * 8
             starts = (apart, apart ^ 512)
@@ -216,108 +194,100 @@
     return high, (value - high.astype(F32)).astype(BF16)
 
 
-def build_weights(sup, layer, major_is_row, lanes, weights):
+def build_weights(sup, layer, pair, major_is_row, lanes, weights):
     def canonical(lane):
+        if lanes is None:
+            return lane & 63
         total = jnp.zeros_like(lane)
         for k in range(6):
             total = total + jnp.left_shift(jnp.right_shift(lane, k) & 1, lanes[k])
         return total
 
+    def uv(major, lane):
+        minor = jnp.right_shift(lane, 2 * pair) & 3
+        return 4 * major + minor if major_is_row else 4 * minor + major
+
     row = lax.broadcasted_iota(jnp.int32, (512, 16), 0)
     col16 = lax.broadcasted_iota(jnp.int32, (512, 16), 1)
 
-    def one_hot(pair, lane):
-        inner = jnp.right_shift(lane, 2 * pair) & 3
-        other = jnp.right_shift(row, 7) if pair else jnp.right_shift(lane, 4) & 3
-        uv = 4 * other + inner if major_is_row else 4 * inner + other
-        return jnp.where(uv == col16, 1.0, 0.0).astype(BF16)
-
+    def one_hot(lane):
+        hit = uv(jnp.right_shift(row, 7), lane) == col16
+        return jnp.where(hit, 1.0, 0.0).astype(BF16)
+
+    expand_out = one_hot(row & 63)
+    expand_in = expand_out if lanes is None else one_hot(canonical(row))
     dims = (((1,), (1,)), ((), ()))
+    raw_in = lax.broadcasted_iota(jnp.int32, (512, 128), 0) & 127
+    lane_in = canonical(raw_in)
+    raw_out = lax.broadcasted_iota(jnp.int32, (512, 128), 1)
+    keep = 63 & ~(3 << (2 * pair))
+    same_rest = (lane_in & keep) == (raw_out & keep)
+    part_in = jnp.right_shift(raw_in, 6)
+    part_out = jnp.right_shift(raw_out, 6)
+    sign = jnp.where(part_out >= part_in, 1.0, -1.0).astype(F32)
     parts = [split_bf16(sup[layer, part]) for part in range(2)]
-    lane_in = canonical(row)
-    source = []
-    target = []
-    for pair in range(2):
-        expand = one_hot(pair, lane_in)
-        source.append(
-            [
-                jnp.concatenate(
-                    [
-                        lax.dot_general(expand, p, dims, preferred_element_type=F32).astype(BF16)
-                        for p in parts[part]
-                    ],
-                    axis=1,
-                )
-                for part in range(2)
-            ]
-        )
-        expand = one_hot(pair, row & 63)
-        target.append(jnp.concatenate([expand, expand], axis=1))
-    part_in = jnp.right_shift(lax.broadcasted_iota(jnp.int32, (512, 128), 0) & 127, 6)
-    part_out = jnp.right_shift(lax.broadcasted_iota(jnp.int32, (512, 128), 1), 6)
-    for block in range(4):
-        columns = slice(block * 128, (block + 1) * 128)
-        (r0, i0), (r1, i1) = (
-            [
-                lax.dot_general(source[pair][part], target[pair][columns], dims, preferred_element_type=F32)
-                for part in range(2)
-            ]
-            for pair in range(2)
-        )
-        imag = r0 * i1 + i0 * r1
-        value = jnp.where(
-            part_in == part_out, r0 * r1 - i0 * i1, jnp.where(part_out > part_in, imag, -imag)
-        )
-        high, low = split_bf16(value)
-        weights[0:512, columns] = high
-        weights[512:1024, columns] = high
-        weights[1024:1536, columns] = low
-
-
-def channel(z, result, major, rest, lane_bits, xa, xb, weights):
-    bases = [major[k] for k in range(4)]
-
-    def split_rows(xs, r, start):
-        vregs = [rest[r + q] for q in range(4)]
+    for which, starts in enumerate(((0, 512), (1024,))):
+        half = [
+            lax.dot_general(expand_in, parts[p][which], dims, preferred_element_type=F32).astype(BF16)
+            for p in range(2)
+        ]
+        for block in range(4):
+            target = expand_out[block * 128 : (block + 1) * 128]
+            real, imag = (
+                lax.dot_general(h, target, dims, preferred_element_type=F32) for h in half
+            )
+            value = jnp.where(part_in == part_out, real, sign * imag)
+            value = jnp.where(same_rest, value, 0.0).astype(BF16)
+            for begin in starts:
+                weights[begin : begin + 512, block * 128 : (block + 1) * 128] = value
+
+
+def apply_pair(z, result, pair, ta, rv, xa, xb, weights):
+    def bases_of(other):
+        first = other * 4 if pair == 0 else other
+        return [ta[first + (1 if pair == 0 else 4) * k] for k in range(4)]
+
+    def split_rows(bases, xs, r, start):
+        vregs = [rv[r], rv[r + 1]]
         for k in range(4):
-            tiles = swap_lane_pairs([z[tile_at(bases[k] + v), :] for v in vregs], lane_bits)
-            for half in range(2):
-                both = jnp.concatenate(tiles[2 * half : 2 * half + 2], axis=0)
-                high, low = split_bf16(both)
-                rows = pl.ds(start + 16 * half, 16)
-                xs[rows, k * 128 : (k + 1) * 128] = high
-                xs[rows, 512 + k * 128 : 512 + (k + 1) * 128] = low
-                xs[rows, 1024 + k * 128 : 1024 + (k + 1) * 128] = high
+            both = [z[tile_at(bases[k] + v), :] for v in vregs]
+            high, low = split_bf16(jnp.concatenate(both, axis=0))
+            rows = pl.ds(start, 16)
+            xs[rows, k * 128 : (k + 1) * 128] = high
+            xs[rows, 512 + k * 128 : 512 + (k + 1) * 128] = low
+            xs[rows, 1024 + k * 128 : 1024 + (k + 1) * 128] = high
+
+    first = bases_of(0)
 
     @pl.loop(0, 8)
     def _(i):
-        for k in range(2):
-            split_rows(xa, i * 8 + k * 4, pl.multiple_of(i * 64 + k * 32, 16))
+        for k in range(4):
+            split_rows(first, xa, i * 8 + k * 2, pl.multiple_of(i * 64 + k * 16, 16))
 
     @pl.loop(0, 2)
     def _(i):
         for k, (xs, spare) in enumerate(((xa, xb), (xb, xa))):
-            block = 2 * i + k
-            following = lax.rem(block + 1, 4)
-            for r in range(0, 64, 4):
-                split_rows(spare, following * 64 + r, 8 * r)
+            other = 2 * i + k
+            following = bases_of(lax.rem(other + 1, 4))
+            bases = bases_of(other)
+            for r in range(0, 64, 2):
+                split_rows(following, spare, r, 8 * r)
             for half in range(2):
                 mixed = jnp.dot(
                     xs[...], weights[:, half * 256 : (half + 1) * 256], preferred_element_type=F32
                 )
                 for r in range(64):
-                    v = rest[block * 64 + r]
+                    v = rv[r]
                     for q in range(2):
                         result[tile_at(bases[2 * half + q] + v), :] = mixed[
                             8 * r : 8 * r + 8, q * 128 : (q + 1) * 128
                         ]
 
 
-def find_lane(lanes, which):
-    found = jnp.int32(0)
-    for k in range(6):
-        found = jnp.where(lanes[k] == which, k, found)
-    return found
+def channel(sup, layer, major_is_row, lanes, z, spare, ta, rv, xa, xb, weights):
+    for pair, (source, result) in enumerate(((z, spare), (spare, z))):
+        build_weights(sup, layer, pair, major_is_row, lanes if pair == 0 else None, weights)
+        apply_pair(source, result, pair, ta, rv, xa, xb, weights)
 
 
 def trace_share(perm, slots, where, sup, out, row_weight, outpos, final, order, tu, tc):
@@ -419,16 +389,14 @@
     for place in range(3, QUBITS):
         rest[count] = jnp.int32(place)
         count = count + jnp.where(mixed_bit(occ[place]), 0, 1)
-    fill(major, [one_shl(loc[m]) for m in mixes[2:]])
-    fill(rv, [one_shl(loc[m]) for m in mixes[:2]] + [one_shl(rest[j]) for j in range(6)])
-    build_weights(sup, 0, True, lanes, weights)
-    channel(z, spare, major, rv, [find_lane(lanes, 4), find_lane(lanes, 5)], xa, xb, weights)
-    fixed = lambda bit: stays(bit) & (bit != mixes[0]) & (bit != mixes[1])
-    plan_sublanes(loc, occ, fixed, everything, places, enabled)
+    fill(major, [one_shl(loc[m]) for m in mixes])
+    fill(rv, [one_shl(rest[j]) for j in range(6)])
+    channel(sup, 0, True, lanes, z, spare, major, rv, xa, xb, weights)
+    plan_sublanes(loc, occ, stays, everything, places, enabled)
 
     @pl.when(enabled[0] + enabled[1] + enabled[2] > 0)
     def _():
-        regroup(lambda row: spare[tile_at(row), :], spare, places, enabled, *groups)
+        regroup(lambda row: z[tile_at(row), :], z, places, enabled, *groups)
 
     for s in range(3):
         rows_out[s] = outpos[occ[s]]
@@ -441,28 +409,16 @@
     for s in range(3):
         out_of[occ[s]] = jnp.int32(0)
         out_of[final[rows_out[3 + s]]] = jnp.int32(1 << s)
-    count = jnp.int32(0)
-    for place in range(3, QUBITS):
-        rest[count] = jnp.int32(place)
-        skip = (loc[mixes[0]] == place) | (loc[mixes[1]] == place)
-        count = count + jnp.where(skip, 0, 1)
-    fill(low_from, [one_shl(rest[j]) for j in range(3)])
-    fill(high_from, [one_shl(rest[3 + j]) for j in range(5)])
-    fill(low_to, [out_of[occ[rest[j]]] for j in range(3)])
-    fill(high_to, [out_of[occ[rest[3 + j]]] for j in range(5)])
-    from_steps = [one_shl(loc[m]) for m in mixes[:2]]
-    to_steps = [out_of[m] for m in mixes[:2]]
-    from_quad = [0, from_steps[0], from_steps[1], from_steps[0] + from_steps[1]]
-    to_quad = [0, to_steps[0], to_steps[1], to_steps[0] + to_steps[1]]
+    fill(low_from, [one_shl(3 + j) for j in range(5)])
+    fill(high_from, [one_shl(8 + j) for j in range(5)])
+    fill(low_to, [out_of[occ[3 + j]] for j in range(5)])
+    fill(high_to, [out_of[occ[8 + j]] for j in range(5)])
 
     @pl.loop(0, 32)
     def _(i):
         origin, target = high_from[i], high_to[i]
-        for j in range(8):
-            start, end = origin + low_from[j], target + low_to[j]
-            tiles = swap_lane_pairs([spare[tile_at(start + f), :] for f in from_quad], (4, 5))
-            for t, tile in zip(to_quad, tiles):
-                out[tile_at(slots[(end + t) ^ mine]), :] = tile
+        for j in range(32):
+            out[tile_at(slots[(target + low_to[j]) ^ mine]), :] = z[tile_at(origin + 8 * j), :]
 
     def row_weight(bit):
         return jnp.where(loc[bit] < 3, one_shl(jnp.minimum(loc[bit], 3)), 8 * out_of[bit])
@@ -471,7 +427,7 @@
 
 
 def gather_back(perm, lanes, slots, where, sup, x, out, y, spare, xa, xb, weights,
-                order, inv, loc, occ, ta, rv, major, rest, origin, places, enabled, *groups):
+                order, inv, loc, occ, ta, rv, origin, places, enabled, *groups):
     column_order(perm, order)
     for i in range(QUBITS):
         inv[order[i]] = jnp.int32(i)
@@ -480,6 +436,7 @@
         loc[q] = place
         occ[place] = jnp.int32(q)
     me = where[0]
+    first_half = lax.broadcasted_iota(jnp.int32, (64, 128), 1) < 64
 
     @pl.loop(0, 16)
     def _(group):
@@ -492,8 +449,9 @@
             turned = jnp.concatenate(tiles, axis=0).T
             real, imag = turned[:64], turned[64:]
             start = pl.multiple_of(p * 64, 64)
-            y[pl.ds(start, 64), :] = jnp.concatenate([real[:, :64], imag[:, :64]], axis=1)
-            y[pl.ds(start + 4096, 64), :] = jnp.concatenate([real[:, 64:], imag[:, 64:]], axis=1)
+            moved = pltpu.roll(jnp.where(first_half, imag, real), 64, 1)
+            y[pl.ds(start, 64), :] = jnp.where(first_half, real, moved)
+            y[pl.ds(start + 4096, 64), :] = jnp.where(first_half, moved, imag)
 
     for sub in range(3):
         inside = loc[4 + sub] < 3
@@ -517,13 +475,10 @@
             loc[leaving[sub]] = places[sub]
 
         loc[4 + sub] = jnp.int32(sub)
-    regroup(lambda row: y[tile_at(row), :], y, places, enabled, *groups, origin=origin)
+    regroup(lambda row: y[tile_at(row), :], spare, places, enabled, *groups, origin=origin)
     fill(ta, [one_shl(loc[q]) for q in range(4)])
     fill(rv, [one_shl(loc[q]) for q in range(7, QUBITS)])
-    fill(major, [one_shl(loc[q]) for q in range(2, 4)])
-    fill(rest, [one_shl(loc[q]) for q in (0, 1, 7, 8, 9, 10, 11, 12)])
-    build_weights(sup, 1, False, lanes, weights)
-    channel(y, spare, major, rest, [find_lane(lanes, 4), find_lane(lanes, 5)], xa, xb, weights)
+    channel(sup, 1, False, lanes, spare, y, ta, rv, xa, xb, weights)
 
     sublane = lax.broadcasted_iota(jnp.int32, (8, 128), 0)
 
@@ -533,8 +488,6 @@
             t = group * 4 + q
             base = rv[t]
             tiles = [spare[tile_at(base + ta[b]), :] for b in range(16)]
-            for b in range(0, 16, 4):
-                tiles[b : b + 4] = swap_lane_pairs(tiles[b : b + 4], (4, 5))
             for k in range(3):
                 step = 1 << k
                 keep = (sublane & step) == 0
@@ -754,7 +707,7 @@
 def spread_call(perm, slots, where, x):
     return call(
         spread, (jax.ShapeDtypeStruct((8192, 128), F32), MAP), (1,), 3, 4,
-        [FULL] + table(14, 14, 14, 8, 64, *GROUPS), (perm, slots, where, x),
+        [FULL, FULL] + table(14, 14, 14, 8, 64, *GROUPS), (perm, slots, where, x),
     )
 
 
@@ -763,7 +716,7 @@
         middle,
         (jax.ShapeDtypeStruct((8192, 128), F32), MAP, jax.ShapeDtypeStruct((1, 128), F32)),
         (1,), 4, 6,
-        [FULL] + WORK + table(13, 13, 13, 13, 14, 4, 256, 14, 16, 64, 13, 8, 8, 32, 32, *GROUPS),
+        [FULL] + WORK + table(13, 13, 13, 13, 14, 16, 64, 14, 16, 64, 13, 32, 32, 32, 32, *GROUPS),
         (perm, lanes, slots, where, sup, x),
     )
 
@@ -771,7 +724,7 @@
 def back_call(perm, lanes, slots, where, sup, x):
     return call(
         gather_back, (jax.ShapeDtypeStruct((2, 64, 8192), F32),), (), 4, 6,
-        [FULL] + WORK + table(14, 13, 13, 13, 16, 64, 4, 256, 3, *GROUPS),
+        [FULL] + WORK + table(14, 13, 13, 13, 16, 64, 3, *GROUPS),
         (perm, lanes, slots, where, sup, x),
     )[0]
 

time: 179 us -> 168 us (0.939)
  Pallas kernels: 172 us -> 162 us
    pallas_call x3, Pallas kernels: 62.1 us -> 52.1 us  [call(): pl.pallas_call(body, out_shape=outs, in_specs=[smem if i < n_smem else vm...]
where the time goes in v6:
time: 168 us
  Pallas kernels  162 us (96%)
  local copies, waits for them, and re-layouts  3.55 us (2%)
  between operations  2.51 us (1%)
    pallas_call x2, Pallas kernels, exchange(): pl.pallas_call(functools.partial(swap_all, extra), out_shape=(whole, jax....  110 us
    pallas_call x3, Pallas kernels, call(): pl.pallas_call(body, out_shape=outs, in_specs=[smem if i < n_smem else vm...  52.1 us
    unnamed x8, local copies, waits for them, and re-layouts  3.55 us

profile of v6, /device:TPU:0, one launch (start us, length us, event | category | flops | bytes accessed | tf_op | source)
XLA Modules:
  0.0 167.9 jit_solution(10024966384497183738)
XLA Ops:
  0.6 0.0 copy-start
  0.6 2.2 %copy-done = f32[2,64,8192]{2,1,0:T(8,128)S(1)} copy-done((f32[2,64,8192]{2,1,0:T(8,128)S(1)}, f32[2,64,8192]{2,1,0:T(8,128)}, u32[]{:S(2)}) %copy-start) | copy-done | bytes 4194328
  2.8 0.0 copy-start.2
  2.8 0.7 copy-done.2
  3.5 0.0 copy-start.3
  3.5 0.7 copy-done.3
  4.2 6.7 %shard_map.59 = (f32[8192,128]{1,0:T(8,128)S(1)}, s32[8]{0:T(128)S(1)}) custom-call(s32[2,13]{1,0:T(2,128)S(1)} %copy-done.3, s32[1024]{0:T(1024)S(1)} %copy-done.2, s32[1]{0:T(128)} %bitcast.where, f32[2,64,8192]{2,1,0:T(8,128)S(1)} %copy-done), custom_call_target="tpu_custom_call" | custom-call | tf_op jit(solution)/shard_map/pallas_call | solution.py:687
  10.9 0.0 copy-start.1
  10.9 56.6 %shard_map.60 = f32[2,8,2,2,2,2,2,2,8,128]{9,8,7,6,5,4,3,2,1,0:T(8,128)S(1)} custom-call(f32[2,8,2,2,2,2,2,2,8,128]{9,8,7,6,5,4,3,2,1,0:T(8,128)S(1)} %bitcast.9), custom_call_target="tpu_custom_call" | custom-call | tf_op jit(solution)/shard_map/pallas_call | solution.py:669
  67.5 0.0 copy-done.1
  67.5 22.0 %shard_map.61 = (f32[8192,128]{1,0:T(8,128)S(1)}, s32[8]{0:T(128)S(1)}, f32[1,128]{1,0:T(1,128)S(1)}) custom-call(s32[2,13]{1,0:T(2,128)S(1)} %copy-done.3, s32[8]{0:T(128)S(1)} %get-tuple-element.9.lanes, s32[1024]{0:T(1024)S(1)} %copy-done.2, s32[1]{0:T(128)} %bitcast.where, f32[2,2,16,16]{3,2,1,0:T(8,128)S(1)} %copy-done.1, f32[8192,128]{1,0:T(8,128)S(1)} %bitcast.6), custom_call_target="tpu_custom_call" | custom-call | tf_op jit(solution)/shard_map/pallas_call | solution.py:687
  89.6 53.1 %shard_map.62 = (f32[2,8,2,2,2,2,2,2,8,128]{9,8,7,6,5,4,3,2,1,0:T(8,128)S(1)}, f32[1,1]{1,0:T(1,128)}) custom-call(f32[2,8,2,2,2,2,2,2,8,128]{9,8,7,6,5,4,3,2,1,0:T(8,128)S(1)} %bitcast.7, f32[1,128]{1,0:T(1,128)S(1)} %get-tuple-element.13.refs_1_), custom_call_target="tpu_custom_call" | custom-call | tf_op jit(solution)/shard_map/pallas_call | solution.py:669
  142.7 23.4 %shard_map.63 = f32[2,64,8192]{2,1,0:T(8,128)} custom-call(s32[2,13]{1,0:T(2,128)S(1)} %copy-done.3, s32[8]{0:T(128)S(1)} %get-tuple-element.11.lanes, s32[1024]{0:T(1024)S(1)} %copy-done.2, s32[1]{0:T(128)} %bitcast.where, f32[2,2,16,16]{3,2,1,0:T(8,128)S(1)} %copy-done.1, f32[8192,128]{1,0:T(8,128)S(1)} %bitcast.8), custom_call_target="tpu_custom_call" | custom-call | tf_op jit(solution)/shard_map/pallas_call | solution.py:687
Async XLA Ops:
  0.6 2.2 %copy-start = (f32[2,64,8192]{2,1,0:T(8,128)S(1)}, f32[2,64,8192]{2,1,0:T(8,128)}, u32[]{:S(2)}) copy-start(f32[2,64,8192]{2,1,0:T(8,128)} %x.1) | copy-start | bytes 12582916
  2.8 0.7 copy-start.2
  3.5 0.7 copy-start.3
  10.9 56.7 %copy-start.1 = (f32[2,2,16,16]{3,2,1,0:T(8,128)S(1)}, f32[2,2,16,16]{3,2,1,0:T(8,128)}, u32[]{:S(2)}) copy-start(f32[2,2,16,16]{3,2,1,0:T(8,128)} %sup.3) | copy-start | bytes 12292

commit v7 on v6

--- a/solution.py
+++ b/solution.py
@@ -290,7 +290,7 @@
         apply_pair(source, result, pair, ta, rv, xa, xb, weights)
 
 
-def trace_share(perm, slots, where, sup, out, row_weight, outpos, final, order, tu, tc):
+def trace_share(perm, where, sup, z, loc, outpos, final, order, tu, tc):
     column_order(perm, order)
     me = where[0]
 
@@ -327,10 +327,10 @@
     exact = functools.partial(jnp.dot, precision=lax.Precision.HIGHEST, preferred_element_type=F32)
     weight = jnp.where(lane < 64, exact(real, hot), -exact(imag, hot))
 
-    fill(tu, [row_weight(final[j]) for j in range(4)])
+    fill(tu, [one_shl(loc[final[j]]) for j in range(4)])
 
     def weight_of(bit):
-        return jnp.where(outpos[bit] >= 4, row_weight(bit), 0)
+        return jnp.where(outpos[bit] >= 4, one_shl(loc[bit]), 0)
 
     fill(tc, [weight_of(order[i]) for i in range(6)])
     base = jnp.int32(0)
@@ -341,12 +341,9 @@
 
     def column(c, rows):
         start = base + tc[c]
-        found = []
-        for u in range(16):
-            index = start + tu[u]
-            row = slots[jnp.right_shift(index, 3) ^ (me * 8)] + (index & 7)
-            found.append(jnp.where(lane1 == c, out[pl.ds(row, 1), :], rows[u]))
-        return tuple(found)
+        return tuple(
+            jnp.where(lane1 == c, z[pl.ds(start + tu[u], 1), :], rows[u]) for u in range(16)
+        )
 
     rows = lax.fori_loop(0, 64, column, tuple(sums for _ in range(16)))
     for u in range(16):
@@ -392,6 +389,7 @@
     fill(major, [one_shl(loc[m]) for m in mixes])
     fill(rv, [one_shl(rest[j]) for j in range(6)])
     channel(sup, 0, True, lanes, z, spare, major, rv, xa, xb, weights)
+    share[...] = trace_share(perm, where, sup, z, loc, outpos, final, order, tu, tc)
     plan_sublanes(loc, occ, stays, everything, places, enabled)
 
     @pl.when(enabled[0] + enabled[1] + enabled[2] > 0)
@@ -419,11 +417,6 @@
         origin, target = high_from[i], high_to[i]
         for j in range(32):
             out[tile_at(slots[(target + low_to[j]) ^ mine]), :] = z[tile_at(origin + 8 * j), :]
-
-    def row_weight(bit):
-        return jnp.where(loc[bit] < 3, one_shl(jnp.minimum(loc[bit], 3)), 8 * out_of[bit])
-
-    share[...] = trace_share(perm, slots, where, sup, out, row_weight, outpos, final, order, tu, tc)
 
 
 def gather_back(perm, lanes, slots, where, sup, x, out, y, spare, xa, xb, weights,
@@ -534,7 +527,7 @@
         x, mine, out, total, shares, share_send, share_recv, *refs = refs
     else:
         x, out, *refs = refs
-    held, (send, recv, first_send, first_recv, out_sem) = refs[:7], refs[7:]
+    held, (send, recv, first_send, first_recv, out_sem) = refs[:6], refs[6:]
     hi = lax.axis_index("hi")
     grp = lax.axis_index("grp")
     bits = [lax.rem(hi // (1 << k), 2) for k in range(6)]
@@ -564,13 +557,24 @@
         )
 
     for p in range(PARTS):
-        pltpu.make_async_copy(x.at[0, p], held[0].at[0, p], first_recv.at[0, p]).start()
-        remote(x.at[1, p], held[0].at[1, p], first_send.at[p], first_recv.at[1, p], core).start()
+        remote(x.at[1, p], held[0].at[p], first_send.at[p], first_recv.at[p], core).start()
+
+    def drained(ref, sem):
+        pltpu.make_async_copy(ref, ref, sem).wait()
+
+    def stage(h, p, s, index=()):
+        if s == 0:
+            return x.at[(0, p) + index] if h == 0 else held[0].at[(p,) + index]
+        return held[s].at[(h, p) + index]
+
+    def landed(h, p):
+        return out.at[(h, p) + (slice(None),) * 5 + (1,)]
 
     def arrived(h, p, s):
-        ref = held[s].at[h, p]
-        sem = first_recv.at[h, p] if s == 0 else recv.at[h, p, s - 1]
-        pltpu.make_async_copy(ref, ref, sem).wait()
+        if s:
+            drained(stage(h, p, s) if s < 6 else landed(h, p), recv.at[h, p, s - 1])
+        elif h:
+            drained(stage(h, p, 0), first_recv.at[p])
 
     def pick(s, chosen):
         return tuple(chosen[b] for b in range(1, 7) if b != s)
@@ -584,19 +588,20 @@
             target = dict(source)
             if j:
                 target[j] = 1
+            place = (h, p) + pick(s, target)
             remote(
-                held[j].at[(h, p) + pick(j, source)], held[s].at[(h, p) + pick(s, target)],
+                stage(h, p, j, pick(j, source)), held[s].at[place] if s < 6 else out.at[place + (1,)],
                 send.at[h, p, s - 1], recv.at[h, p, s - 1], link_device[link],
             ).start()
 
     def deliver(h, p):
-        for j in range(7):
+        for j in range(6):
             source = {b: slice(None) if b < j else 0 for b in range(1, 7)}
             target = dict(source)
             if j:
                 target[j] = 1
             pltpu.make_async_copy(
-                held[j].at[(h, p) + pick(j, source)],
+                stage(h, p, j, pick(j, source)),
                 out.at[(h, p) + tuple(target[b] for b in range(1, 7))],
                 out_sem.at[h, p],
             ).start()
@@ -614,14 +619,14 @@
             )
 
     for t in range(8):
-
-        @pl.loop(0, 2)
-        def _(h):
+        for h in range(2):
             for p in range(PARTS):
                 link = (p + t) % 8
                 if link < LINKS:
                     arrived(h, p, done[p])
                     cross(h, p, done[p] + 1, link)
+                    if done[p] == 5:
+                        deliver(h, p)
 
         if with_sum and t < 7:
             if t:
@@ -631,11 +636,9 @@
             if (p + t) % 8 < LINKS:
                 done[p] += 1
 
-    @pl.loop(0, 2)
-    def _(h):
-        for p in (0, 7, 1, 2, 3, 4, 5, 6):
+    for h in range(2):
+        for p in range(PARTS):
             arrived(h, p, 6)
-            deliver(h, p)
 
     if with_sum:
         double(6).wait()
@@ -643,15 +646,12 @@
         total[...] = jnp.sum(grand, axis=1, keepdims=True) / ROWS
 
     for p in range(PARTS):
-        pltpu.make_async_copy(x.at[1, p], x.at[1, p], first_send.at[p]).wait()
-
-    @pl.loop(0, 2)
-    def _(h):
+        drained(x.at[1, p], first_send.at[p])
+    for h in range(2):
         for p in range(PARTS):
             for s in range(1, 7):
-                ref = held[s].at[h, p]
-                pltpu.make_async_copy(ref, ref, send.at[h, p, s - 1]).wait()
-            pltpu.make_async_copy(out.at[h, p], out.at[h, p], out_sem.at[h, p]).wait()
+                drained(landed(h, p), send.at[h, p, s - 1])
+            drained(out.at[h, p, 0], out_sem.at[h, p])
 
 
 def exchange(value, collective_id, share=None):
@@ -661,9 +661,9 @@
     anywhere = pl.BlockSpec(memory_space=pltpu.HBM)
     vmem = pl.BlockSpec(memory_space=VMEM)
     extra = share is not None
-    scratch = [VMEM((2, PARTS) + two + (8, 128), F32)]
-    scratch += [VMEM((2, PARTS) + two[:5] + (8, 128), F32) for _ in range(6)]
-    scratch += [dma((2, PARTS, 6)), dma((2, PARTS, 6)), dma((PARTS,)), dma((2, PARTS)), dma((2, PARTS))]
+    scratch = [VMEM((PARTS,) + two + (8, 128), F32)]
+    scratch += [VMEM((2, PARTS) + two[:5] + (8, 128), F32) for _ in range(5)]
+    scratch += [dma((2, PARTS, 6)), dma((2, PARTS, 6)), dma((PARTS,)), dma((PARTS,)), dma((2, PARTS))]
     if extra:
         scratch = [VMEM((128, 1, 128), F32), dma((7,)), dma((8,))] + scratch
     result = pl.pallas_call(

time: 168 us -> 166 us (0.988)
  Pallas kernels: 162 us -> 160 us
where the time goes in v7:
time: 166 us
  Pallas kernels  160 us (96%)
  local copies, waits for them, and re-layouts  3.55 us (2%)
  between operations  2.51 us (2%)
    pallas_call x2, Pallas kernels, exchange(): pl.pallas_call(functools.partial(swap_all, extra), out_shape=(whole, jax....  109 us
    pallas_call x3, Pallas kernels, call(): pl.pallas_call(body, out_shape=outs, in_specs=[smem if i < n_smem else vm...  50.7 us
    unnamed x8, local copies, waits for them, and re-layouts  3.55 us

profile of v7, /device:TPU:0, one launch (start us, length us, event | category | flops | bytes accessed | tf_op | source)
XLA Modules:
  0.0 165.9 jit_solution(10475733604106261562)
XLA Ops:
  0.6 0.0 copy-start
  0.6 2.2 %copy-done = f32[2,64,8192]{2,1,0:T(8,128)S(1)} copy-done((f32[2,64,8192]{2,1,0:T(8,128)S(1)}, f32[2,64,8192]{2,1,0:T(8,128)}, u32[]{:S(2)}) %copy-start) | copy-done | bytes 4194328
  2.8 0.0 copy-start.2
  2.8 0.7 copy-done.2
  3.5 0.0 copy-start.3
  3.5 0.7 copy-done.3
  4.2 6.7 %shard_map.59 = (f32[8192,128]{1,0:T(8,128)S(1)}, s32[8]{0:T(128)S(1)}) custom-call(s32[2,13]{1,0:T(2,128)S(1)} %copy-done.3, s32[1024]{0:T(1024)S(1)} %copy-done.2, s32[1]{0:T(128)} %bitcast.where, f32[2,64,8192]{2,1,0:T(8,128)S(1)} %copy-done), custom_call_target="tpu_custom_call" | custom-call | tf_op jit(solution)/shard_map/pallas_call | solution.py:687
  10.9 0.0 copy-start.1
  10.9 56.3 %shard_map.60 = f32[2,8,2,2,2,2,2,2,8,128]{9,8,7,6,5,4,3,2,1,0:T(8,128)S(1)} custom-call(f32[2,8,2,2,2,2,2,2,8,128]{9,8,7,6,5,4,3,2,1,0:T(8,128)S(1)} %bitcast.9), custom_call_target="tpu_custom_call" | custom-call | tf_op jit(solution)/shard_map/pallas_call | solution.py:669
  67.2 0.0 copy-done.1
  67.2 20.6 %shard_map.61 = (f32[8192,128]{1,0:T(8,128)S(1)}, s32[8]{0:T(128)S(1)}, f32[1,128]{1,0:T(1,128)S(1)}) custom-call(s32[2,13]{1,0:T(2,128)S(1)} %copy-done.3, s32[8]{0:T(128)S(1)} %get-tuple-element.9.lanes, s32[1024]{0:T(1024)S(1)} %copy-done.2, s32[1]{0:T(128)} %bitcast.where, f32[2,2,16,16]{3,2,1,0:T(8,128)S(1)} %copy-done.1, f32[8192,128]{1,0:T(8,128)S(1)} %bitcast.6), custom_call_target="tpu_custom_call" | custom-call | tf_op jit(solution)/shard_map/pallas_call | solution.py:687
  87.8 52.8 %shard_map.62 = (f32[2,8,2,2,2,2,2,2,8,128]{9,8,7,6,5,4,3,2,1,0:T(8,128)S(1)}, f32[1,1]{1,0:T(1,128)}) custom-call(f32[2,8,2,2,2,2,2,2,8,128]{9,8,7,6,5,4,3,2,1,0:T(8,128)S(1)} %bitcast.7, f32[1,128]{1,0:T(1,128)S(1)} %get-tuple-element.13.refs_1_), custom_call_target="tpu_custom_call" | custom-call | tf_op jit(solution)/shard_map/pallas_call | solution.py:669
  140.7 23.4 %shard_map.63 = f32[2,64,8192]{2,1,0:T(8,128)} custom-call(s32[2,13]{1,0:T(2,128)S(1)} %copy-done.3, s32[8]{0:T(128)S(1)} %get-tuple-element.11.lanes, s32[1024]{0:T(1024)S(1)} %copy-done.2, s32[1]{0:T(128)} %bitcast.where, f32[2,2,16,16]{3,2,1,0:T(8,128)S(1)} %copy-done.1, f32[8192,128]{1,0:T(8,128)S(1)} %bitcast.8), custom_call_target="tpu_custom_call" | custom-call | tf_op jit(solution)/shard_map/pallas_call | solution.py:687
Async XLA Ops:
  0.6 2.2 %copy-start = (f32[2,64,8192]{2,1,0:T(8,128)S(1)}, f32[2,64,8192]{2,1,0:T(8,128)}, u32[]{:S(2)}) copy-start(f32[2,64,8192]{2,1,0:T(8,128)} %x.1) | copy-start | bytes 12582916
  2.8 0.7 copy-start.2
  3.5 0.7 copy-start.3
  10.9 56.3 %copy-start.1 = (f32[2,2,16,16]{3,2,1,0:T(8,128)S(1)}, f32[2,2,16,16]{3,2,1,0:T(8,128)}, u32[]{:S(2)}) copy-start(f32[2,2,16,16]{3,2,1,0:T(8,128)} %sup.3) | copy-start | bytes 12292

commit v8 on v7

--- a/solution.py
+++ b/solution.py
@@ -284,10 +284,9 @@
                         ]
 
 
-def channel(sup, layer, major_is_row, lanes, z, spare, ta, rv, xa, xb, weights):
+def channel(z, spare, ta, rv, xa, xb, weights):
     for pair, (source, result) in enumerate(((z, spare), (spare, z))):
-        build_weights(sup, layer, pair, major_is_row, lanes if pair == 0 else None, weights)
-        apply_pair(source, result, pair, ta, rv, xa, xb, weights)
+        apply_pair(source, result, pair, ta, rv, xa, xb, weights[pair])
 
 
 def trace_share(perm, where, sup, z, loc, outpos, final, order, tu, tc):
@@ -351,7 +350,7 @@
     return sums
 
 
-def middle(perm, lanes, slots, where, sup, x, out, rows_out, share, z, spare, xa, xb, weights,
+def middle(perm, slots, where, sup, x, w0, w1, out, rows_out, share, z, spare, xa, xb,
            final, outpos, loc, occ, rest, major, rv, order, tu, tc, out_of, low_from, low_to,
            high_from, high_to, places, enabled, *groups):
     me = where[0]
@@ -388,7 +387,7 @@
         count = count + jnp.where(mixed_bit(occ[place]), 0, 1)
     fill(major, [one_shl(loc[m]) for m in mixes])
     fill(rv, [one_shl(rest[j]) for j in range(6)])
-    channel(sup, 0, True, lanes, z, spare, major, rv, xa, xb, weights)
+    channel(z, spare, major, rv, xa, xb, (w0, w1))
     share[...] = trace_share(perm, where, sup, z, loc, outpos, final, order, tu, tc)
     plan_sublanes(loc, occ, stays, everything, places, enabled)
 
@@ -419,7 +418,7 @@
             out[tile_at(slots[(target + low_to[j]) ^ mine]), :] = z[tile_at(origin + 8 * j), :]
 
 
-def gather_back(perm, lanes, slots, where, sup, x, out, y, spare, xa, xb, weights,
+def gather_back(perm, slots, where, x, w0, w1, out, y, spare, xa, xb,
                 order, inv, loc, occ, ta, rv, origin, places, enabled, *groups):
     column_order(perm, order)
     for i in range(QUBITS):
@@ -471,7 +470,7 @@
     regroup(lambda row: y[tile_at(row), :], spare, places, enabled, *groups, origin=origin)
     fill(ta, [one_shl(loc[q]) for q in range(4)])
     fill(rv, [one_shl(loc[q]) for q in range(7, QUBITS)])
-    channel(sup, 1, False, lanes, spare, y, ta, rv, xa, xb, weights)
+    channel(spare, y, ta, rv, xa, xb, (w0, w1))
 
     sublane = lax.broadcasted_iota(jnp.int32, (8, 128), 0)
 
@@ -524,9 +523,9 @@
 
 def swap_all(with_sum, *refs):
     if with_sum:
-        x, mine, out, total, shares, share_send, share_recv, *refs = refs
+        x, lanes, sup, mine, out, w0, w1, total, shares, share_send, share_recv, *refs = refs
     else:
-        x, out, *refs = refs
+        x, lanes, sup, out, w0, w1, *refs = refs
     held, (send, recv, first_send, first_recv, out_sem) = refs[:6], refs[6:]
     hi = lax.axis_index("hi")
     grp = lax.axis_index("grp")
@@ -628,6 +627,10 @@
                     if done[p] == 5:
                         deliver(h, p)
 
+        if t < 2:
+            build_weights(
+                sup, int(with_sum), t, not with_sum, None if t else lanes, w1 if t else w0
+            )
         if with_sum and t < 7:
             if t:
                 double(t - 1).wait()
@@ -654,7 +657,7 @@
             drained(out.at[h, p, 0], out_sem.at[h, p])
 
 
-def exchange(value, collective_id, share=None):
+def exchange(value, collective_id, lanes, sup, share=None):
     two = (2,) * 6
     whole = jax.ShapeDtypeStruct((2, PARTS) + two + (8, 128), F32)
     dma = pltpu.SemaphoreType.DMA
@@ -666,19 +669,20 @@
     scratch += [dma((2, PARTS, 6)), dma((2, PARTS, 6)), dma((PARTS,)), dma((PARTS,)), dma((2, PARTS))]
     if extra:
         scratch = [VMEM((128, 1, 128), F32), dma((7,)), dma((8,))] + scratch
+    matrix = jax.ShapeDtypeStruct((1536, 512), BF16)
+    smem = pl.BlockSpec(memory_space=SMEM)
+    outs = (whole, matrix, matrix) + ((jax.ShapeDtypeStruct((1, 1), F32),) if extra else ())
     result = pl.pallas_call(
         functools.partial(swap_all, extra),
-        out_shape=(whole, jax.ShapeDtypeStruct((1, 1), F32)) if extra else whole,
-        in_specs=[anywhere] * (1 + extra),
-        out_specs=(anywhere, vmem) if extra else anywhere,
+        out_shape=outs,
+        in_specs=[anywhere, smem, vmem] + [anywhere] * extra,
+        out_specs=(anywhere, vmem, vmem) + (vmem,) * extra,
         scratch_shapes=scratch,
         compiler_params=pltpu.CompilerParams(
             collective_id=collective_id, has_side_effects=True, vmem_limit_bytes=24 * 2**20
         ),
-    )(*((value.reshape(whole.shape), share) if extra else (value.reshape(whole.shape),)))
-    if extra:
-        return result[0].reshape(8192, 128), result[1]
-    return result.reshape(8192, 128)
+    )(value.reshape(whole.shape), lanes, sup, *((share,) if extra else ()))
+    return result[0].reshape(8192, 128), *result[1:]
 
 
 def call(body, outs, out_smem, n_smem, n_args, scratch, args):
@@ -701,7 +705,7 @@
 FULL = VMEM((8192, 128), F32)
 GROUPS = (3, 3, 14, 8, 16)
 MAP = jax.ShapeDtypeStruct((8,), jnp.int32)
-WORK = [FULL, VMEM((512, 1536), BF16), VMEM((512, 1536), BF16), VMEM((1536, 512), BF16)]
+WORK = [FULL, VMEM((512, 1536), BF16), VMEM((512, 1536), BF16)]
 
 
 def spread_call(perm, slots, where, x):
@@ -711,21 +715,21 @@
     )
 
 
-def middle_call(perm, lanes, slots, where, sup, x):
+def middle_call(perm, slots, where, sup, x, w0, w1):
     return call(
         middle,
         (jax.ShapeDtypeStruct((8192, 128), F32), MAP, jax.ShapeDtypeStruct((1, 128), F32)),
-        (1,), 4, 6,
+        (1,), 3, 7,
         [FULL] + WORK + table(13, 13, 13, 13, 14, 16, 64, 14, 16, 64, 13, 32, 32, 32, 32, *GROUPS),
-        (perm, lanes, slots, where, sup, x),
+        (perm, slots, where, sup, x, w0, w1),
     )
 
 
-def back_call(perm, lanes, slots, where, sup, x):
+def back_call(perm, slots, where, x, w0, w1):
     return call(
-        gather_back, (jax.ShapeDtypeStruct((2, 64, 8192), F32),), (), 4, 6,
+        gather_back, (jax.ShapeDtypeStruct((2, 64, 8192), F32),), (), 3, 6,
         [FULL] + WORK + table(14, 13, 13, 13, 16, 64, 3, *GROUPS),
-        (perm, lanes, slots, where, sup, x),
+        (perm, slots, where, x, w0, w1),
     )[0]
 
 
@@ -733,9 +737,10 @@
     slots = jnp.asarray(slot_table())
     where = lax.axis_index(HI_GRP).astype(jnp.int32).reshape(1)
     sent, lanes = spread_call(perm, slots, where, rho)
-    mid, rows, share = middle_call(perm, lanes, slots, where, superop, exchange(sent, 0))
-    last, total = exchange(mid, 1, share)
-    return back_call(perm, rows, slots, where, superop, last), total.reshape(())
+    first = exchange(sent, 0, lanes, superop)
+    mid, rows, share = middle_call(perm, slots, where, superop, *first)
+    *last, total = exchange(mid, 1, rows, superop, share)
+    return back_call(perm, slots, where, *last), total.reshape(())
 
 
 def solution(mesh):

time: 166 us -> 162 us (0.976)
  Pallas kernels: 160 us -> 156 us
    pallas_call x3, Pallas kernels: 50.7 us -> 45.9 us  [call(): pl.pallas_call(body, out_shape=outs, in_specs=[smem if i < n_smem else vm...]
where the time goes in v8:
time: 162 us
  Pallas kernels  156 us (96%)
  local copies, waits for them, and re-layouts  3.55 us (2%)
  between operations  2.38 us (1%)
    pallas_call x2, Pallas kernels, exchange(): pl.pallas_call(functools.partial(swap_all, extra), out_shape=outs, in_spe...  110 us
    pallas_call x3, Pallas kernels, call(): pl.pallas_call(body, out_shape=outs, in_specs=[smem if i < n_smem else vm...  45.9 us
    unnamed x8, local copies, waits for them, and re-layouts  3.55 us

profile of v8, /device:TPU:0, one launch (start us, length us, event | category | flops | bytes accessed | tf_op | source)
XLA Modules:
  0.0 161.9 jit_solution(7583091069645338611)
XLA Ops:
  0.6 0.0 copy-start
  0.6 2.2 %copy-done = f32[2,64,8192]{2,1,0:T(8,128)S(1)} copy-done((f32[2,64,8192]{2,1,0:T(8,128)S(1)}, f32[2,64,8192]{2,1,0:T(8,128)}, u32[]{:S(2)}) %copy-start) | copy-done | bytes 4194328
  2.8 0.0 copy-start.2
  2.8 0.7 copy-done.2
  3.5 0.0 copy-start.3
  3.5 0.7 copy-done.3
  4.2 0.0 copy-start.1
  4.2 6.7 %shard_map.59 = (f32[8192,128]{1,0:T(8,128)S(1)}, s32[8]{0:T(128)S(1)}) custom-call(s32[2,13]{1,0:T(2,128)S(1)} %copy-done.3, s32[1024]{0:T(1024)S(1)} %copy-done.2, s32[1]{0:T(128)} %bitcast.where, f32[2,64,8192]{2,1,0:T(8,128)S(1)} %copy-done), custom_call_target="tpu_custom_call" | custom-call | tf_op jit(solution)/shard_map/pallas_call | solution.py:691
  10.9 0.0 copy-done.1
  10.9 56.7 %shard_map.60 = (f32[2,8,2,2,2,2,2,2,8,128]{9,8,7,6,5,4,3,2,1,0:T(8,128)S(1)}, bf16[1536,512]{1,0:T(8,128)(2,1)S(1)}, bf16[1536,512]{1,0:T(8,128)(2,1)S(1)}) custom-call(f32[2,8,2,2,2,2,2,2,8,128]{9,8,7,6,5,4,3,2,1,0:T(8,128)S(1)} %bitcast.8, s32[8]{0:T(128)S(1)} %get-tuple-element.15.refs_1_, f32[2,2,16,16]{3,2,1,0:T(8,128)S(1)} %copy-done.1), custom_call_target="tpu_custom_call" | custom-call | tf_op jit(solution)/shard_map/pallas_call | solution.py:675
  67.6 18.2 %shard_map.61 = (f32[8192,128]{1,0:T(8,128)S(1)}, s32[8]{0:T(128)S(1)}, f32[1,128]{1,0:T(1,128)S(1)}) custom-call(s32[2,13]{1,0:T(2,128)S(1)} %copy-done.3, s32[1024]{0:T(1024)S(1)} %copy-done.2, s32[1]{0:T(128)} %bitcast.where, f32[2,2,16,16]{3,2,1,0:T(8,128)S(1)} %copy-done.1, f32[8192,128]{1,0:T(8,128)S(1)} %bitcast.6, ...), custom_call_target="tpu_custom_call" | custom-call | tf_op jit(solution)/shard_map/pallas_call | solution.py:691
  85.8 53.4 %shard_map.62 = (f32[2,8,2,2,2,2,2,2,8,128]{9,8,7,6,5,4,3,2,1,0:T(8,128)S(1)}, bf16[1536,512]{1,0:T(8,128)(2,1)S(1)}, bf16[1536,512]{1,0:T(8,128)(2,1)S(1)}, f32[1,1]{1,0:T(1,128)}) custom-call(f32[2,8,2,2,2,2,2,2,8,128]{9,8,7,6,5,4,3,2,1,0:T(8,128)S(1)} %bitcast.7, s32[8]{0:T(128)S(1)} %get-tuple-element.20.refs_1_, f32[2,2,16,16]{3,2,1,0:T(8,128)S(1)} %copy-done.1, ...), custom_call_target="tpu_custom_call" | custom-call | tf_op jit(solution)/shard_map/pallas_call | solution.py:675
  139.2 20.9 %shard_map.63 = f32[2,64,8192]{2,1,0:T(8,128)} custom-call(s32[2,13]{1,0:T(2,128)S(1)} %copy-done.3, s32[1024]{0:T(1024)S(1)} %copy-done.2, s32[1]{0:T(128)} %bitcast.where, f32[8192,128]{1,0:T(8,128)S(1)} %bitcast.9, bf16[1536,512]{1,0:T(8,128)(2,1)S(1)} %get-tuple-element.23.w0, bf16[1536,512]{1,0:T(8,128)(2,1)S(1)} %get-tuple-element.24.w1), custom_call_target="tpu_custom_call" | custom-call | tf_op jit(solution)/shard_map/pallas_call | solution.py:691
Async XLA Ops:
  0.6 2.2 %copy-start = (f32[2,64,8192]{2,1,0:T(8,128)S(1)}, f32[2,64,8192]{2,1,0:T(8,128)}, u32[]{:S(2)}) copy-start(f32[2,64,8192]{2,1,0:T(8,128)} %x.1) | copy-start | bytes 12582916
  2.8 0.7 copy-start.2
  3.5 0.7 copy-start.3
  4.2 6.7 %copy-start.1 = (f32[2,2,16,16]{3,2,1,0:T(8,128)S(1)}, f32[2,2,16,16]{3,2,1,0:T(8,128)}, u32[]{:S(2)}) copy-start(f32[2,2,16,16]{3,2,1,0:T(8,128)} %refs_2_.3) | copy-start | bytes 12292

commit v9 on v8

--- a/solution.py
+++ b/solution.py
@@ -418,7 +418,7 @@
             out[tile_at(slots[(target + low_to[j]) ^ mine]), :] = z[tile_at(origin + 8 * j), :]
 
 
-def gather_back(perm, slots, where, x, w0, w1, out, y, spare, xa, xb,
+def gather_back(perm, slots, where, x, w0, w1, out, y, spare, xa, xb, ready, done,
                 order, inv, loc, occ, ta, rv, origin, places, enabled, *groups):
     column_order(perm, order)
     for i in range(QUBITS):
@@ -473,6 +473,10 @@
     channel(spare, y, ta, rv, xa, xb, (w0, w1))
 
     sublane = lax.broadcasted_iota(jnp.int32, (8, 128), 0)
+
+    def leave(group):
+        columns = pl.ds(pl.multiple_of(group * 512, 512), 512)
+        return pltpu.make_async_copy(ready.at[:, :, columns], out.at[:, :, columns], done)
 
     @pl.loop(0, 16)
     def _(group):
@@ -491,8 +495,15 @@
             ordered = [tiles[8 * (v % 2) + v // 2] for v in range(16)]
             columns = pl.ds(pl.multiple_of(t * 128, 128), 128)
             turned = jnp.concatenate(ordered, axis=0).T
-            out[0, :, columns] = turned[:64]
-            out[1, :, columns] = turned[64:]
+            ready[0, :, columns] = turned[:64]
+            ready[1, :, columns] = turned[64:]
+
+        @pl.when(group > 0)
+        def _():
+            leave(group - 1).start()
+
+    leave(15).start()
+    pltpu.make_async_copy(ready, out, done).wait()
 
 
 LINKS = 6
@@ -685,14 +696,16 @@
     return result[0].reshape(8192, 128), *result[1:]
 
 
-def call(body, outs, out_smem, n_smem, n_args, scratch, args):
+def call(body, outs, out_smem, n_smem, n_args, scratch, args, out_space=VMEM):
     smem = pl.BlockSpec(memory_space=SMEM)
     vmem = pl.BlockSpec(memory_space=VMEM)
     return pl.pallas_call(
         body,
         out_shape=outs,
         in_specs=[smem if i < n_smem else vmem for i in range(n_args)],
-        out_specs=tuple(smem if i in out_smem else vmem for i in range(len(outs))),
+        out_specs=tuple(
+            smem if i in out_smem else pl.BlockSpec(memory_space=out_space) for i in range(len(outs))
+        ),
         scratch_shapes=scratch,
         compiler_params=pltpu.CompilerParams(vmem_limit_bytes=26 * 2**20),
     )(*args)
@@ -728,8 +741,9 @@
 def back_call(perm, slots, where, x, w0, w1):
     return call(
         gather_back, (jax.ShapeDtypeStruct((2, 64, 8192), F32),), (), 3, 6,
-        [FULL] + WORK + table(14, 13, 13, 13, 16, 64, 3, *GROUPS),
-        (perm, slots, where, x, w0, w1),
+        [FULL] + WORK + [VMEM((2, 64, 8192), F32), pltpu.SemaphoreType.DMA]
+        + table(14, 13, 13, 13, 16, 64, 3, *GROUPS),
+        (perm, slots, where, x, w0, w1), out_space=pltpu.HBM,
     )[0]
 
 

time: 162 us -> 161 us (level)
  no operation moved by 1% of the time
where the time goes in v9:
time: 161 us
  Pallas kernels  155 us (96%)
  local copies, waits for them, and re-layouts  3.55 us (2%)
  between operations  2.38 us (1%)
    pallas_call x2, Pallas kernels, exchange(): pl.pallas_call(functools.partial(swap_all, extra), out_shape=outs, in_spe...  110 us
    pallas_call x3, Pallas kernels, call(): pl.pallas_call(body, out_shape=outs, in_specs=[smem if i < n_smem else vm...  44.7 us
    unnamed x8, local copies, waits for them, and re-layouts  3.55 us

profile of v9, /device:TPU:0, one launch (start us, length us, event | category | flops | bytes accessed | tf_op | source)
XLA Modules:
  0.0 160.7 jit_solution(13672735127546039337)
XLA Ops:
  0.6 0.0 copy-start
  0.6 2.2 %copy-done = f32[2,64,8192]{2,1,0:T(8,128)S(1)} copy-done((f32[2,64,8192]{2,1,0:T(8,128)S(1)}, f32[2,64,8192]{2,1,0:T(8,128)}, u32[]{:S(2)}) %copy-start) | copy-done | bytes 4194328
  2.8 0.0 copy-start.2
  2.8 0.7 copy-done.2
  3.5 0.0 copy-start.3
  3.5 0.7 copy-done.3
  4.2 0.0 copy-start.1
  4.2 6.7 %shard_map.59 = (f32[8192,128]{1,0:T(8,128)S(1)}, s32[8]{0:T(128)S(1)}) custom-call(s32[2,13]{1,0:T(2,128)S(1)} %copy-done.3, s32[1024]{0:T(1024)S(1)} %copy-done.2, s32[1]{0:T(128)} %bitcast.where, f32[2,64,8192]{2,1,0:T(8,128)S(1)} %copy-done), custom_call_target="tpu_custom_call" | custom-call | tf_op jit(solution)/shard_map/pallas_call | solution.py:702
  10.9 0.0 copy-done.1
  10.9 56.7 %shard_map.60 = (f32[2,8,2,2,2,2,2,2,8,128]{9,8,7,6,5,4,3,2,1,0:T(8,128)S(1)}, bf16[1536,512]{1,0:T(8,128)(2,1)S(1)}, bf16[1536,512]{1,0:T(8,128)(2,1)S(1)}) custom-call(f32[2,8,2,2,2,2,2,2,8,128]{9,8,7,6,5,4,3,2,1,0:T(8,128)S(1)} %bitcast.8, s32[8]{0:T(128)S(1)} %get-tuple-element.15.refs_1_, f32[2,2,16,16]{3,2,1,0:T(8,128)S(1)} %copy-done.1), custom_call_target="tpu_custom_call" | custom-call | tf_op jit(solution)/shard_map/pallas_call | solution.py:686
  67.6 18.3 %shard_map.61 = (f32[8192,128]{1,0:T(8,128)S(1)}, s32[8]{0:T(128)S(1)}, f32[1,128]{1,0:T(1,128)S(1)}) custom-call(s32[2,13]{1,0:T(2,128)S(1)} %copy-done.3, s32[1024]{0:T(1024)S(1)} %copy-done.2, s32[1]{0:T(128)} %bitcast.where, f32[2,2,16,16]{3,2,1,0:T(8,128)S(1)} %copy-done.1, f32[8192,128]{1,0:T(8,128)S(1)} %bitcast.6, ...), custom_call_target="tpu_custom_call" | custom-call | tf_op jit(solution)/shard_map/pallas_call | solution.py:702
  85.8 53.4 %shard_map.62 = (f32[2,8,2,2,2,2,2,2,8,128]{9,8,7,6,5,4,3,2,1,0:T(8,128)S(1)}, bf16[1536,512]{1,0:T(8,128)(2,1)S(1)}, bf16[1536,512]{1,0:T(8,128)(2,1)S(1)}, f32[1,1]{1,0:T(1,128)}) custom-call(f32[2,8,2,2,2,2,2,2,8,128]{9,8,7,6,5,4,3,2,1,0:T(8,128)S(1)} %bitcast.7, s32[8]{0:T(128)S(1)} %get-tuple-element.20.refs_1_, f32[2,2,16,16]{3,2,1,0:T(8,128)S(1)} %copy-done.1, ...), custom_call_target="tpu_custom_call" | custom-call | tf_op jit(solution)/shard_map/pallas_call | solution.py:686
  139.3 19.7 %shard_map.63 = f32[2,64,8192]{2,1,0:T(8,128)} custom-call(s32[2,13]{1,0:T(2,128)S(1)} %copy-done.3, s32[1024]{0:T(1024)S(1)} %copy-done.2, s32[1]{0:T(128)} %bitcast.where, f32[8192,128]{1,0:T(8,128)S(1)} %bitcast.9, bf16[1536,512]{1,0:T(8,128)(2,1)S(1)} %get-tuple-element.23.w0, bf16[1536,512]{1,0:T(8,128)(2,1)S(1)} %get-tuple-element.24.w1), custom_call_target="tpu_custom_call" | custom-call | tf_op jit(solution)/shard_map/pallas_call | solution.py:702
Async XLA Ops:
  0.6 2.2 %copy-start = (f32[2,64,8192]{2,1,0:T(8,128)S(1)}, f32[2,64,8192]{2,1,0:T(8,128)}, u32[]{:S(2)}) copy-start(f32[2,64,8192]{2,1,0:T(8,128)} %x.1) | copy-start | bytes 12582916
  2.8 0.7 copy-start.2
  3.5 0.7 copy-start.3
  4.2 6.7 %copy-start.1 = (f32[2,2,16,16]{3,2,1,0:T(8,128)S(1)}, f32[2,2,16,16]{3,2,1,0:T(8,128)}, u32[]{:S(2)}) copy-start(f32[2,2,16,16]{3,2,1,0:T(8,128)} %refs_2_.3) | copy-start | bytes 12292
